TPU v7x, 256 devices: a whole 4x4x8 slice. The times are simulated.
256 devices in a mesh: grp: 4 (over y), blk: 64 (over z, x, core).
Axes of the slice: x: 4, y: 4, z: 8, core: 2. Of those that a mesh axis runs over, the one named last changes fastest.
Arguments:
- features: bfloat16 [262144, 256], P(('grp', 'blk')), may hold values from -40 to 40, as said below
- source_index: int32 [4096, 128], P(('grp', 'blk')), may hold values from 0 to 3071
- target_index: int32 [4096, 128], P(('grp', 'blk')), may hold values from 0 to 1023
- edge_valid: int32 [4096, 128], P(('grp', 'blk')), may hold values from 0 to 1, as said below
- edge_bias: float32 [8, 524288], P(None, ('grp', 'blk')), may hold values from -4 to 284
- send_list: int32 [256, 2048], P(('grp', 'blk')), may hold values from 0 to 1023
- w_left: bfloat16 [2, 256, 256], replicated, may hold values from -0.375 to 0.375
- w_right: bfloat16 [2, 256, 256], replicated, may hold values from -0.375 to 0.375
- w_skip: bfloat16 [2, 256, 256], replicated, may hold values from -0.375 to 0.375
- attn_vec: bfloat16 [2, 256], replicated, may hold values from -1 to 1
- norm_gain: bfloat16 [2, 256], replicated, may hold values from 0.5 to 1.5
- norm_shift: bfloat16 [2, 256], replicated, may hold values from -3 to 3
Outputs:
- node_states: bfloat16 [262144, 256], P(('grp', 'blk'))
Inputs may be any that keep to these rules, and one draw needn't show every extreme that they name: `features`: A spread of order one around a few large per-device offsets. `edge_valid`: the live slots of each device form a prefix of its 2048 slots, at least a quarter of them; in every draw some device has all its slots live.
All inputs are finite; a program needn't handle non-finite values.
Results may differ from a plain program's by a relative error of at most 0.007.
Values may be sent and summed in bfloat16 or wider, within the bound.
No kernel may reach another device: no remote copies, remote signals or barrier semaphores. Data moves between devices by JAX's collectives and lax.ppermute only.
A program may use at most 64 MiB of HBM per device.

v0:
```python
import functools

import jax
import jax.numpy as jnp
from jax import lax
from jax.sharding import Mesh
from jax.sharding import PartitionSpec as P

HEADS = 8
LAYERS = 2
GRP_BLK = ("grp", "blk_0", "blk_1", "blk_2")
BLK = ("blk_0", "blk_1", "blk_2")


def in_blocks(value, dim, devices):
    before, after = (value.shape[:dim], value.shape[dim + 1 :])
    return jnp.moveaxis(value.reshape(*before, devices, -1, *after), dim, 0)


def in_order(pieces, dim):
    lengths = list(pieces.shape[1:])
    lengths[dim] *= pieces.shape[0]
    return jnp.moveaxis(pieces, 0, dim).reshape(lengths)


def exchange_both(value, axis, axes, splits, concats):
    sizes = [lax.axis_size(a) for a in axes]
    pieces = in_blocks(value, splits[0], sizes[0])
    pieces = jnp.moveaxis(in_blocks(pieces, splits[1] + 1, sizes[1]), 0, 1)
    inside = pieces.shape[2:]
    pieces = pieces.reshape(-1, *inside)
    pieces = lax.all_to_all(pieces, axis, split_axis=0, concat_axis=0, tiled=True)
    pieces = in_order(pieces.reshape(*sizes, *inside), concats[0] + 1)
    return in_order(pieces, concats[1])


def by_axis(value, axes):
    return functools.reduce(lax.psum, axes, value)


def project(inputs, weight):
    return jnp.dot(inputs, weight, preferred_element_type=jnp.float32)


def leaky(values):
    return jnp.where(values > 0, values, 0.2 * values)


def head_columns(attn_row, head_count):
    feat_width = attn_row.shape[0]
    head_ids = jnp.arange(feat_width, dtype=jnp.int32) // (feat_width // head_count)
    owner_mask = head_ids[:, None] == jnp.arange(head_count, dtype=jnp.int32)[None, :]
    return jnp.where(owner_mask, attn_row.astype(jnp.float32)[:, None], jnp.zeros((), jnp.float32))


def score_rows(hidden, head_cols):
    return jnp.dot(hidden, head_cols, precision=lax.Precision.HIGHEST)


def weigh_rows(rows, weights):
    row_count, feat_width = rows.shape
    head_count = weights.shape[1]
    split_rows = rows.astype(jnp.float32).reshape(row_count, head_count, feat_width // head_count)
    return (split_rows * weights.astype(jnp.float32)[:, :, None]).reshape(row_count, feat_width)


def attend(source_table, left_own, right_own, sources, targets, valids, bias_rows, head_cols):
    node_count, feat_width = left_own.shape
    src_rows = source_table[sources]
    dst_rows = right_own[targets]
    hidden = leaky(src_rows.astype(jnp.float32) + dst_rows.astype(jnp.float32))
    scores = score_rows(hidden, head_cols) + bias_rows.T
    live_edges = valids[:, None] > 0
    scores = jnp.where(live_edges, scores, jnp.full((), -1e30, scores.dtype))
    own_hidden = leaky(left_own.astype(jnp.float32) + right_own.astype(jnp.float32))
    own_scores = score_rows(own_hidden, head_cols)
    seg_max = jax.ops.segment_max(scores, targets, num_segments=node_count)
    score_top = jnp.maximum(seg_max, own_scores)
    edge_weights = jnp.where(
        live_edges, jnp.exp(scores - score_top[targets]), jnp.zeros((), scores.dtype)
    )
    own_weights = jnp.exp(own_scores - score_top)
    denom_sum = own_weights + jax.ops.segment_sum(edge_weights, targets, num_segments=node_count)
    edge_alpha = (edge_weights / denom_sum[targets]).astype(jnp.bfloat16)
    own_alpha = (own_weights / denom_sum).astype(jnp.bfloat16)
    messages = weigh_rows(src_rows, edge_alpha)
    start_sum = weigh_rows(left_own, own_alpha)
    return start_sum + jax.ops.segment_sum(messages, targets, num_segments=node_count)


def normalize(summed, feat_mean, spread, gain_row, shift_row):
    scaled = (summed - feat_mean) * lax.rsqrt(spread + 0.1)
    return jax.nn.elu(scaled * gain_row.astype(jnp.float32) + shift_row.astype(jnp.float32)).astype(
        jnp.bfloat16
    )


def deliver(bundle):
    return exchange_both(bundle, GRP_BLK, ("grp", BLK), (0, 1), (0, 1))


def local(
    features,
    source_index,
    target_index,
    edge_valid,
    edge_bias,
    send_list,
    w_left,
    w_right,
    w_skip,
    attn_vec,
    norm_gain,
    norm_shift,
):
    group_count = lax.axis_size("grp")
    member_count = lax.axis_size(BLK)
    peer_count = group_count * member_count
    node_count, feat_width = features.shape
    slot_count = send_list.shape[1] // peer_count
    total_nodes = node_count * peer_count
    sources = source_index.reshape(-1)
    targets = target_index.reshape(-1)
    valids = edge_valid.reshape(-1)
    node_states = features
    for layer_idx in range(LAYERS):
        left_own = project(node_states, w_left[layer_idx]).astype(jnp.bfloat16)
        bundle = left_own[send_list[0]].reshape(group_count, member_count, slot_count, feat_width)
        received = deliver(bundle)
        right_own = project(node_states, w_right[layer_idx]).astype(jnp.bfloat16)
        skip_own = project(node_states, w_skip[layer_idx])
        head_cols = head_columns(attn_vec[layer_idx], HEADS)
        source_table = jnp.concatenate(
            [left_own, received.reshape(peer_count * slot_count, feat_width)], axis=0
        )
        gathered = attend(
            source_table, left_own, right_own, sources, targets, valids, edge_bias, head_cols
        )
        summed = node_states.astype(jnp.float32) + gathered + skip_own
        feat_total, feat_squares = (
            by_axis(jnp.sum(summed, axis=0), GRP_BLK),
            by_axis(jnp.sum(summed * summed, axis=0), GRP_BLK),
        )
        feat_mean = feat_total / total_nodes
        spread = jnp.maximum(feat_squares / total_nodes - feat_mean * feat_mean, 0.0)
        node_states = normalize(
            summed, feat_mean, spread, norm_gain[layer_idx], norm_shift[layer_idx]
        )
    return node_states


def solution(mesh):
    split = Mesh(
        mesh.devices.reshape(mesh.shape["grp"], 8, 4, 2), ("grp", "blk_0", "blk_1", "blk_2")
    )
    in_specs = (
        P(GRP_BLK, None),
        P(GRP_BLK, None),
        P(GRP_BLK, None),
        P(GRP_BLK, None),
        P(None, GRP_BLK),
        P(GRP_BLK, None),
        P(),
        P(),
        P(),
        P(),
        P(),
        P(),
    )
    out_specs = P(GRP_BLK, None)
    return jax.shard_map(local, mesh=split, in_specs=in_specs, out_specs=out_specs, check_vma=False)
```

profile of v0, /device:TPU:1, one launch (start us, length us, event | category | flops | bytes accessed | tf_op | source)
XLA Modules:
  0.0 326.1 jit_solution(2322974837071484632)
XLA Ops:
  0.0 0.7 compare_select_fusion.14
  0.7 1.4 convolution_convert_fusion.3
  2.1 9.0 %gather_fusion = bf16[2048,256]{1,0:T(8,128)(2,1)} fusion(bf16[1024,256]{1,0:T(8,128)(2,1)S(1)} %convolution_convert_fusion.3, s32[2048]{0:T(1024)S(1)} %broadcast_clamp_fusion.2), kind=kCustom, calls=%fused_computation | custom fusion | bytes 2105344 | tf_op jit(solution)/shard_map/gather | solution.py:128
  11.1 15.6 %all-to-all-start = ((bf16[256,1,1,8,256]{4,3,2,1,0:T(8,128)(2,1)}), bf16[256,1,1,8,256]{4,3,2,1,0:T(8,128)(2,1)S(1)}, u32[]{:S(2)}, u32[]{:S(2)}) async-start(bf16[256,1,1,8,256]{4,3,2,1,0:T(8,128)(2,1)} %bitcast.77), calls=%async_computation | async-start | bytes 2097152 | tf_op jit(solution)/shard_map/all_to_all | solution.py:32
  27.2 9.0 %gather_fusion.2 = bf16[2048,256]{1,0:T(8,128)(2,1)} fusion(bf16[1024,256]{1,0:T(8,128)(2,1)S(1)} %convolution_convert_fusion.2, s32[2048]{0:T(1024)S(1)} %broadcast_clamp_fusion.1), kind=kCustom, calls=%fused_computation.2 | custom fusion | bytes 2105344 | tf_op jit(solution)/shard_map/gather | solution.py:70
  36.7 0.6 slice_convert_fusion
  37.3 0.6 slice_convert_fusion.1
  38.0 19.9 %all-to-all-done = bf16[256,1,1,8,256]{4,3,2,1,0:T(8,128)(2,1)S(1)} async-done(((bf16[256,1,1,8,256]{4,3,2,1,0:T(8,128)(2,1)}), bf16[256,1,1,8,256]{4,3,2,1,0:T(8,128)(2,1)S(1)}, u32[]{:S(2)}, u32[]{:S(2)}) %all-to-all-start) | async-done | bytes 1048608 | tf_op jit(solution)/shard_map/all_to_all | solution.py:32
  57.9 1.0 copy-done.1
  58.9 1.3 pad_maximum_fusion
  60.2 9.0 %gather_fusion.1 = bf16[2048,256]{1,0:T(8,128)(2,1)} fusion(bf16[3072,256]{1,0:T(8,128)(2,1)S(1)} %pad_maximum_fusion, s32[2048]{0:T(1024)S(1)} %broadcast_clamp_fusion), kind=kCustom, calls=%fused_computation.1 | custom fusion | bytes 2105344 | tf_op jit(solution)/shard_map/gather | solution.py:69
  69.2 3.8 %fusion.1 = f32[2048,8]{0,1:T(8,128)S(1)} fusion(bf16[2048,256]{1,0:T(8,128)(2,1)} %gather_fusion.1, bf16[2048,256]{1,0:T(8,128)(2,1)} %gather_fusion.2, f32[8,2048]{1,0:T(8,128)} %param.16, f32[256]{0:T(256)S(1)} %bitcast.96, s32[256]{0:T(256)S(1)} %and_select_fusion, pred[2048]{0:T(1024)(128)(4,1)S(1)} %compare_bitcast_fusion), kind=kOutput, calls=%fused_computation.31 | convolution fusion | flops 53514240 | bytes 2232320 | tf_op jit(solution)/shard_map/dot_general | solution.py:57
  73.4 11.6 %scatter_custom_fusion = f32[1024,8]{1,0:T(8,128)S(1)} fusion(s32[2048]{0:T(1024)S(1)} %bitcast.80, f32[2048,8]{1,0:T(8,128)S(1)} %copy.46, f32[]{:T(128)} %constant.47.clone.1), kind=kCustom, calls=%fused_computation.70 | custom fusion | flops 16384 | bytes 32772 | tf_op jit(solution)/shard_map/scatter-max | solution.py:77
  85.1 1.2 subtract_exponential_fusion.1
  87.2 5.5 %gather_fusion.3 = f32[2048,8]{1,0:T(8,128)S(1)} fusion(f32[1024,8]{1,0:T(8,128)S(1)} %copy.48, s32[2048]{0:T(1024)S(1)} %broadcast_clamp_fusion.1), kind=kCustom, calls=%fused_computation.3 | custom fusion | bytes 139264 | tf_op jit(solution)/shard_map/gather | solution.py:80
  93.0 0.7 exponential_select_fusion.1
  94.0 11.9 %scatter_fusion = f32[1024,8]{1,0:T(8,128)S(1)} fusion(f32[1024,8]{1,0:T(8,128)S(1)} %copy.50, s32[2048]{0:T(1024)S(1)} %bitcast.81, f32[2048,8]{1,0:T(8,128)S(1)} %copy.51), kind=kCustom, calls=%fused_computation.11 | custom fusion | flops 16384 | bytes 204800 | tf_op jit(solution)/shard_map/scatter-add | solution.py:83
  106.0 5.5 %gather_fusion.4 = f32[2048,8]{1,0:T(8,128)S(1)} fusion(f32[1024,8]{1,0:T(8,128)S(1)} %scatter_fusion, s32[2048]{0:T(1024)S(1)} %broadcast_clamp_fusion.1), kind=kCustom, calls=%fused_computation.4 | custom fusion | bytes 139264 | tf_op jit(solution)/shard_map/gather | solution.py:84
  111.7 1.3 copy.53
  113.6 1.9 copy.55
  115.4 1.7 convolution_add_fusion.3
  117.2 12.6 %scatter_custom_fusion.2 = f32[1024,256]{1,0:T(8,128)S(1)} fusion(f32[1024,256]{1,0:T(8,128)S(1)} %convolution_add_fusion.3, s32[2048]{0:T(1024)S(1)} %bitcast.82, f32[2048,256]{1,0:T(8,128)} %copy.55, bf16[2048,256]{1,0:T(8,128)(2,1)S(1)} %copy-done.4), kind=kCustom, calls=%fused_computation.32 | custom fusion | flops 1572864 | bytes 4194304 | tf_op jit(solution)/shard_map/scatter-add | solution.py:88
  129.9 6.5 %all-reduce.5 = (f32[256]{0:T(256)S(1)}, f32[256]{0:T(256)S(1)}) all-reduce(f32[256]{0:T(256)S(1)} %get-tuple-element.8, f32[256]{0:T(256)S(1)} %get-tuple-element.7), channel_id=1, replica_groups=mesh['grp'=4,'blk_0'=8,'blk_1'=4,'blk_2'=2] {'grp'}, use_global_device_ids=true, to_apply=%region_9.10 | all-reduce | flops 512 | bytes 4096 | tf_op jit(solution)/shard_map/psum | solution.py:38
  136.4 11.2 %all-reduce.1 = (f32[256]{0:T(256)S(1)}, f32[256]{0:T(256)S(1)}) all-reduce(f32[256]{0:T(256)S(1)} %get-tuple-element.19, f32[256]{0:T(256)S(1)} %get-tuple-element.20), channel_id=1, replica_groups=mesh['grp'=4,'blk_0'=8,'blk_1'=4,'blk_2'=2] {'blk_0'}, use_global_device_ids=true, to_apply=%region_10.11 | all-reduce | flops 512 | bytes 4096 | tf_op jit(solution)/shard_map/psum | solution.py:38
  147.7 7.8 %all-reduce.3 = (f32[256]{0:T(256)S(1)}, f32[256]{0:T(256)S(1)}) all-reduce(f32[256]{0:T(256)S(1)} %get-tuple-element.11, f32[256]{0:T(256)S(1)} %get-tuple-element.12), channel_id=1, replica_groups=mesh['grp'=4,'blk_0'=8,'blk_1'=4,'blk_2'=2] {'blk_1'}, use_global_device_ids=true, to_apply=%region_11.12 | all-reduce | flops 512 | bytes 4096 | tf_op jit(solution)/shard_map/psum | solution.py:38
  155.4 10.7 %all-reduce.7 = (f32[256]{0:T(256)S(1)}, f32[256]{0:T(256)S(1)}) all-reduce(f32[256]{0:T(256)S(1)} %get-tuple-element.15, f32[256]{0:T(256)S(1)} %get-tuple-element.16), channel_id=1, replica_groups=mesh['grp'=4,'blk_0'=8,'blk_1'=4,'blk_2'=2] {'blk_2'}, use_global_device_ids=true, to_apply=%region_12.13 | all-reduce | flops 512 | bytes 4096 | tf_op jit(solution)/shard_map/psum | solution.py:38
  167.0 9.0 %gather_fusion.5 = bf16[2048,256]{1,0:T(8,128)(2,1)} fusion(bf16[1024,256]{1,0:T(8,128)(2,1)S(1)} %convolution_convert_fusion.1, s32[2048]{0:T(1024)S(1)} %copy-done.12), kind=kCustom, calls=%fused_computation.5 | custom fusion | bytes 2105344 | tf_op jit(solution)/shard_map/gather | solution.py:128
  176.0 6.5 %all-to-all-start.1 = ((bf16[256,1,1,8,256]{4,3,2,1,0:T(8,128)(2,1)}), bf16[256,1,1,8,256]{4,3,2,1,0:T(8,128)(2,1)S(1)}, u32[]{:S(2)}, u32[]{:S(2)}) async-start(bf16[256,1,1,8,256]{4,3,2,1,0:T(8,128)(2,1)} %bitcast.78), calls=%async_computation.1 | async-start | bytes 2097152 | tf_op jit(solution)/shard_map/all_to_all | solution.py:32
  182.8 9.0 %gather_fusion.7 = bf16[2048,256]{1,0:T(8,128)(2,1)} fusion(bf16[1024,256]{1,0:T(8,128)(2,1)S(1)} %convolution_convert_fusion, s32[2048]{0:T(1024)S(1)} %broadcast_clamp_fusion.1), kind=kCustom, calls=%fused_computation.7 | custom fusion | bytes 2105344 | tf_op jit(solution)/shard_map/gather | solution.py:70
  191.8 21.8 %all-to-all-done.1 = bf16[256,1,1,8,256]{4,3,2,1,0:T(8,128)(2,1)S(1)} async-done(((bf16[256,1,1,8,256]{4,3,2,1,0:T(8,128)(2,1)}), bf16[256,1,1,8,256]{4,3,2,1,0:T(8,128)(2,1)S(1)}, u32[]{:S(2)}, u32[]{:S(2)}) %all-to-all-start.1) | async-done | bytes 1048608 | tf_op jit(solution)/shard_map/all_to_all | solution.py:32
  213.6 1.0 copy-done.2
  214.7 1.3 pad_maximum_fusion.1
  216.0 9.0 %gather_fusion.6 = bf16[2048,256]{1,0:T(8,128)(2,1)} fusion(bf16[3072,256]{1,0:T(8,128)(2,1)S(1)} %pad_maximum_fusion.1, s32[2048]{0:T(1024)S(1)} %copy-done.14), kind=kCustom, calls=%fused_computation.6 | custom fusion | bytes 2105344 | tf_op jit(solution)/shard_map/gather | solution.py:69
  225.1 3.8 %fusion = f32[2048,8]{0,1:T(8,128)S(1)} fusion(bf16[2048,256]{1,0:T(8,128)(2,1)} %gather_fusion.6, bf16[2048,256]{1,0:T(8,128)(2,1)} %gather_fusion.7, f32[8,2048]{1,0:T(8,128)S(1)} %copy-done.27, f32[256]{0:T(256)S(1)} %bitcast.94, s32[256]{0:T(256)S(1)} %copy-done.29, pred[2048]{0:T(1024)(128)(4,1)S(1)} %copy-done.16), kind=kOutput, calls=%fused_computation.29 | convolution fusion | flops 53514240 | bytes 2232320 | tf_op jit(solution)/shard_map/dot_general | solution.py:57
  229.2 11.8 %scatter_custom_fusion.3 = f32[1024,8]{1,0:T(8,128)S(1)} fusion(s32[2048]{0:T(1024)S(1)} %bitcast.83, f32[2048,8]{1,0:T(8,128)S(1)} %copy.57, f32[]{:T(128)} %constant.47.clone.1), kind=kCustom, calls=%fused_computation.68 | custom fusion | flops 16384 | bytes 32772 | tf_op jit(solution)/shard_map/scatter-max | solution.py:77
  241.2 1.2 subtract_exponential_fusion
  242.9 5.5 %gather_fusion.8 = f32[2048,8]{1,0:T(8,128)S(1)} fusion(f32[1024,8]{1,0:T(8,128)S(1)} %copy.59, s32[2048]{0:T(1024)S(1)} %broadcast_clamp_fusion.1), kind=kCustom, calls=%fused_computation.8 | custom fusion | bytes 139264 | tf_op jit(solution)/shard_map/gather | solution.py:80
  249.0 11.7 %scatter_fusion.1 = f32[1024,8]{1,0:T(8,128)S(1)} fusion(f32[1024,8]{1,0:T(8,128)S(1)} %copy.61, s32[2048]{0:T(1024)S(1)} %bitcast.84, f32[2048,8]{1,0:T(8,128)S(1)} %copy.62), kind=kCustom, calls=%fused_computation.14 | custom fusion | flops 16384 | bytes 204800 | tf_op jit(solution)/shard_map/scatter-add | solution.py:83
  260.9 7.6 %gather_fusion.9 = f32[2048,8]{1,0:T(8,128)} fusion(f32[1024,8]{1,0:T(8,128)S(1)} %scatter_fusion.1, s32[2048]{0:T(1024)S(1)} %broadcast_clamp_fusion.1), kind=kCustom, calls=%fused_computation.9 | custom fusion | bytes 139264 | tf_op jit(solution)/shard_map/gather | solution.py:84
  269.7 1.5 copy.65
  271.2 1.5 mul.131
  272.8 3.0 copy.66
  275.8 12.6 %scatter_custom_fusion.5 = f32[1024,256]{1,0:T(8,128)S(1)} fusion(f32[1024,256]{1,0:T(8,128)S(1)} %convolution_add_fusion.2, s32[2048]{0:T(1024)S(1)} %bitcast.85, f32[2048,256]{1,0:T(8,128)} %copy.66, bf16[2048,256]{1,0:T(8,128)(2,1)S(1)} %copy-done.3), kind=kCustom, calls=%fused_computation.33 | custom fusion | flops 1572864 | bytes 4194304 | tf_op jit(solution)/shard_map/scatter-add | solution.py:88
  288.5 6.5 %all-reduce.4 = (f32[256]{0:T(256)S(1)}, f32[256]{0:T(256)S(1)}) all-reduce(f32[256]{0:T(256)S(1)} %get-tuple-element.6, f32[256]{0:T(256)S(1)} %get-tuple-element.5), channel_id=1, replica_groups=mesh['grp'=4,'blk_0'=8,'blk_1'=4,'blk_2'=2] {'grp'}, use_global_device_ids=true, to_apply=%region_22.23 | all-reduce | flops 512 | bytes 4096 | tf_op jit(solution)/shard_map/psum | solution.py:38
  295.0 11.3 %all-reduce = (f32[256]{0:T(256)S(1)}, f32[256]{0:T(256)S(1)}) all-reduce(f32[256]{0:T(256)S(1)} %get-tuple-element.17, f32[256]{0:T(256)S(1)} %get-tuple-element.18), channel_id=1, replica_groups=mesh['grp'=4,'blk_0'=8,'blk_1'=4,'blk_2'=2] {'blk_0'}, use_global_device_ids=true, to_apply=%region_23.24 | all-reduce | flops 512 | bytes 4096 | tf_op jit(solution)/shard_map/psum | solution.py:38
  306.3 7.8 %all-reduce.2 = (f32[256]{0:T(256)S(1)}, f32[256]{0:T(256)S(1)}) all-reduce(f32[256]{0:T(256)S(1)} %get-tuple-element.9, f32[256]{0:T(256)S(1)} %get-tuple-element.10), channel_id=1, replica_groups=mesh['grp'=4,'blk_0'=8,'blk_1'=4,'blk_2'=2] {'blk_1'}, use_global_device_ids=true, to_apply=%region_24.25 | all-reduce | flops 512 | bytes 4096 | tf_op jit(solution)/shard_map/psum | solution.py:38
  314.1 10.7 %all-reduce.6 = (f32[256]{0:T(256)S(1)}, f32[256]{0:T(256)S(1)}) all-reduce(f32[256]{0:T(256)S(1)} %get-tuple-element.13, f32[256]{0:T(256)S(1)} %get-tuple-element.14), channel_id=1, replica_groups=mesh['grp'=4,'blk_0'=8,'blk_1'=4,'blk_2'=2] {'blk_2'}, use_global_device_ids=true, to_apply=%region_25.26 | all-reduce | flops 512 | bytes 4096 | tf_op jit(solution)/shard_map/psum | solution.py:38
  324.8 1.3 fusion.13
  (99 shorter events, 8.2 us)
Async XLA Ops:
  0.7 1.4 copy-start.11
  11.1 15.7 %copy-start.10 = (s32[16,128]{1,0:T(8,128)S(1)}, s32[16,128]{1,0:T(8,128)}, u32[]{:S(2)}) copy-start(s32[16,128]{1,0:T(8,128)} %param.14) | copy-start | bytes 24580
  11.1 15.7 %copy-start = (bf16[1024,256]{1,0:T(8,128)(2,1)S(1)}, bf16[1024,256]{1,0:T(8,128)(2,1)}, u32[]{:S(2)}) copy-start(bf16[1024,256]{1,0:T(8,128)(2,1)} %param.12) | copy-start | bytes 1572868
  11.1 15.7 %copy-start.6 = (bf16[2,256,256]{2,1,0:T(8,128)(2,1)S(1)}, bf16[2,256,256]{2,1,0:T(8,128)(2,1)}, u32[]{:S(2)}) copy-start(bf16[2,256,256]{2,1,0:T(8,128)(2,1)} %param.19) | copy-start | bytes 786436
  11.1 46.8 %all-to-all-start = ((bf16[256,1,1,8,256]{4,3,2,1,0:T(8,128)(2,1)}), bf16[256,1,1,8,256]{4,3,2,1,0:T(8,128)(2,1)S(1)}, u32[]{:S(2)}, u32[]{:S(2)}) async-start(bf16[256,1,1,8,256]{4,3,2,1,0:T(8,128)(2,1)} %bitcast.77), calls=%async_computation | async-start | bytes 2097152 | tf_op jit(solution)/shard_map/all_to_all | solution.py:32
  27.1 9.1 %copy-start.23 = (bf16[2,256]{1,0:T(2,128)(2,1)S(1)}, bf16[2,256]{1,0:T(2,128)(2,1)}, u32[]{:S(2)}) copy-start(bf16[2,256]{1,0:T(2,128)(2,1)} %param.21) | copy-start | bytes 3076
  27.1 9.6 %copy-start.24 = (bf16[2,256]{1,0:T(2,128)(2,1)S(1)}, bf16[2,256]{1,0:T(2,128)(2,1)}, u32[]{:S(2)}) copy-start(bf16[2,256]{1,0:T(2,128)(2,1)} %param.23) | copy-start | bytes 3076
  27.1 10.2 %copy-start.25 = (bf16[2,256]{1,0:T(2,128)(2,1)S(1)}, bf16[2,256]{1,0:T(2,128)(2,1)}, u32[]{:S(2)}) copy-start(bf16[2,256]{1,0:T(2,128)(2,1)} %param.22) | copy-start | bytes 3076
  27.2 10.8 %copy-start.17 = (s32[16,128]{1,0:T(8,128)S(1)}, s32[16,128]{1,0:T(8,128)}, u32[]{:S(2)}) copy-start(s32[16,128]{1,0:T(8,128)} %param.15) | copy-start | bytes 24580
  27.2 10.8 %copy-start.18 = (s32[16,128]{1,0:T(8,128)S(1)}, s32[16,128]{1,0:T(8,128)}, u32[]{:S(2)}) copy-start(s32[16,128]{1,0:T(8,128)} %param.13) | copy-start | bytes 24580
  36.2 49.0 %copy-start.28 = (s32[256]{0:T(256)}, s32[256]{0:T(256)S(1)}, u32[]{:S(2)}) copy-start(s32[256]{0:T(256)S(1)} %and_select_fusion) | copy-start | bytes 3076
  37.9 31.3 %copy-start.15 = (pred[2048]{0:T(1024)(128)(4,1)}, pred[2048]{0:T(1024)(128)(4,1)S(1)}, u32[]{:S(2)}) copy-start(pred[2048]{0:T(1024)(128)(4,1)S(1)} %compare_bitcast_fusion) | copy-start | bytes 6148
  38.0 31.2 %copy-start.13 = (s32[2048]{0:T(1024)}, s32[2048]{0:T(1024)S(1)}, u32[]{:S(2)}) copy-start(s32[2048]{0:T(1024)S(1)} %broadcast_clamp_fusion) | copy-start | bytes 24580
  57.9 1.0 copy-start.1
  86.4 0.6 copy-start.8
  106.0 5.5 %copy-start.9 = (f32[1024,8]{0,1:T(8,128)S(1)}, f32[1024,8]{0,1:T(8,128)}, u32[]{:S(2)}) copy-start(f32[1024,8]{0,1:T(8,128)} %copy-done.8) | copy-start | bytes 98308
  115.4 1.7 copy-start.4
  117.1 49.0 %copy-start.21 = (f32[1,256]{1,0:T(1,128)S(1)}, f32[1,256]{1,0:T(1,128)}, u32[]{:S(2)}) copy-start(f32[1,256]{1,0:T(1,128)} %get-tuple-element.34) | copy-start | bytes 3076
  117.1 49.0 %copy-start.22 = (f32[1,256]{1,0:T(1,128)S(1)}, f32[1,256]{1,0:T(1,128)}, u32[]{:S(2)}) copy-start(f32[1,256]{1,0:T(1,128)} %get-tuple-element.32) | copy-start | bytes 3076
  129.7 36.9 %copy-start.5 = (bf16[2,256,256]{2,1,0:T(8,128)(2,1)S(1)}, bf16[2,256,256]{2,1,0:T(8,128)(2,1)}, u32[]{:S(2)}) copy-start(bf16[2,256,256]{2,1,0:T(8,128)(2,1)} %param.18) | copy-start | bytes 786436
  129.7 37.2 %copy-start.12 = (s32[2048]{0:T(1024)S(1)}, s32[2048]{0:T(1024)}, u32[]{:S(2)}) copy-start(s32[2048]{0:T(1024)} %copy-done.11) | copy-start | bytes 24580
  176.0 37.7 %all-to-all-start.1 = ((bf16[256,1,1,8,256]{4,3,2,1,0:T(8,128)(2,1)}), bf16[256,1,1,8,256]{4,3,2,1,0:T(8,128)(2,1)S(1)}, u32[]{:S(2)}, u32[]{:S(2)}) async-start(bf16[256,1,1,8,256]{4,3,2,1,0:T(8,128)(2,1)} %bitcast.78), calls=%async_computation.1 | async-start | bytes 2097152 | tf_op jit(solution)/shard_map/all_to_all | solution.py:32
  191.8 24.2 %copy-start.14 = (s32[2048]{0:T(1024)S(1)}, s32[2048]{0:T(1024)}, u32[]{:S(2)}) copy-start(s32[2048]{0:T(1024)} %copy-done.13) | copy-start | bytes 24580
  213.6 1.0 copy-start.2
  216.0 9.0 %copy-start.16 = (pred[2048]{0:T(1024)(128)(4,1)S(1)}, pred[2048]{0:T(1024)(128)(4,1)}, u32[]{:S(2)}) copy-start(pred[2048]{0:T(1024)(128)(4,1)} %copy-done.15) | copy-start | bytes 6148
  216.0 9.0 %copy-start.26 = (f32[1,256]{1,0:T(1,128)S(1)}, f32[1,256]{1,0:T(1,128)}, u32[]{:S(2)}) copy-start(f32[1,256]{1,0:T(1,128)} %get-tuple-element.35) | copy-start | bytes 3076
  216.0 9.0 %copy-start.27 = (f32[8,2048]{1,0:T(8,128)S(1)}, f32[8,2048]{1,0:T(8,128)}, u32[]{:S(2)}) copy-start(f32[8,2048]{1,0:T(8,128)} %param.16) | copy-start | bytes 196612
  216.0 9.0 %copy-start.29 = (s32[256]{0:T(256)S(1)}, s32[256]{0:T(256)}, u32[]{:S(2)}) copy-start(s32[256]{0:T(256)} %copy-done.28) | copy-start | bytes 3076
  268.4 0.9 copy-start.7
  272.8 3.0 copy-start.3
  275.8 49.0 %copy-start.19 = (f32[1,256]{1,0:T(1,128)S(1)}, f32[1,256]{1,0:T(1,128)}, u32[]{:S(2)}) copy-start(f32[1,256]{1,0:T(1,128)} %get-tuple-element.33) | copy-start | bytes 3076
  275.8 49.0 %copy-start.20 = (f32[1,256]{1,0:T(1,128)S(1)}, f32[1,256]{1,0:T(1,128)}, u32[]{:S(2)}) copy-start(f32[1,256]{1,0:T(1,128)} %get-tuple-element.31) | copy-start | bytes 3076
where the time goes:
time: 327 us; the launch traced here: 326 us
  local copies, waits for them, and re-layouts  94.7 us (29%)
  other arithmetic  80.2 us (25%)
  blocking collectives  72.4 us (22%)
  waiting for transfers between devices  41.7 us (13%)
  starting transfers between devices  22.2 us (7%)
  matrix products  14.3 us (4%)
    psum x8, blocking collectives, by_axis(): return functools.reduce(lax.psum, axes, value)  72.4 us
    all_to_all x2, waiting for transfers between devices, exchange_both(): lax.all_to_all(pieces, axis, split_axis=0, concat_axis=0, tiled=True)  41.7 us
    scatter-add x2, other arithmetic, attend(): jax.ops.segment_sum(messages, targets, num_segments=node_count)  25.1 us
    scatter-add x2, other arithmetic, attend(): jax.ops.segment_sum(edge_weights, targets, num_segments=node_count)  23.6 us
    another operation x2, other arithmetic, attend(): seg_max = jax.ops.segment_max(scores, targets, num_segments=node_count)  23.4 us
    all_to_all x2, starting transfers between devices, exchange_both(): lax.all_to_all(pieces, axis, split_axis=0, concat_axis=0, tiled=True)  22.2 us
    gather x2, local copies, waits for them, and re-layouts, attend(): dst_rows = right_own[targets]  18 us
    gather x2, local copies, waits for them, and re-layouts, local(): left_own[send_list[0]]  18 us
  transfers between devices with their start and end apart: 2, of which 2 were waited for; matrix products, arithmetic and copies ran while one was open for 6% of the time, Pallas kernels for 0%

commit v1 on v0

v1 whole, which is shorter than its diff:
```python
import functools

import jax
import jax.numpy as jnp
from jax import lax
from jax.experimental import pallas as pl
from jax.experimental.pallas import tpu as pltpu
from jax.sharding import Mesh
from jax.sharding import PartitionSpec as P

HEADS = 8
LAYERS = 2
GRP_BLK = ("grp", "blk_0", "blk_1", "blk_2")
NODES_OWN = 1024
EDGES_OWN = 2048
ROWS_IN = 2048
FEAT = 256
CHUNK = 256
EDGE_CHUNKS = EDGES_OWN // CHUNK
NODE_CHUNKS = NODES_OWN // CHUNK
F32 = jnp.float32
BF16 = jnp.bfloat16


def iota(shape, dim):
    return lax.broadcasted_iota(jnp.int32, shape, dim)


def one_hot(mask):
    return jnp.where(mask, 1.0, 0.0).astype(BF16)


def dot(lhs, rhs):
    return jnp.dot(lhs, rhs, preferred_element_type=F32)


def dot_t(lhs, rhs):
    return lax.dot_general(lhs, rhs, (((1,), (1,)), ((), ())), preferred_element_type=F32)


def leaky(values):
    return jnp.where(values > 0, values, 0.2 * values)


def split_two(values):
    high = values.astype(BF16)
    return high, (values - high.astype(F32)).astype(BF16)


def split_three(values):
    high = values.astype(BF16)
    rest = values - high.astype(F32)
    mid = rest.astype(BF16)
    return high, mid, (rest - mid.astype(F32)).astype(BF16)


def head_rows(attn_ref, layer):
    shape = (16, FEAT)
    owner = iota(shape, 1) // (FEAT // HEADS) == iota(shape, 0)
    row = attn_ref[layer : layer + 1, :].astype(F32)
    return jnp.where(owner, row, 0.0).astype(BF16)


def head_spread():
    shape = (16, 2 * FEAT)
    return one_hot(iota(shape, 1) // (FEAT // HEADS) == iota(shape, 0))


def scores_of(heads, hidden):
    high, low = split_two(hidden)
    return (dot_t(heads, high) + dot_t(heads, low))[:HEADS]


def norm_terms(stats, total_nodes, gain, shift):
    mean = stats[0:1, :] / total_nodes
    spread = jnp.maximum(stats[1:2, :] / total_nodes - mean * mean, 0.0)
    return mean, lax.rsqrt(spread + 0.1), gain, shift


def normalize(values, terms):
    mean, inv, gain, shift = terms
    scaled = (values - mean) * inv * gain + shift
    grown = jnp.exp(jnp.minimum(scaled, 0.0)) - 1.0
    return jnp.where(scaled > 0, scaled, grown).astype(BF16)


def columns_of(row):
    return jnp.transpose(jnp.broadcast_to(row, (8, row.shape[1])))


def pick_rows(list_ref, table_ref, out_ref, col_ref):
    col_ref[...] = columns_of(list_ref[...].astype(F32)).astype(jnp.int32)

    def step(c, carry):
        at = pl.ds(pl.multiple_of(c * CHUNK, CHUNK), CHUNK)
        hot = one_hot(col_ref[at, 0:1] == iota((CHUNK, NODES_OWN), 1))
        out_ref[at, :] = dot(hot, table_ref[...]).astype(BF16)
        return carry

    lax.fori_loop(0, ROWS_IN // CHUNK, step, 0)


def send_kernel(list_ref, table_ref, out_ref, col_ref):
    pick_rows(list_ref, table_ref, out_ref, col_ref)


def sort_kernel(
    src_ref, tgt_ref, valid_ref, bias_ref, rows_ref, cols_ref, bias_out, noedge_ref, bound_ref,
    key_ref, pos_ref, meta_ref,
):
    width = (1, EDGES_OWN)
    live_in = valid_ref[...] > 0
    src = src_ref[...]
    tgt = jnp.where(live_in, tgt_ref[...], NODES_OWN)
    key = tgt * EDGES_OWN + iota(width, 1)
    key_ref[...] = columns_of(key.astype(F32)).astype(jnp.int32)
    pos_ref[...] = jnp.zeros_like(pos_ref)

    def rank(c, carry):
        at = pl.ds(pl.multiple_of(c * CHUNK, CHUNK), CHUNK)
        less = jnp.where(key_ref[at, 0:1] < key, 1.0, 0.0)
        pos_ref[...] += jnp.sum(less, axis=0, keepdims=True)
        return carry

    lax.fori_loop(0, EDGE_CHUNKS, rank, 0)
    pos = pos_ref[...].astype(jnp.int32)
    sub = iota((8, EDGES_OWN), 0)
    ints = jnp.where(
        sub == 0,
        src // 256,
        jnp.where(sub == 1, src % 256, jnp.where(sub == 2, tgt // 256, tgt % 256)),
    )
    high, mid, low = split_three(bias_ref[...])
    meta = jnp.concatenate(
        [ints.astype(F32), high.astype(F32), mid.astype(F32), low.astype(F32)], axis=0
    ).astype(BF16)

    def place(c, carry):
        at = pl.ds(pl.multiple_of(c * CHUNK, CHUNK), CHUNK)
        perm = one_hot(pos == iota((CHUNK, EDGES_OWN), 0) + c * CHUNK)
        meta_ref[:, at] = dot_t(meta, perm)
        return carry

    lax.fori_loop(0, EDGE_CHUNKS, place, 0)
    placed = meta_ref[...]
    bias_out[...] = placed[8:16] + placed[16:24] + placed[24:32]
    src_s = (placed[0:1] * 256.0 + placed[1:2]).astype(jnp.int32)
    tgt_s = (placed[2:3] * 256.0 + placed[3:4]).astype(jnp.int32)
    lane8 = iota((8, EDGES_OWN), 1)
    both = jnp.where(sub == 0, src_s, tgt_s)
    cols_ref[...] = jnp.transpose(both.astype(F32)).astype(jnp.int32)
    tgt8 = jnp.broadcast_to(tgt_s, (8, EDGES_OWN))
    before = pltpu.roll(tgt8, 1, 1)
    after = pltpu.roll(tgt8, EDGES_OWN - 1, 1)
    live = tgt8 < NODES_OWN
    first = (lane8 == 0) | (before != tgt8)
    last = (lane8 == EDGES_OWN - 1) | (after != tgt8)
    start = jnp.where(first, lane8, 0)
    end = jnp.where(last, lane8, EDGES_OWN)
    step = 1
    while step < EDGES_OWN:
        start = jnp.maximum(start, jnp.where(lane8 >= step, pltpu.roll(start, step, 1), 0))
        shifted = pltpu.roll(end, EDGES_OWN - step, 1)
        end = jnp.minimum(end, jnp.where(lane8 + step < EDGES_OWN, shifted, EDGES_OWN))
        step *= 2
    start = jnp.where(live, start, lane8)
    end = jnp.where(live, end, lane8)
    rows_ref[...] = jnp.where(
        sub == 0, tgt8, jnp.where(sub == 1, start, jnp.where(sub == 2, end, lane8))
    )
    bound_ref[0, 2 * EDGE_CHUNKS] = jnp.max(end - start) + 1
    for c in range(EDGE_CHUNKS):
        piece = tgt8[:, c * CHUNK : (c + 1) * CHUNK]
        bound_ref[0, 2 * c] = jnp.min(piece)
        bound_ref[0, 2 * c + 1] = jnp.max(jnp.where(piece < NODES_OWN, piece, -1))
    for k in range(NODE_CHUNKS):
        hit = jnp.where(iota((CHUNK, EDGES_OWN), 0) + k * CHUNK == tgt_s, 1.0, 0.0)
        found = jnp.max(hit, axis=1, keepdims=True)
        noedge_ref[k * CHUNK : (k + 1) * CHUNK, :] = jnp.broadcast_to(1.0 - found, (CHUNK, 8))


def own_kernel(
    layer, total_nodes, with_norm, *refs,
):
    if with_norm:
        (state_ref, stats_ref, gain_ref, shift_ref, wl_ref, wr_ref, ws_ref, attn_ref, cols_ref,
         left_ref, base_ref, src_out, dst_out, self_out, right_ref) = refs
        terms = norm_terms(
            stats_ref[...],
            total_nodes,
            gain_ref[layer - 1 : layer, :].astype(F32),
            shift_ref[layer - 1 : layer, :].astype(F32),
        )
    else:
        (state_ref, wl_ref, wr_ref, ws_ref, attn_ref, cols_ref,
         left_ref, base_ref, src_out, dst_out, self_out, right_ref) = refs
    heads = head_rows(attn_ref, layer)
    self_parts = []
    for k in range(NODE_CHUNKS):
        at = slice(k * CHUNK, (k + 1) * CHUNK)
        states = state_ref[at, :]
        if with_norm:
            states = normalize(states, terms)
        left = dot(states, wl_ref[layer]).astype(BF16)
        right = dot(states, wr_ref[layer]).astype(BF16)
        left_ref[at, :] = left
        right_ref[at, :] = right
        base_ref[at, :] = states.astype(F32) + dot(states, ws_ref[layer])
        self_parts.append(scores_of(heads, leaky(left.astype(F32) + right.astype(F32))))
    own = jnp.concatenate(self_parts, axis=1)
    high, mid, low = split_three(own)
    own32 = jnp.concatenate(
        [high.astype(F32), mid.astype(F32), low.astype(F32), jnp.zeros_like(own)], axis=0
    ).astype(BF16)

    def step(c, carry):
        at = pl.ds(pl.multiple_of(c * CHUNK, CHUNK), CHUNK)
        node_ids = iota((CHUNK, NODES_OWN), 1)
        hot = one_hot(cols_ref[at, 1:2] == node_ids)
        dst_out[at, :] = dot(hot, right_ref[...]).astype(BF16)
        back = dot_t(own32, hot)
        self_out[:, at] = back[0:8] + back[8:16] + back[16:24]
        hot = one_hot(cols_ref[at, 0:1] == node_ids)
        src_out[at, :] = dot(hot, left_ref[...]).astype(BF16)
        return carry

    lax.fori_loop(0, EDGE_CHUNKS, step, 0)


def scan_both(ref, bound, lane, start, end, join, neutral):
    ref[0] = ref[2]
    ref[1] = ref[2]
    step = 1
    while step < EDGES_OWN:

        def advance(step=step):
            ahead = ref[0]
            back = ref[1]
            moved = pltpu.roll(ahead, step, 1)
            ref[0] = join(ahead, jnp.where(lane - step >= start, moved, neutral))
            moved = pltpu.roll(back, EDGES_OWN - step, 1)
            ref[1] = join(back, jnp.where(lane + step <= end, moved, neutral))

        pl.when(bound > step)(advance)
        step *= 2
    return ref[0], ref[1]


def edge_kernel(layer, total_nodes, with_norm, with_send, *refs):
    refs = list(refs)
    recv_ref, wl_ref, attn_ref, src_in, dst_in, self_ref, rows_ref, cols_ref, bias_ref = refs[:9]
    noedge_ref, bound_ref, left_ref, base_ref = refs[9:13]
    refs = refs[13:]
    if with_norm:
        stats_in, gain_ref, shift_ref = refs[:3]
        refs = refs[3:]
    if with_send:
        list_ref = refs.pop(0)
    summed_ref, stats_ref = refs[:2]
    refs = refs[2:]
    if with_send:
        send_ref = refs.pop(0)
    table_ref, edge_ref, score_ref, scan_ref, mix_ref, acc_ref = refs[:6]
    refs = refs[6:]
    if with_send:
        round_ref, col_ref = refs
    if with_norm:
        terms = norm_terms(
            stats_in[...],
            total_nodes,
            gain_ref[layer - 1 : layer, :].astype(F32),
            shift_ref[layer - 1 : layer, :].astype(F32),
        )
    heads = head_rows(attn_ref, layer)

    def fill(c, carry):
        at = pl.ds(pl.multiple_of(c * CHUNK, CHUNK), CHUNK)
        states = recv_ref[at, :]
        if with_norm:
            states = normalize(states.astype(F32), terms)
        table_ref[at, :] = dot(states, wl_ref[layer]).astype(BF16)
        return carry

    lax.fori_loop(0, ROWS_IN // CHUNK, fill, 0)

    def score(c, carry):
        at = pl.ds(pl.multiple_of(c * CHUNK, CHUNK), CHUNK)
        hot = one_hot(cols_ref[at, 0:1] - NODES_OWN == iota((CHUNK, ROWS_IN), 1))
        src = dot(hot, table_ref[...]) + src_in[at, :].astype(F32)
        edge_ref[at, :] = src.astype(BF16)
        score_ref[:, at] = scores_of(heads, leaky(src + dst_in[at, :].astype(F32)))
        return carry

    lax.fori_loop(0, EDGE_CHUNKS, score, 0)

    tgt = rows_ref[0:1, :]
    start = rows_ref[1:2, :]
    end = rows_ref[2:3, :]
    lane = iota((8, EDGES_OWN), 1)
    live = tgt < NODES_OWN
    longest = bound_ref[0, 2 * EDGE_CHUNKS]
    scores = jnp.where(live, score_ref[...] + bias_ref[...], -1e30)
    own = self_ref[...]
    scan_ref[2] = scores
    ahead, back = scan_both(scan_ref, longest, lane, start, end, jnp.maximum, -1e30)
    top = jnp.maximum(jnp.maximum(ahead, back), own)
    weights = jnp.where(live, jnp.exp(scores - top), 0.0)
    own_weights = jnp.exp(own - top)
    scan_ref[2] = weights
    ahead, back = scan_both(scan_ref, longest, lane, start, end, jnp.add, 0.0)
    denom = own_weights + (ahead + (back - weights))
    score_ref[...] = weights / denom
    last = live & (lane == end)
    scan_ref[0] = jnp.where(last, own_weights / denom, 0.0)
    spread = head_spread()

    def mix(c, carry):
        at = pl.ds(pl.multiple_of(c * CHUNK, CHUNK), CHUNK)
        pair = jnp.concatenate([score_ref[:, at], scan_ref[0, :, at]], axis=0)
        wide = dot(jnp.transpose(pair).astype(BF16), spread)
        mix_ref[at, :FEAT] = (wide[:, :FEAT] * edge_ref[at, :].astype(F32)).astype(BF16)
        mix_ref[at, FEAT:] = wide[:, FEAT:].astype(BF16)
        return carry

    lax.fori_loop(0, EDGE_CHUNKS, mix, 0)
    stats_ref[...] = jnp.zeros_like(stats_ref)
    for k in range(NODE_CHUNKS):
        at = slice(k * CHUNK, (k + 1) * CHUNK)
        acc_ref[...] = jnp.zeros_like(acc_ref)

        def gather_in(c, carry, k=k):
            near = (bound_ref[0, 2 * c] < (k + 1) * CHUNK) & (
                bound_ref[0, 2 * c + 1] >= k * CHUNK
            )

            def add():
                here = pl.ds(pl.multiple_of(c * CHUNK, CHUNK), CHUNK)
                hot = one_hot(iota((CHUNK, CHUNK), 0) + k * CHUNK == rows_ref[0:1, here])
                acc_ref[...] += dot(hot, mix_ref[here, :])

            pl.when(near)(add)
            return carry

        lax.fori_loop(0, EDGE_CHUNKS, gather_in, 0)
        own_alpha = jnp.where(noedge_ref[at, 0:1] > 0, 1.0, acc_ref[:, FEAT:])
        message = acc_ref[:, :FEAT] + own_alpha * left_ref[at, :].astype(F32)
        summed = base_ref[at, :] + message
        summed_ref[at, :] = summed
        stats_ref[0:1, :] += jnp.sum(summed, axis=0, keepdims=True)
        stats_ref[1:2, :] += jnp.sum(summed * summed, axis=0, keepdims=True)
        if with_send:
            round_ref[at, :] = summed.astype(BF16)
    if with_send:
        pick_rows(list_ref, round_ref, send_ref, col_ref)


def norm_kernel(layer, total_nodes, summed_ref, stats_ref, gain_ref, shift_ref, out_ref):
    terms = norm_terms(
        stats_ref[...],
        total_nodes,
        gain_ref[layer : layer + 1, :].astype(F32),
        shift_ref[layer : layer + 1, :].astype(F32),
    )
    out_ref[...] = normalize(summed_ref[...], terms)


def shaped(rows, cols, dtype):
    return jax.ShapeDtypeStruct((rows, cols), dtype)


SMEM = pl.BlockSpec(memory_space=pltpu.SMEM)
VMEM = pl.BlockSpec(memory_space=pltpu.VMEM)


def call(body, name, outs, scratch, flops, args, in_specs=None, out_specs=None):
    cost = pl.CostEstimate(flops=flops, bytes_accessed=4 << 20, transcendentals=0)
    return pl.pallas_call(
        body,
        name=name,
        out_shape=outs,
        in_specs=in_specs or [VMEM] * len(args),
        out_specs=out_specs or [VMEM] * len(outs),
        scratch_shapes=scratch,
        cost_estimate=cost,
    )(*args)


GIGA = 1 << 30


def send_rows(send_list, table):
    return call(
        send_kernel,
        "send_rows",
        [shaped(ROWS_IN, FEAT, BF16)],
        [pltpu.VMEM((ROWS_IN, 8), jnp.int32)],
        GIGA,
        [send_list, table],
    )[0]


def sort_edges(sources, targets, valids, bias):
    return call(
        sort_kernel,
        "sort_edges",
        [
            shaped(8, EDGES_OWN, jnp.int32),
            shaped(EDGES_OWN, 8, jnp.int32),
            shaped(8, EDGES_OWN, F32),
            shaped(NODES_OWN, 8, F32),
            shaped(1, 32, jnp.int32),
        ],
        [
            pltpu.VMEM((EDGES_OWN, 8), jnp.int32),
            pltpu.VMEM((1, EDGES_OWN), F32),
            pltpu.VMEM((32, EDGES_OWN), F32),
        ],
        2 * GIGA,
        [sources, targets, valids, bias],
        out_specs=[VMEM, VMEM, VMEM, VMEM, SMEM],
    )


def own_part(layer, total_nodes, args):
    with_norm = layer > 0
    return call(
        functools.partial(own_kernel, layer, total_nodes, with_norm),
        "own_part",
        [
            shaped(NODES_OWN, FEAT, BF16),
            shaped(NODES_OWN, FEAT, F32),
            shaped(EDGES_OWN, FEAT, BF16),
            shaped(EDGES_OWN, FEAT, BF16),
            shaped(8, EDGES_OWN, F32),
        ],
        [pltpu.VMEM((NODES_OWN, FEAT), BF16)],
        3 * GIGA,
        args,
    )


def edge_part(layer, total_nodes, with_send, args):
    with_norm = layer > 0
    outs = [shaped(NODES_OWN, FEAT, F32), shaped(2, FEAT, F32)]
    scratch = [
        pltpu.VMEM((ROWS_IN, FEAT), BF16),
        pltpu.VMEM((EDGES_OWN, FEAT), BF16),
        pltpu.VMEM((8, EDGES_OWN), F32),
        pltpu.VMEM((3, 8, EDGES_OWN), F32),
        pltpu.VMEM((EDGES_OWN, 2 * FEAT), BF16),
        pltpu.VMEM((CHUNK, 2 * FEAT), F32),
    ]
    if with_send:
        outs.append(shaped(ROWS_IN, FEAT, BF16))
        scratch += [pltpu.VMEM((NODES_OWN, FEAT), BF16), pltpu.VMEM((ROWS_IN, 8), jnp.int32)]
    in_specs = [VMEM] * len(args)
    in_specs[10] = SMEM
    return call(
        functools.partial(edge_kernel, layer, total_nodes, with_norm, with_send),
        "edge_part",
        outs,
        scratch,
        5 * GIGA,
        args,
        in_specs=in_specs,
    )


def deliver(rows):
    return lax.all_to_all(
        rows.reshape(-1, 8, rows.shape[1]), GRP_BLK, split_axis=0, concat_axis=0, tiled=True
    ).reshape(rows.shape)


def shifted(value, axis, amount):
    size = lax.axis_size(axis)
    return lax.ppermute(value, axis, [(i, (i + amount) % size) for i in range(size)])


def total_inside(stats):
    stats = stats + shifted(stats, "blk_2", 1)
    for axis in ("blk_1", "grp"):
        stats = stats + (
            shifted(stats, axis, 1) + shifted(stats, axis, 2) + shifted(stats, axis, 3)
        )
    stats = stats + (
        shifted(stats, "blk_0", 2) + shifted(stats, "blk_0", 4) + shifted(stats, "blk_0", 6)
    )
    return stats + shifted(stats, "blk_0", 1)


def total_alone(stats):
    for axes in (("blk_1", "blk_2"), ("grp", "blk_0")):
        size = lax.axis_size(axes)
        copies = jnp.broadcast_to(stats[None], (size,) + stats.shape)
        stats = jnp.sum(lax.all_to_all(copies, axes, 0, 0, tiled=True), axis=0)
    return stats


def local(
    features,
    source_index,
    target_index,
    edge_valid,
    edge_bias,
    send_list,
    w_left,
    w_right,
    w_skip,
    attn_vec,
    norm_gain,
    norm_shift,
    peers,
):
    total_nodes = float(features.shape[0] * peers)
    row = (1, EDGES_OWN)
    sent = send_rows(send_list, features)
    received = deliver(sent)
    rows, cols, bias, noedge, bound = sort_edges(
        source_index.reshape(row), target_index.reshape(row), edge_valid.reshape(row), edge_bias
    )
    weights = [w_left, w_right, w_skip, attn_vec, cols]
    left, base, src, dst, own = own_part(0, total_nodes, [features] + weights)
    tail = [rows, cols, bias, noedge, bound]
    summed, stats, sent = edge_part(
        0,
        total_nodes,
        True,
        [received, w_left, attn_vec, src, dst, own] + tail + [left, base, send_list],
    )
    received = deliver(sent)
    stats = total_inside(stats)
    norms = [stats, norm_gain, norm_shift]
    left, base, src, dst, own = own_part(1, total_nodes, [summed] + norms + weights)
    summed, stats = edge_part(
        1,
        total_nodes,
        False,
        [received, w_left, attn_vec, src, dst, own] + tail + [left, base] + norms,
    )
    stats = total_alone(stats)
    return call(
        functools.partial(norm_kernel, 1, total_nodes),
        "norm_out",
        [shaped(NODES_OWN, FEAT, BF16)],
        [],
        1 << 20,
        [summed, stats, norm_gain, norm_shift],
    )[0]


def solution(mesh):
    split = Mesh(
        mesh.devices.reshape(mesh.shape["grp"], 8, 4, 2), ("grp", "blk_0", "blk_1", "blk_2")
    )
    edge = P(GRP_BLK, None)
    in_specs = (edge,) * 4 + (P(None, GRP_BLK), edge) + (P(),) * 6
    return jax.shard_map(
        functools.partial(local, peers=mesh.size),
        mesh=split,
        in_specs=in_specs,
        out_specs=edge,
        check_vma=False,
    )
```

time: 327 us -> 172 us (0.53)
  local copies, waits for them, and re-layouts: 94.7 us -> 2.65 us
  other arithmetic: 80.2 us -> 1.25 us
  Pallas kernels: 0 us -> 76.2 us
  blocking collectives: 72.4 us -> 26.4 us
  starting transfers between devices: 22.2 us -> 38.4 us
  waiting for transfers between devices: 41.7 us -> 26.7 us
  matrix products: 14.3 us -> 0 us
    gather x14 -> x0, local copies, waits for them, and re-layouts: 80.4 us -> none  [the longest x2 18 us: attend(): dst_rows = right_own[targets]]
    pallas_call x0 -> x7, Pallas kernels: none -> 76.2 us  [call(): pl.pallas_call(body, name=name, out_shape=outs, in_specs=in_specs or [VME...]
    psum x8 -> x0, blocking collectives: 72.4 us -> none  [by_axis(): return functools.reduce(lax.psum, axes, value)]
    scatter-add x4 -> x0, other arithmetic: 48.7 us -> none  [the longest x2 25.1 us: attend(): jax.ops.segment_sum(messages, targets, num_segments=node_count)]
    all_to_all x2, waiting for transfers between devices: 41.7 us -> 11.9 us  [deliver(): lax.all_to_all(rows.reshape(-1, 8, rows.shape[1]), GRP_BLK, split_axis=0,...]
    all_to_all x0 -> x2, blocking collectives: none -> 26.4 us  [total_alone(): stats = jnp.sum(lax.all_to_all(copies, axes, 0, 0, tiled=True), axis=0)]
    another operation x2 -> x0, other arithmetic: 23.4 us -> none  [attend(): seg_max = jax.ops.segment_max(scores, targets, num_segments=node_count)]
    ppermute x0 -> x11, starting transfers between devices: none -> 16.8 us  [shifted(): lax.ppermute(value, axis, [(i, (i + amount) % size) for i in range(size)])]
  transfers between devices with their start and end apart: 2 -> 13, of which waited for: 2 -> 9; matrix products, arithmetic and copies ran while one was open for 6% -> 0% of each run, Pallas kernels for 0% -> 17%
where the time goes in v1:
time: 172 us
  Pallas kernels  76.2 us (44%)
  starting transfers between devices  38.4 us (22%)
  waiting for transfers between devices  26.7 us (16%)
  blocking collectives  26.4 us (15%)
  local copies, waits for them, and re-layouts  2.65 us (2%)
    pallas_call x7, Pallas kernels, call(): pl.pallas_call(body, name=name, out_shape=outs, in_specs=in_specs or [VME...  76.2 us
    all_to_all x2, blocking collectives, total_alone(): stats = jnp.sum(lax.all_to_all(copies, axes, 0, 0, tiled=True), axis=0)  26.4 us
    all_to_all x2, starting transfers between devices, deliver(): lax.all_to_all(rows.reshape(-1, 8, rows.shape[1]), GRP_BLK, split_axis=0,...  21.6 us
    ppermute x11, starting transfers between devices, shifted(): lax.ppermute(value, axis, [(i, (i + amount) % size) for i in range(size)])  16.8 us
    ppermute x11, waiting for transfers between devices, shifted(): lax.ppermute(value, axis, [(i, (i + amount) % size) for i in range(size)])  14.8 us
    all_to_all x2, waiting for transfers between devices, deliver(): lax.all_to_all(rows.reshape(-1, 8, rows.shape[1]), GRP_BLK, split_axis=0,...  11.9 us
  transfers between devices with their start and end apart: 13, of which 9 were waited for; matrix products, arithmetic and copies ran while one was open for 0% of the time, Pallas kernels for 17%

profile of v1, /device:TPU:1, one launch (start us, length us, event | category | flops | bytes accessed | tf_op | source)
XLA Modules:
  0.0 171.6 jit_solution(18350816672538123701)
XLA Ops:
  0.0 5.6 %send_rows.1 = bf16[2048,256]{1,0:T(8,128)(2,1)} custom-call(s32[1,2048]{1,0:T(1,128)} %refs_13_.1, bf16[1024,256]{1,0:T(8,128)(2,1)} %refs_0_.1), custom_call_target="tpu_custom_call" | custom-call | flops 1073741824 | bytes 4194304 | tf_op jit(solution)/shard_map/send_rows/pallas_call | solution.py:377
  5.6 15.6 %all-to-all-start = ((bf16[256,8,256]{2,1,0:T(8,128)(2,1)}), bf16[256,8,256]{2,1,0:T(8,128)(2,1)S(1)}, u32[]{:S(2)}, u32[]{:S(2)}) async-start(bf16[256,8,256]{2,1,0:T(8,128)(2,1)} %bitcast.10), calls=%async_computation | async-start | bytes 2097152 | tf_op jit(solution)/shard_map/all_to_all | solution.py:470
  21.2 9.8 %sort_edges.1 = (s32[8,2048]{1,0:T(8,128)}, s32[2048,8]{1,0:T(8,128)}, f32[8,2048]{1,0:T(8,128)}, f32[1024,8]{1,0:T(8,128)}, s32[1,32]{1,0:T(1,128)}) custom-call(s32[1,2048]{1,0:T(1,128)} %bitcast.11, s32[1,2048]{1,0:T(1,128)} %bitcast.12, s32[1,2048]{1,0:T(1,128)} %bitcast.13, f32[8,2048]{1,0:T(8,128)} %bias_ref.1), custom_call_target="tpu_custom_call" | custom-call | flops 2147483648 | bytes 4194304 | tf_op jit(solution)/shard_map/sort_edges/pallas_call | solution.py:377
  31.1 9.4 %own_part.2 = (bf16[1024,256]{1,0:T(8,128)(2,1)}, f32[1024,256]{1,0:T(8,128)}, bf16[2048,256]{1,0:T(8,128)(2,1)}, bf16[2048,256]{1,0:T(8,128)(2,1)}, f32[8,2048]{1,0:T(8,128)}) custom-call(bf16[1024,256]{1,0:T(8,128)(2,1)} %refs_0_.1, bf16[2,256,256]{2,1,0:T(8,128)(2,1)} %refs_1_.5, bf16[2,256,256]{2,1,0:T(8,128)(2,1)} %refs_5_.1, ...), custom_call_target="tpu_custom_call" | custom-call | flops 3221225472 | bytes 4194304 | tf_op jit(solution)/shard_map/own_part/pallas_call | solution.py:377
  40.4 11.9 %all-to-all-done = bf16[256,8,256]{2,1,0:T(8,128)(2,1)S(1)} async-done(((bf16[256,8,256]{2,1,0:T(8,128)(2,1)}), bf16[256,8,256]{2,1,0:T(8,128)(2,1)S(1)}, u32[]{:S(2)}, u32[]{:S(2)}) %all-to-all-start) | async-done | bytes 1048608 | tf_op jit(solution)/shard_map/all_to_all | solution.py:470
  52.3 0.0 copy-start.1
  52.3 1.0 copy-done.1
  53.3 21.2 %edge_part.2 = (f32[1024,256]{1,0:T(8,128)}, f32[2,256]{1,0:T(2,128)}, bf16[2048,256]{1,0:T(8,128)(2,1)}) custom-call(bf16[2048,256]{1,0:T(8,128)(2,1)} %bitcast.9, bf16[2,256,256]{2,1,0:T(8,128)(2,1)} %refs_1_.5, bf16[2,256]{1,0:T(2,128)(2,1)} %refs_2_.7, bf16[2048,256]{1,0:T(8,128)(2,1)} %get-tuple-element.26.refs_3_, ...), custom_call_target="tpu_custom_call" | custom-call | flops 5368709120 | bytes 4194304 | tf_op jit(solution)/shard_map/edge_part/pallas_call | solution.py:377
  74.6 0.0 copy-start.2
  74.6 5.9 %all-to-all-start.1 = ((bf16[256,8,256]{2,1,0:T(8,128)(2,1)}), bf16[256,8,256]{2,1,0:T(8,128)(2,1)S(1)}, u32[]{:S(2)}, u32[]{:S(2)}) async-start(bf16[256,8,256]{2,1,0:T(8,128)(2,1)} %bitcast.8), calls=%async_computation.1 | async-start | bytes 2097152 | tf_op jit(solution)/shard_map/all_to_all | solution.py:470
  80.5 0.0 copy-done.2
  80.5 2.2 %collective-permute-start = (f32[2,256]{1,0:T(2,128)S(1)}, f32[2,256]{1,0:T(2,128)S(1)}, u32[]{:S(2)}, u32[]{:S(2)}) collective-permute-start(f32[2,256]{1,0:T(2,128)S(1)} %copy-done.2), channel_id=1, source_target_pairs={{0,1},{1,0},{2,3},{3,2},{4,5},{5,4},{6,7},{7,6},{8,9},{9,8},{10,11... | collective-permute-start | bytes 6152 | tf_op jit(solution)/shard_map/ppermute | solution.py:477
  82.7 0.8 collective-permute-done
  83.6 0.8 collective-permute-start.3
  84.4 0.6 collective-permute-start.2
  85.0 0.6 collective-permute-start.1
  85.5 0.8 collective-permute-done.3
  86.3 2.3 %collective-permute-done.2 = f32[2,256]{1,0:T(2,128)S(1)} collective-permute-done((f32[2,256]{1,0:T(2,128)S(1)}, f32[2,256]{1,0:T(2,128)S(1)}, u32[]{:S(2)}, u32[]{:S(2)}) %collective-permute-start.2) | collective-permute-done | bytes 2080 | tf_op jit(solution)/shard_map/ppermute | solution.py:477
  88.6 0.4 collective-permute-done.1
  89.0 2.6 %collective-permute-start.6 = (f32[2,256]{1,0:T(2,128)S(1)}, f32[2,256]{1,0:T(2,128)S(1)}, u32[]{:S(2)}, u32[]{:S(2)}) collective-permute-start(f32[2,256]{1,0:T(2,128)S(1)} %add_add_fusion.2), channel_id=1, source_target_pairs={{0,192},{64,0},{128,64},{192,128},{1,193},{65,1},{129,65},{193,129... | collective-permute-start | bytes 6152 | tf_op jit(solution)/shard_map/ppermute | solution.py:477
  91.6 0.4 collective-permute-start.5
  92.1 0.7 collective-permute-start.4
  92.7 0.0 collective-permute-done.6
  92.7 3.1 %collective-permute-done.5 = f32[2,256]{1,0:T(2,128)S(1)} collective-permute-done((f32[2,256]{1,0:T(2,128)S(1)}, f32[2,256]{1,0:T(2,128)S(1)}, u32[]{:S(2)}, u32[]{:S(2)}) %collective-permute-start.5) | collective-permute-done | bytes 2080 | tf_op jit(solution)/shard_map/ppermute | solution.py:477
  95.9 0.1 collective-permute-done.4
  96.0 4.7 %collective-permute-start.9 = (f32[2,256]{1,0:T(2,128)S(1)}, f32[2,256]{1,0:T(2,128)S(1)}, u32[]{:S(2)}, u32[]{:S(2)}) collective-permute-start(f32[2,256]{1,0:T(2,128)S(1)} %add_add_fusion.1), channel_id=1, source_target_pairs={{0,48},{8,56},{16,0},{24,8},{32,16},{40,24},{48,32},{56,40},{1,49}... | collective-permute-start | bytes 6152 | tf_op jit(solution)/shard_map/ppermute | solution.py:477
  100.7 1.3 collective-permute-start.8
  102.1 2.3 %collective-permute-start.7 = (f32[2,256]{1,0:T(2,128)S(1)}, f32[2,256]{1,0:T(2,128)S(1)}, u32[]{:S(2)}, u32[]{:S(2)}) collective-permute-start(f32[2,256]{1,0:T(2,128)S(1)} %add_add_fusion.1), channel_id=1, source_target_pairs={{0,16},{8,24},{16,32},{24,40},{32,48},{40,56},{48,0},{56,8},{1,17}... | collective-permute-start | bytes 6152 | tf_op jit(solution)/shard_map/ppermute | solution.py:477
  104.3 0.0 collective-permute-done.9
  104.3 4.1 %collective-permute-done.8 = f32[2,256]{1,0:T(2,128)S(1)} collective-permute-done((f32[2,256]{1,0:T(2,128)S(1)}, f32[2,256]{1,0:T(2,128)S(1)}, u32[]{:S(2)}, u32[]{:S(2)}) %collective-permute-start.8) | collective-permute-done | bytes 2080 | tf_op jit(solution)/shard_map/ppermute | solution.py:477
  108.4 0.0 collective-permute-done.7
  108.4 0.5 collective-permute-start.10
  109.0 3.2 %collective-permute-done.10 = f32[2,256]{1,0:T(2,128)S(1)} collective-permute-done((f32[2,256]{1,0:T(2,128)S(1)}, f32[2,256]{1,0:T(2,128)S(1)}, u32[]{:S(2)}, u32[]{:S(2)}) %collective-permute-start.10) | collective-permute-done | bytes 2080 | tf_op jit(solution)/shard_map/ppermute | solution.py:477
  112.1 0.6 add.43.refs_1_.refs_13_
  112.7 9.7 %own_part.3 = (bf16[1024,256]{1,0:T(8,128)(2,1)}, f32[1024,256]{1,0:T(8,128)}, bf16[2048,256]{1,0:T(8,128)(2,1)}, bf16[2048,256]{1,0:T(8,128)(2,1)}, f32[8,2048]{1,0:T(8,128)}) custom-call(f32[1024,256]{1,0:T(8,128)} %get-tuple-element.36.refs_0_, f32[2,256]{1,0:T(2,128)} %add.43.refs_1_.refs_13_, bf16[2,256]{1,0:T(2,128)(2,1)} %gain_ref.1, ...), custom_call_target="tpu_custom_call" | custom-call | flops 3221225472 | bytes 4194304 | tf_op jit(solution)/shard_map/own_part/pallas_call | solution.py:377
  122.4 0.0 all-to-all-done.1
  122.4 0.0 copy-start
  122.4 1.0 copy-done
  123.4 18.2 %edge_part.3 = (f32[1024,256]{1,0:T(8,128)}, f32[2,256]{1,0:T(2,128)}) custom-call(bf16[2048,256]{1,0:T(8,128)(2,1)} %bitcast.7, bf16[2,256,256]{2,1,0:T(8,128)(2,1)} %refs_1_.5, bf16[2,256]{1,0:T(2,128)(2,1)} %refs_2_.7, bf16[2048,256]{1,0:T(8,128)(2,1)} %get-tuple-element.38.refs_3_, bf16[2048,256]{1,0:T(8,128)(2,1)} %get-tuple-element.39.refs_4_, ...), custom_call_target="tpu_custom_call" | custom-call | flops 5368709120 | bytes 4194304 | tf_op jit(solution)/shard_map/edge_part/pallas_call | solution.py:377
  141.5 0.7 broadcast_in_dim.4
  142.2 11.6 %all_to_all.20 = f32[8,2,256]{2,1,0:T(2,128)S(1)} all-to-all(f32[8,2,256]{2,1,0:T(2,128)S(1)} %broadcast_in_dim.4), channel_id=1, replica_groups=mesh['grp'=4,'blk_0'=8,'blk_1'=4,'blk_2'=2] {'blk_1','blk_2'}, dimensions={0} | all-to-all | bytes 32768 | tf_op jit(solution)/shard_map/all_to_all | solution.py:496
  153.8 14.8 %all_to_all.21 = f32[32,2,256]{2,1,0:T(2,128)S(1)} all-to-all(f32[32,2,256]{2,1,0:T(2,128)S(1)} %broadcast_in_dim.5), channel_id=1, replica_groups=mesh['grp'=4,'blk_0'=8,'blk_1'=4,'blk_2'=2] {'grp','blk_0'}, dimensions={0} | all-to-all | bytes 131072 | tf_op jit(solution)/shard_map/all_to_all | solution.py:496
  168.6 0.6 reduce_sum.19.stats_ref
  169.2 2.4 %norm_out.1 = bf16[1024,256]{1,0:T(8,128)(2,1)} custom-call(f32[1024,256]{1,0:T(8,128)} %get-tuple-element.43.summed_ref, f32[2,256]{1,0:T(2,128)} %reduce_sum.19.stats_ref, bf16[2,256]{1,0:T(2,128)(2,1)} %gain_ref.1, bf16[2,256]{1,0:T(2,128)(2,1)} %shift_ref.1), custom_call_target="tpu_custom_call" | custom-call | flops 1048576 | bytes 4194304 | tf_op jit(solution)/shard_map/norm_out/pallas_call | solution.py:377
  (6 shorter events, 0.1 us)
Async XLA Ops:
  5.6 46.8 %all-to-all-start = ((bf16[256,8,256]{2,1,0:T(8,128)(2,1)}), bf16[256,8,256]{2,1,0:T(8,128)(2,1)S(1)}, u32[]{:S(2)}, u32[]{:S(2)}) async-start(bf16[256,8,256]{2,1,0:T(8,128)(2,1)} %bitcast.10), calls=%async_computation | async-start | bytes 2097152 | tf_op jit(solution)/shard_map/all_to_all | solution.py:470
  52.3 1.0 copy-start.1
  74.6 5.9 %copy-start.2 = (f32[2,256]{1,0:T(2,128)S(1)}, f32[2,256]{1,0:T(2,128)}, u32[]{:S(2)}) copy-start(f32[2,256]{1,0:T(2,128)} %get-tuple-element.37) | copy-start | bytes 6148
  74.6 47.8 %all-to-all-start.1 = ((bf16[256,8,256]{2,1,0:T(8,128)(2,1)}), bf16[256,8,256]{2,1,0:T(8,128)(2,1)S(1)}, u32[]{:S(2)}, u32[]{:S(2)}) async-start(bf16[256,8,256]{2,1,0:T(8,128)(2,1)} %bitcast.8), calls=%async_computation.1 | async-start | bytes 2097152 | tf_op jit(solution)/shard_map/all_to_all | solution.py:470
  80.5 3.1 %collective-permute-start = (f32[2,256]{1,0:T(2,128)S(1)}, f32[2,256]{1,0:T(2,128)S(1)}, u32[]{:S(2)}, u32[]{:S(2)}) collective-permute-start(f32[2,256]{1,0:T(2,128)S(1)} %copy-done.2), channel_id=1, source_target_pairs={{0,1},{1,0},{2,3},{3,2},{4,5},{5,4},{6,7},{7,6},{8,9},{9,8},{10,11... | collective-permute-start | bytes 6152 | tf_op jit(solution)/shard_map/ppermute | solution.py:477
  83.6 2.7 %collective-permute-start.3 = (f32[2,256]{1,0:T(2,128)S(1)}, f32[2,256]{1,0:T(2,128)S(1)}, u32[]{:S(2)}, u32[]{:S(2)}) collective-permute-start(f32[2,256]{1,0:T(2,128)S(1)} %add.33), channel_id=1, source_target_pairs={{0,6},{2,0},{4,2},{6,4},{1,7},{3,1},{5,3},{7,5},{8,14},{10,8},{12,... | collective-permute-start | bytes 6152 | tf_op jit(solution)/shard_map/ppermute | solution.py:477
  84.4 4.2 %collective-permute-start.2 = (f32[2,256]{1,0:T(2,128)S(1)}, f32[2,256]{1,0:T(2,128)S(1)}, u32[]{:S(2)}, u32[]{:S(2)}) collective-permute-start(f32[2,256]{1,0:T(2,128)S(1)} %add.33), channel_id=1, source_target_pairs={{0,4},{2,6},{4,0},{6,2},{1,5},{3,7},{5,1},{7,3},{8,12},{10,14},{12... | collective-permute-start | bytes 6152 | tf_op jit(solution)/shard_map/ppermute | solution.py:477
  85.0 4.0 %collective-permute-start.1 = (f32[2,256]{1,0:T(2,128)S(1)}, f32[2,256]{1,0:T(2,128)S(1)}, u32[]{:S(2)}, u32[]{:S(2)}) collective-permute-start(f32[2,256]{1,0:T(2,128)S(1)} %add.33), channel_id=1, source_target_pairs={{0,2},{2,4},{4,6},{6,0},{1,3},{3,5},{5,7},{7,1},{8,10},{10,12},{12... | collective-permute-start | bytes 6152 | tf_op jit(solution)/shard_map/ppermute | solution.py:477
  89.0 3.7 %collective-permute-start.6 = (f32[2,256]{1,0:T(2,128)S(1)}, f32[2,256]{1,0:T(2,128)S(1)}, u32[]{:S(2)}, u32[]{:S(2)}) collective-permute-start(f32[2,256]{1,0:T(2,128)S(1)} %add_add_fusion.2), channel_id=1, source_target_pairs={{0,192},{64,0},{128,64},{192,128},{1,193},{65,1},{129,65},{193,129... | collective-permute-start | bytes 6152 | tf_op jit(solution)/shard_map/ppermute | solution.py:477
  91.6 4.2 %collective-permute-start.5 = (f32[2,256]{1,0:T(2,128)S(1)}, f32[2,256]{1,0:T(2,128)S(1)}, u32[]{:S(2)}, u32[]{:S(2)}) collective-permute-start(f32[2,256]{1,0:T(2,128)S(1)} %add_add_fusion.2), channel_id=1, source_target_pairs={{0,128},{64,192},{128,0},{192,64},{1,129},{65,193},{129,1},{193,65... | collective-permute-start | bytes 6152 | tf_op jit(solution)/shard_map/ppermute | solution.py:477
  92.1 3.9 %collective-permute-start.4 = (f32[2,256]{1,0:T(2,128)S(1)}, f32[2,256]{1,0:T(2,128)S(1)}, u32[]{:S(2)}, u32[]{:S(2)}) collective-permute-start(f32[2,256]{1,0:T(2,128)S(1)} %add_add_fusion.2), channel_id=1, source_target_pairs={{0,64},{64,128},{128,192},{192,0},{1,65},{65,129},{129,193},{193,1... | collective-permute-start | bytes 6152 | tf_op jit(solution)/shard_map/ppermute | solution.py:477
  96.0 8.3 %collective-permute-start.9 = (f32[2,256]{1,0:T(2,128)S(1)}, f32[2,256]{1,0:T(2,128)S(1)}, u32[]{:S(2)}, u32[]{:S(2)}) collective-permute-start(f32[2,256]{1,0:T(2,128)S(1)} %add_add_fusion.1), channel_id=1, source_target_pairs={{0,48},{8,56},{16,0},{24,8},{32,16},{40,24},{48,32},{56,40},{1,49}... | collective-permute-start | bytes 6152 | tf_op jit(solution)/shard_map/ppermute | solution.py:477
  100.7 7.7 %collective-permute-start.8 = (f32[2,256]{1,0:T(2,128)S(1)}, f32[2,256]{1,0:T(2,128)S(1)}, u32[]{:S(2)}, u32[]{:S(2)}) collective-permute-start(f32[2,256]{1,0:T(2,128)S(1)} %add_add_fusion.1), channel_id=1, source_target_pairs={{0,32},{8,40},{16,48},{24,56},{32,0},{40,8},{48,16},{56,24},{1,33}... | collective-permute-start | bytes 6152 | tf_op jit(solution)/shard_map/ppermute | solution.py:477
  102.1 6.3 %collective-permute-start.7 = (f32[2,256]{1,0:T(2,128)S(1)}, f32[2,256]{1,0:T(2,128)S(1)}, u32[]{:S(2)}, u32[]{:S(2)}) collective-permute-start(f32[2,256]{1,0:T(2,128)S(1)} %add_add_fusion.1), channel_id=1, source_target_pairs={{0,16},{8,24},{16,32},{24,40},{32,48},{40,56},{48,0},{56,8},{1,17}... | collective-permute-start | bytes 6152 | tf_op jit(solution)/shard_map/ppermute | solution.py:477
  108.4 3.7 %collective-permute-start.10 = (f32[2,256]{1,0:T(2,128)S(1)}, f32[2,256]{1,0:T(2,128)S(1)}, u32[]{:S(2)}, u32[]{:S(2)}) collective-permute-start(f32[2,256]{1,0:T(2,128)S(1)} %add_add_fusion), channel_id=1, source_target_pairs={{0,8},{8,16},{16,24},{24,32},{32,40},{40,48},{48,56},{56,0},{1,9},... | collective-permute-start | bytes 6152 | tf_op jit(solution)/shard_map/ppermute | solution.py:477
  122.4 1.0 copy-start

commit v2 on v1

--- a/solution.py
+++ b/solution.py
@@ -18,6 +18,8 @@
 CHUNK = 256
 EDGE_CHUNKS = EDGES_OWN // CHUNK
 NODE_CHUNKS = NODES_OWN // CHUNK
+WINDOW = 160
+TABLE_ROWS = NODES_OWN + ROWS_IN
 F32 = jnp.float32
 BF16 = jnp.bfloat16
 
@@ -105,7 +107,7 @@
 
 
 def sort_kernel(
-    src_ref, tgt_ref, valid_ref, bias_ref, rows_ref, cols_ref, bias_out, noedge_ref, bound_ref,
+    src_ref, tgt_ref, valid_ref, bias_ref, rows_ref, srcs_ref, bias_out, noedge_ref, bound_ref,
     key_ref, pos_ref, meta_ref,
 ):
     width = (1, EDGES_OWN)
@@ -147,8 +149,7 @@
     src_s = (placed[0:1] * 256.0 + placed[1:2]).astype(jnp.int32)
     tgt_s = (placed[2:3] * 256.0 + placed[3:4]).astype(jnp.int32)
     lane8 = iota((8, EDGES_OWN), 1)
-    both = jnp.where(sub == 0, src_s, tgt_s)
-    cols_ref[...] = jnp.transpose(both.astype(F32)).astype(jnp.int32)
+    srcs_ref[...] = src_s
     tgt8 = jnp.broadcast_to(tgt_s, (8, EDGES_OWN))
     before = pltpu.roll(tgt8, 1, 1)
     after = pltpu.roll(tgt8, EDGES_OWN - 1, 1)
@@ -179,23 +180,21 @@
         noedge_ref[k * CHUNK : (k + 1) * CHUNK, :] = jnp.broadcast_to(1.0 - found, (CHUNK, 8))
 
 
-def own_kernel(
-    layer, total_nodes, with_norm, *refs,
-):
+def own_kernel(layer, total_nodes, with_norm, *refs):
+    refs = list(refs)
+    state_ref = refs.pop(0)
     if with_norm:
-        (state_ref, stats_ref, gain_ref, shift_ref, wl_ref, wr_ref, ws_ref, attn_ref, cols_ref,
-         left_ref, base_ref, src_out, dst_out, self_out, right_ref) = refs
+        stats_ref, gain_ref, shift_ref = refs[:3]
+        refs = refs[3:]
         terms = norm_terms(
             stats_ref[...],
             total_nodes,
             gain_ref[layer - 1 : layer, :].astype(F32),
             shift_ref[layer - 1 : layer, :].astype(F32),
         )
-    else:
-        (state_ref, wl_ref, wr_ref, ws_ref, attn_ref, cols_ref,
-         left_ref, base_ref, src_out, dst_out, self_out, right_ref) = refs
+    wl_ref, wr_ref, ws_ref, attn_ref, rows_ref, bound_ref = refs[:6]
+    left_ref, base_ref, dst_out, self_out, table_ref, acc_ref = refs[6:]
     heads = head_rows(attn_ref, layer)
-    self_parts = []
     for k in range(NODE_CHUNKS):
         at = slice(k * CHUNK, (k + 1) * CHUNK)
         states = state_ref[at, :]
@@ -204,53 +203,69 @@
         left = dot(states, wl_ref[layer]).astype(BF16)
         right = dot(states, wr_ref[layer]).astype(BF16)
         left_ref[at, :] = left
-        right_ref[at, :] = right
+        table_ref[at, :FEAT] = right
         base_ref[at, :] = states.astype(F32) + dot(states, ws_ref[layer])
-        self_parts.append(scores_of(heads, leaky(left.astype(F32) + right.astype(F32))))
-    own = jnp.concatenate(self_parts, axis=1)
-    high, mid, low = split_three(own)
-    own32 = jnp.concatenate(
-        [high.astype(F32), mid.astype(F32), low.astype(F32), jnp.zeros_like(own)], axis=0
-    ).astype(BF16)
+        own = scores_of(heads, leaky(left.astype(F32) + right.astype(F32)))
+        high, mid, low = split_three(own)
+        parts = [high.astype(F32), mid.astype(F32), low.astype(F32)]
+        parts += [jnp.zeros((128 - 3 * HEADS, CHUNK), F32)]
+        table_ref[at, FEAT:] = jnp.transpose(jnp.concatenate(parts, axis=0)).astype(BF16)
+    table_ref[NODES_OWN:, :] = jnp.zeros((CHUNK, FEAT + 128), BF16)
 
     def step(c, carry):
         at = pl.ds(pl.multiple_of(c * CHUNK, CHUNK), CHUNK)
-        node_ids = iota((CHUNK, NODES_OWN), 1)
-        hot = one_hot(cols_ref[at, 1:2] == node_ids)
-        dst_out[at, :] = dot(hot, right_ref[...]).astype(BF16)
-        back = dot_t(own32, hot)
+        col = columns_of(rows_ref[0:1, at].astype(F32)).astype(jnp.int32)[:, 0:1]
+        low = lax.div(bound_ref[0, 2 * c], 16) * 16
+        extra = lax.div(jnp.maximum(bound_ref[0, 2 * c + 1] - low, 0), CHUNK)
+
+        def window(w):
+            base = pl.multiple_of(jnp.minimum(low + w * CHUNK, NODES_OWN), 16)
+            hot = one_hot(col - base == iota((CHUNK, CHUNK), 1))
+            return dot(hot, table_ref[pl.ds(base, CHUNK), :])
+
+        acc_ref[...] = window(0)
+
+        def more(w, carry):
+            acc_ref[...] += window(w)
+            return carry
+
+        lax.fori_loop(1, extra + 1, more, 0)
+        dst_out[at, :] = acc_ref[:, :FEAT].astype(BF16)
+        back = jnp.transpose(acc_ref[:, FEAT:])
         self_out[:, at] = back[0:8] + back[8:16] + back[16:24]
-        hot = one_hot(cols_ref[at, 0:1] == node_ids)
-        src_out[at, :] = dot(hot, left_ref[...]).astype(BF16)
         return carry
 
-    lax.fori_loop(0, EDGE_CHUNKS, step, 0)
-
-
-def scan_both(ref, bound, lane, start, end, join, neutral):
-    ref[0] = ref[2]
-    ref[1] = ref[2]
-    step = 1
-    while step < EDGES_OWN:
-
-        def advance(step=step):
-            ahead = ref[0]
-            back = ref[1]
-            moved = pltpu.roll(ahead, step, 1)
-            ref[0] = join(ahead, jnp.where(lane - step >= start, moved, neutral))
-            moved = pltpu.roll(back, EDGES_OWN - step, 1)
-            ref[1] = join(back, jnp.where(lane + step <= end, moved, neutral))
-
-        pl.when(bound > step)(advance)
-        step *= 2
+    lax.fori_loop(0, EDGE_CHUNKS, step, 0, unroll=2)
+
+
+def scan_both(ref, longest, lane, start, end, join, neutral, values):
+    def advance(ahead, back, step):
+        moved = pltpu.roll(ahead, step, 1)
+        ahead = join(ahead, jnp.where(lane - step >= start, moved, neutral))
+        moved = pltpu.roll(back, EDGES_OWN - step, 1)
+        return ahead, join(back, jnp.where(lane + step <= end, moved, neutral))
+
+    ahead, back = values, values
+    for step in (1, 2, 4, 8):
+        ahead, back = advance(ahead, back, step)
+    ref[0] = ahead
+    ref[1] = back
+
+    def rest():
+        step = 16
+        while step < EDGES_OWN:
+            ref[0], ref[1] = advance(ref[0], ref[1], step)
+            step *= 2
+
+    pl.when(longest > 16)(rest)
     return ref[0], ref[1]
 
 
 def edge_kernel(layer, total_nodes, with_norm, with_send, *refs):
     refs = list(refs)
-    recv_ref, wl_ref, attn_ref, src_in, dst_in, self_ref, rows_ref, cols_ref, bias_ref = refs[:9]
-    noedge_ref, bound_ref, left_ref, base_ref = refs[9:13]
-    refs = refs[13:]
+    recv_any, left_any, dst_any, noedge_any, base_any = refs[:5]
+    wl_ref, attn_ref, self_ref, rows_ref, srcs_ref, bias_ref, bound_ref = refs[5:12]
+    refs = refs[12:]
     if with_norm:
         stats_in, gain_ref, shift_ref = refs[:3]
         refs = refs[3:]
@@ -260,10 +275,25 @@
     refs = refs[2:]
     if with_send:
         send_ref = refs.pop(0)
-    table_ref, edge_ref, score_ref, scan_ref, mix_ref, acc_ref = refs[:6]
-    refs = refs[6:]
+    recv_ref, left_ref, dst_ref, noedge_ref, base_ref, sems = refs[:6]
+    table_ref, even_ref, odd_ref, edge_ref, score_ref, scan_ref, mix_ref, acc_ref = refs[6:14]
+    refs = refs[14:]
     if with_send:
         round_ref, col_ref = refs
+    copies = [
+        pltpu.make_async_copy(source, target, sems.at[i])
+        for i, (source, target) in enumerate(
+            (
+                (left_any, left_ref),
+                (recv_any, recv_ref),
+                (dst_any, dst_ref),
+                (noedge_any, noedge_ref),
+                (base_any, base_ref),
+            )
+        )
+    ]
+    for copy in copies:
+        copy.start()
     if with_norm:
         terms = norm_terms(
             stats_in[...],
@@ -272,26 +302,53 @@
             shift_ref[layer - 1 : layer, :].astype(F32),
         )
     heads = head_rows(attn_ref, layer)
+    half = FEAT // 2
+
+    def put_rows(first, values):
+        table_ref[pl.ds(2 * first, CHUNK, stride=2), :] = values[:, :half]
+        table_ref[pl.ds(2 * first + 1, CHUNK, stride=2), :] = values[:, half:]
+
+    copies[0].wait()
+    for k in range(NODE_CHUNKS):
+        put_rows(k * CHUNK, left_ref[k * CHUNK : (k + 1) * CHUNK, :].astype(F32))
+    copies[1].wait()
 
     def fill(c, carry):
         at = pl.ds(pl.multiple_of(c * CHUNK, CHUNK), CHUNK)
         states = recv_ref[at, :]
         if with_norm:
             states = normalize(states.astype(F32), terms)
-        table_ref[at, :] = dot(states, wl_ref[layer]).astype(BF16)
+        left = dot(states, wl_ref[layer]).astype(BF16).astype(F32)
+        put_rows(pl.multiple_of(NODES_OWN + c * CHUNK, CHUNK), left)
         return carry
 
-    lax.fori_loop(0, ROWS_IN // CHUNK, fill, 0)
-
-    def score(c, carry):
+    lax.fori_loop(0, ROWS_IN // CHUNK, fill, 0, unroll=2)
+
+    def fetch(c, out_ref):
+        first = c * CHUNK
+        for e in range(CHUNK):
+            row = srcs_ref[0, first + e]
+            out_ref[2 * e : 2 * e + 2, :] = table_ref[pl.ds(pl.multiple_of(2 * row, 2), 2), :]
+
+    def score(c, in_ref):
         at = pl.ds(pl.multiple_of(c * CHUNK, CHUNK), CHUNK)
-        hot = one_hot(cols_ref[at, 0:1] - NODES_OWN == iota((CHUNK, ROWS_IN), 1))
-        src = dot(hot, table_ref[...]) + src_in[at, :].astype(F32)
+        src = jnp.concatenate(
+            [in_ref[pl.ds(0, CHUNK, stride=2), :], in_ref[pl.ds(1, CHUNK, stride=2), :]], axis=1
+        )
         edge_ref[at, :] = src.astype(BF16)
-        score_ref[:, at] = scores_of(heads, leaky(src + dst_in[at, :].astype(F32)))
+        score_ref[:, at] = scores_of(heads, leaky(src + dst_ref[at, :].astype(F32)))
+
+    fetch(0, even_ref)
+    copies[2].wait()
+
+    def pair(c, carry):
+        fetch(2 * c + 1, odd_ref)
+        score(2 * c, even_ref)
+        fetch(lax.rem(2 * c + 2, EDGE_CHUNKS), even_ref)
+        score(2 * c + 1, odd_ref)
         return carry
 
-    lax.fori_loop(0, EDGE_CHUNKS, score, 0)
+    lax.fori_loop(0, EDGE_CHUNKS // 2, pair, 0)
 
     tgt = rows_ref[0:1, :]
     start = rows_ref[1:2, :]
@@ -301,16 +358,14 @@
     longest = bound_ref[0, 2 * EDGE_CHUNKS]
     scores = jnp.where(live, score_ref[...] + bias_ref[...], -1e30)
     own = self_ref[...]
-    scan_ref[2] = scores
-    ahead, back = scan_both(scan_ref, longest, lane, start, end, jnp.maximum, -1e30)
+    ahead, back = scan_both(scan_ref, longest, lane, start, end, jnp.maximum, -1e30, scores)
     top = jnp.maximum(jnp.maximum(ahead, back), own)
     weights = jnp.where(live, jnp.exp(scores - top), 0.0)
     own_weights = jnp.exp(own - top)
-    scan_ref[2] = weights
-    ahead, back = scan_both(scan_ref, longest, lane, start, end, jnp.add, 0.0)
+    ahead, back = scan_both(scan_ref, longest, lane, start, end, jnp.add, 0.0, weights)
     denom = own_weights + (ahead + (back - weights))
+    last = live & (lane == end)
     score_ref[...] = weights / denom
-    last = live & (lane == end)
     scan_ref[0] = jnp.where(last, own_weights / denom, 0.0)
     spread = head_spread()
 
@@ -322,28 +377,30 @@
         mix_ref[at, FEAT:] = wide[:, FEAT:].astype(BF16)
         return carry
 
-    lax.fori_loop(0, EDGE_CHUNKS, mix, 0)
+    lax.fori_loop(0, EDGE_CHUNKS, mix, 0, unroll=4)
+    acc_ref[...] = jnp.zeros_like(acc_ref)
+
+    def gather_in(c, carry):
+        here = pl.ds(pl.multiple_of(c * CHUNK, CHUNK), CHUNK)
+        low = lax.div(bound_ref[0, 2 * c], 8) * 8
+        count = lax.div(jnp.maximum(bound_ref[0, 2 * c + 1] - low + WINDOW, 0), WINDOW)
+
+        def window(w, carry):
+            first = pl.multiple_of(low + w * WINDOW, 8)
+            hot = one_hot(iota((WINDOW, CHUNK), 0) + first == rows_ref[0:1, here])
+            acc_ref[pl.ds(first, WINDOW), :] += dot(hot, mix_ref[here, :])
+            return carry
+
+        return lax.fori_loop(0, count, window, carry)
+
+    lax.fori_loop(0, EDGE_CHUNKS, gather_in, 0)
+    copies[3].wait()
+    copies[4].wait()
     stats_ref[...] = jnp.zeros_like(stats_ref)
     for k in range(NODE_CHUNKS):
         at = slice(k * CHUNK, (k + 1) * CHUNK)
-        acc_ref[...] = jnp.zeros_like(acc_ref)
-
-        def gather_in(c, carry, k=k):
-            near = (bound_ref[0, 2 * c] < (k + 1) * CHUNK) & (
-                bound_ref[0, 2 * c + 1] >= k * CHUNK
-            )
-
-            def add():
-                here = pl.ds(pl.multiple_of(c * CHUNK, CHUNK), CHUNK)
-                hot = one_hot(iota((CHUNK, CHUNK), 0) + k * CHUNK == rows_ref[0:1, here])
-                acc_ref[...] += dot(hot, mix_ref[here, :])
-
-            pl.when(near)(add)
-            return carry
-
-        lax.fori_loop(0, EDGE_CHUNKS, gather_in, 0)
-        own_alpha = jnp.where(noedge_ref[at, 0:1] > 0, 1.0, acc_ref[:, FEAT:])
-        message = acc_ref[:, :FEAT] + own_alpha * left_ref[at, :].astype(F32)
+        own_alpha = jnp.where(noedge_ref[at, 0:1] > 0, 1.0, acc_ref[at, FEAT:])
+        message = acc_ref[at, :FEAT] + own_alpha * left_ref[at, :].astype(F32)
         summed = base_ref[at, :] + message
         summed_ref[at, :] = summed
         stats_ref[0:1, :] += jnp.sum(summed, axis=0, keepdims=True)
@@ -370,6 +427,7 @@
 
 SMEM = pl.BlockSpec(memory_space=pltpu.SMEM)
 VMEM = pl.BlockSpec(memory_space=pltpu.VMEM)
+ANY = pl.BlockSpec(memory_space=pl.ANY)
 
 
 def call(body, name, outs, scratch, flops, args, in_specs=None, out_specs=None):
@@ -382,6 +440,7 @@
         out_specs=out_specs or [VMEM] * len(outs),
         scratch_shapes=scratch,
         cost_estimate=cost,
+        compiler_params=pltpu.CompilerParams(vmem_limit_bytes=24 << 20),
     )(*args)
 
 
@@ -405,7 +464,7 @@
         "sort_edges",
         [
             shaped(8, EDGES_OWN, jnp.int32),
-            shaped(EDGES_OWN, 8, jnp.int32),
+            shaped(1, EDGES_OWN, jnp.int32),
             shaped(8, EDGES_OWN, F32),
             shaped(NODES_OWN, 8, F32),
             shaped(1, 32, jnp.int32),
@@ -422,41 +481,51 @@
 
 
 def own_part(layer, total_nodes, args):
-    with_norm = layer > 0
+    in_specs = [VMEM] * len(args)
+    in_specs[-1] = SMEM
     return call(
-        functools.partial(own_kernel, layer, total_nodes, with_norm),
+        functools.partial(own_kernel, layer, total_nodes, layer > 0),
         "own_part",
         [
             shaped(NODES_OWN, FEAT, BF16),
             shaped(NODES_OWN, FEAT, F32),
             shaped(EDGES_OWN, FEAT, BF16),
-            shaped(EDGES_OWN, FEAT, BF16),
             shaped(8, EDGES_OWN, F32),
         ],
-        [pltpu.VMEM((NODES_OWN, FEAT), BF16)],
+        [pltpu.VMEM((NODES_OWN + CHUNK, FEAT + 128), BF16), pltpu.VMEM((CHUNK, FEAT + 128), F32)],
         3 * GIGA,
         args,
+        in_specs=in_specs,
     )
 
 
 def edge_part(layer, total_nodes, with_send, args):
-    with_norm = layer > 0
     outs = [shaped(NODES_OWN, FEAT, F32), shaped(2, FEAT, F32)]
+    half = FEAT // 2
     scratch = [
         pltpu.VMEM((ROWS_IN, FEAT), BF16),
+        pltpu.VMEM((NODES_OWN, FEAT), BF16),
+        pltpu.VMEM((EDGES_OWN, FEAT), BF16),
+        pltpu.VMEM((NODES_OWN, 8), F32),
+        pltpu.VMEM((NODES_OWN, FEAT), F32),
+        pltpu.SemaphoreType.DMA((5,)),
+        pltpu.VMEM((2 * TABLE_ROWS, half), F32),
+        pltpu.VMEM((2 * CHUNK, half), F32),
+        pltpu.VMEM((2 * CHUNK, half), F32),
         pltpu.VMEM((EDGES_OWN, FEAT), BF16),
         pltpu.VMEM((8, EDGES_OWN), F32),
-        pltpu.VMEM((3, 8, EDGES_OWN), F32),
+        pltpu.VMEM((2, 8, EDGES_OWN), F32),
         pltpu.VMEM((EDGES_OWN, 2 * FEAT), BF16),
-        pltpu.VMEM((CHUNK, 2 * FEAT), F32),
+        pltpu.VMEM((NODES_OWN + WINDOW, 2 * FEAT), F32),
     ]
     if with_send:
         outs.append(shaped(ROWS_IN, FEAT, BF16))
         scratch += [pltpu.VMEM((NODES_OWN, FEAT), BF16), pltpu.VMEM((ROWS_IN, 8), jnp.int32)]
-    in_specs = [VMEM] * len(args)
-    in_specs[10] = SMEM
+    in_specs = [ANY] * 5 + [VMEM] * (len(args) - 5)
+    in_specs[9] = SMEM
+    in_specs[11] = SMEM
     return call(
-        functools.partial(edge_kernel, layer, total_nodes, with_norm, with_send),
+        functools.partial(edge_kernel, layer, total_nodes, layer > 0, with_send),
         "edge_part",
         outs,
         scratch,
@@ -516,27 +585,27 @@
     row = (1, EDGES_OWN)
     sent = send_rows(send_list, features)
     received = deliver(sent)
-    rows, cols, bias, noedge, bound = sort_edges(
+    rows, srcs, bias, noedge, bound = sort_edges(
         source_index.reshape(row), target_index.reshape(row), edge_valid.reshape(row), edge_bias
     )
-    weights = [w_left, w_right, w_skip, attn_vec, cols]
-    left, base, src, dst, own = own_part(0, total_nodes, [features] + weights)
-    tail = [rows, cols, bias, noedge, bound]
+    weights = [w_left, w_right, w_skip, attn_vec, rows, bound]
+    left, base, dst, own = own_part(0, total_nodes, [features] + weights)
+    edges = [rows, srcs, bias, bound]
     summed, stats, sent = edge_part(
         0,
         total_nodes,
         True,
-        [received, w_left, attn_vec, src, dst, own] + tail + [left, base, send_list],
+        [received, left, dst, noedge, base, w_left, attn_vec, own] + edges + [send_list],
     )
     received = deliver(sent)
     stats = total_inside(stats)
     norms = [stats, norm_gain, norm_shift]
-    left, base, src, dst, own = own_part(1, total_nodes, [summed] + norms + weights)
+    left, base, dst, own = own_part(1, total_nodes, [summed] + norms + weights)
     summed, stats = edge_part(
         1,
         total_nodes,
         False,
-        [received, w_left, attn_vec, src, dst, own] + tail + [left, base] + norms,
+        [received, left, dst, noedge, base, w_left, attn_vec, own] + edges + norms,
     )
     stats = total_alone(stats)
     return call(

time: 172 us -> 166 us (0.965)
  Pallas kernels: 76.2 us -> 49.7 us
  local copies, waits for them, and re-layouts: 2.65 us -> 22.2 us
    pallas_call x7, Pallas kernels: 76.2 us -> 49.7 us  [call(): pl.pallas_call(body, name=name, out_shape=outs, in_specs=in_specs or [VME...]
    unnamed x6 -> x78, local copies, waits for them, and re-layouts: 1.96 us -> 22.1 us
  transfers between devices with their start and end apart: 13 -> 13, of which waited for: 9 -> 9; matrix products, arithmetic and copies ran while one was open for 0% -> 0% of each run, Pallas kernels for 17% -> 12%
where the time goes in v2:
time: 166 us; the launch traced here: 165 us
  Pallas kernels  49.7 us (30%)
  starting transfers between devices  38.5 us (23%)
  waiting for transfers between devices  27.5 us (17%)
  blocking collectives  26.7 us (16%)
  local copies, waits for them, and re-layouts  22.2 us (13%)
    pallas_call x7, Pallas kernels, call(): pl.pallas_call(body, name=name, out_shape=outs, in_specs=in_specs or [VME...  49.7 us
    all_to_all x2, blocking collectives, total_alone(): stats = jnp.sum(lax.all_to_all(copies, axes, 0, 0, tiled=True), axis=0)  26.7 us
    unnamed x78, local copies, waits for them, and re-layouts  22.1 us
    all_to_all x2, starting transfers between devices, deliver(): lax.all_to_all(rows.reshape(-1, 8, rows.shape[1]), GRP_BLK, split_axis=0,...  21.7 us
    ppermute x11, starting transfers between devices, shifted(): lax.ppermute(value, axis, [(i, (i + amount) % size) for i in range(size)])  16.8 us
    ppermute x11, waiting for transfers between devices, shifted(): lax.ppermute(value, axis, [(i, (i + amount) % size) for i in range(size)])  14.8 us
    all_to_all x2, waiting for transfers between devices, deliver(): lax.all_to_all(rows.reshape(-1, 8, rows.shape[1]), GRP_BLK, split_axis=0,...  12.6 us
  transfers between devices with their start and end apart: 13, of which 9 were waited for; matrix products, arithmetic and copies ran while one was open for 0% of the time, Pallas kernels for 12%

profile of v2, /device:TPU:1, one launch (start us, length us, event | category | flops | bytes accessed | tf_op | source)
XLA Modules:
  0.0 164.8 jit_solution(17837863647716104368)
XLA Ops:
  0.0 1.0 copy-done.2
  1.0 0.7 copy-done.11
  1.7 4.5 %send_rows.1 = bf16[2048,256]{1,0:T(8,128)(2,1)} custom-call(s32[1,2048]{1,0:T(1,128)S(1)} %copy-done.11, bf16[1024,256]{1,0:T(8,128)(2,1)S(1)} %copy-done.2), custom_call_target="tpu_custom_call" | custom-call | flops 1073741824 | bytes 4194304 | tf_op jit(solution)/shard_map/send_rows/pallas_call | solution.py:435
  6.3 15.7 %all-to-all-start = ((bf16[256,8,256]{2,1,0:T(8,128)(2,1)}), bf16[256,8,256]{2,1,0:T(8,128)(2,1)S(1)}, u32[]{:S(2)}, u32[]{:S(2)}) async-start(bf16[256,8,256]{2,1,0:T(8,128)(2,1)} %bitcast), calls=%async_computation | async-start | bytes 2097152 | tf_op jit(solution)/shard_map/all_to_all | solution.py:539
  22.0 8.3 %sort_edges.1 = (s32[8,2048]{1,0:T(8,128)S(1)}, s32[1,2048]{1,0:T(1,128)S(1)}, f32[8,2048]{1,0:T(8,128)S(1)}, f32[1024,8]{1,0:T(8,128)S(1)}, s32[1,32]{1,0:T(1,128)S(1)}) custom-call(s32[1,2048]{1,0:T(1,128)S(1)} %bitcast.9, s32[1,2048]{1,0:T(1,128)S(1)} %bitcast.10, s32[1,2048]{1,0:T(1,128)S(1)} %bitcast.11, f32[8,2048]{1,0:T(8,128)S(1)} %copy-done.7), custom_call_target="tpu_custom_call" | custom-call | flops 2147483648 | bytes 4194304 | tf_op jit(solution)/shard_map/sort_edges/pallas_call | solution.py:435
  31.6 5.5 %own_part.2 = (bf16[1024,256]{1,0:T(8,128)(2,1)S(1)}, f32[1024,256]{1,0:T(8,128)S(1)}, bf16[2048,256]{1,0:T(8,128)(2,1)S(1)}, f32[8,2048]{1,0:T(8,128)S(1)}) custom-call(bf16[1024,256]{1,0:T(8,128)(2,1)S(1)} %copy-done.3, bf16[2,256,256]{2,1,0:T(8,128)(2,1)S(1)} %copy-done.6, bf16[2,256,256]{2,1,0:T(8,128)(2,1)S(1)} %copy-done.4, ...), custom_call_target="tpu_custom_call" | custom-call | flops 3221225472 | bytes 4194304 | tf_op jit(solution)/shard_map/own_part/pallas_call | solution.py:435
  37.1 1.0 copy-done.20
  38.0 1.0 copy-done.22
  39.0 0.8 copy-done.26
  39.8 0.6 copy-done.30
  40.4 12.6 %all-to-all-done = bf16[256,8,256]{2,1,0:T(8,128)(2,1)S(1)} async-done(((bf16[256,8,256]{2,1,0:T(8,128)(2,1)}), bf16[256,8,256]{2,1,0:T(8,128)(2,1)S(1)}, u32[]{:S(2)}, u32[]{:S(2)}) %all-to-all-start) | async-done | bytes 1048608 | tf_op jit(solution)/shard_map/all_to_all | solution.py:539
  53.1 0.7 copy-done.36
  53.7 1.2 copy-done.21
  54.9 1.2 copy-done.23
  56.2 1.0 copy-done.27
  57.2 0.8 copy-done.31
  58.0 0.7 copy-done.33
  58.7 14.4 %edge_part.2 = (f32[1024,256]{1,0:T(8,128)S(1)}, f32[2,256]{1,0:T(2,128)S(1)}, bf16[2048,256]{1,0:T(8,128)(2,1)}) custom-call(bf16[2048,256]{1,0:T(8,128)(2,1)S(1)} %bitcast.8, bf16[1024,256]{1,0:T(8,128)(2,1)S(1)} %copy-done.27, bf16[2048,256]{1,0:T(8,128)(2,1)S(1)} %copy-done.23, f32[1024,8]{1,0:T(8,128)S(1)} %get-tuple-element.27.refs_3_, ...), custom_call_target="tpu_custom_call" | custom-call | flops 5368709120 | bytes 4194304 | tf_op jit(solution)/shard_map/edge_part/pallas_call | solution.py:435
  73.2 1.0 copy-done.14
  74.1 6.1 %all-to-all-start.1 = ((bf16[256,8,256]{2,1,0:T(8,128)(2,1)}), bf16[256,8,256]{2,1,0:T(8,128)(2,1)S(1)}, u32[]{:S(2)}, u32[]{:S(2)}) async-start(bf16[256,8,256]{2,1,0:T(8,128)(2,1)} %bitcast.5), calls=%async_computation.1 | async-start | bytes 2097152 | tf_op jit(solution)/shard_map/all_to_all | solution.py:539
  80.2 2.2 %collective-permute-start = (f32[2,256]{1,0:T(2,128)S(1)}, f32[2,256]{1,0:T(2,128)S(1)}, u32[]{:S(2)}, u32[]{:S(2)}) collective-permute-start(f32[2,256]{1,0:T(2,128)S(1)} %get-tuple-element.34), channel_id=1, source_target_pairs={{0,1},{1,0},{2,3},{3,2},{4,5},{5,4},{6,7},{7,6},{8,9},{9,8},{10,11... | collective-permute-start | bytes 6152 | tf_op jit(solution)/shard_map/ppermute | solution.py:546
  82.4 0.8 collective-permute-done
  83.3 0.8 collective-permute-start.3
  85.2 0.8 collective-permute-done.3
  86.0 2.3 %collective-permute-done.2 = f32[2,256]{1,0:T(2,128)S(1)} collective-permute-done((f32[2,256]{1,0:T(2,128)S(1)}, f32[2,256]{1,0:T(2,128)S(1)}, u32[]{:S(2)}, u32[]{:S(2)}) %collective-permute-start.2) | collective-permute-done | bytes 2080 | tf_op jit(solution)/shard_map/ppermute | solution.py:546
  88.7 2.6 %collective-permute-start.6 = (f32[2,256]{1,0:T(2,128)S(1)}, f32[2,256]{1,0:T(2,128)S(1)}, u32[]{:S(2)}, u32[]{:S(2)}) collective-permute-start(f32[2,256]{1,0:T(2,128)S(1)} %add_add_fusion.2), channel_id=1, source_target_pairs={{0,192},{64,0},{128,64},{192,128},{1,193},{65,1},{129,65},{193,129... | collective-permute-start | bytes 6152 | tf_op jit(solution)/shard_map/ppermute | solution.py:546
  91.8 0.7 collective-permute-start.4
  92.4 3.1 %collective-permute-done.5 = f32[2,256]{1,0:T(2,128)S(1)} collective-permute-done((f32[2,256]{1,0:T(2,128)S(1)}, f32[2,256]{1,0:T(2,128)S(1)}, u32[]{:S(2)}, u32[]{:S(2)}) %collective-permute-start.5) | collective-permute-done | bytes 2080 | tf_op jit(solution)/shard_map/ppermute | solution.py:546
  95.7 4.7 %collective-permute-start.9 = (f32[2,256]{1,0:T(2,128)S(1)}, f32[2,256]{1,0:T(2,128)S(1)}, u32[]{:S(2)}, u32[]{:S(2)}) collective-permute-start(f32[2,256]{1,0:T(2,128)S(1)} %add_add_fusion.1), channel_id=1, source_target_pairs={{0,48},{8,56},{16,0},{24,8},{32,16},{40,24},{48,32},{56,40},{1,49}... | collective-permute-start | bytes 6152 | tf_op jit(solution)/shard_map/ppermute | solution.py:546
  100.4 1.3 collective-permute-start.8
  101.8 2.3 %collective-permute-start.7 = (f32[2,256]{1,0:T(2,128)S(1)}, f32[2,256]{1,0:T(2,128)S(1)}, u32[]{:S(2)}, u32[]{:S(2)}) collective-permute-start(f32[2,256]{1,0:T(2,128)S(1)} %add_add_fusion.1), channel_id=1, source_target_pairs={{0,16},{8,24},{16,32},{24,40},{32,48},{40,56},{48,0},{56,8},{1,17}... | collective-permute-start | bytes 6152 | tf_op jit(solution)/shard_map/ppermute | solution.py:546
  104.1 4.1 %collective-permute-done.8 = f32[2,256]{1,0:T(2,128)S(1)} collective-permute-done((f32[2,256]{1,0:T(2,128)S(1)}, f32[2,256]{1,0:T(2,128)S(1)}, u32[]{:S(2)}, u32[]{:S(2)}) %collective-permute-start.8) | collective-permute-done | bytes 2080 | tf_op jit(solution)/shard_map/ppermute | solution.py:546
  108.7 3.2 %collective-permute-done.10 = f32[2,256]{1,0:T(2,128)S(1)} collective-permute-done((f32[2,256]{1,0:T(2,128)S(1)}, f32[2,256]{1,0:T(2,128)S(1)}, u32[]{:S(2)}, u32[]{:S(2)}) %collective-permute-start.10) | collective-permute-done | bytes 2080 | tf_op jit(solution)/shard_map/ppermute | solution.py:546
  111.9 0.7 copy-done
  112.5 5.5 %own_part.3 = (bf16[1024,256]{1,0:T(8,128)(2,1)S(1)}, f32[1024,256]{1,0:T(8,128)S(1)}, bf16[2048,256]{1,0:T(8,128)(2,1)S(1)}, f32[8,2048]{1,0:T(8,128)S(1)}) custom-call(f32[1024,256]{1,0:T(8,128)S(1)} %copy-done.15, f32[2,256]{1,0:T(2,128)S(1)} %add.43.refs_1_.refs_12_, bf16[2,256]{1,0:T(2,128)(2,1)S(1)} %copy-done, bf16[2,256]{1,0:T(2,128)(2,1)S(1)} %copy-done.1, ...), custom_call_target="tpu_custom_call" | custom-call | flops 3221225472 | bytes 4194304 | tf_op jit(solution)/shard_map/own_part/pallas_call | solution.py:435
  118.1 1.0 copy-done.16
  119.0 1.0 copy-done.18
  120.0 0.8 copy-done.24
  120.8 0.6 copy-done.28
  121.4 0.7 copy-done.34
  122.1 1.2 copy-done.17
  123.4 1.2 copy-done.19
  124.6 1.0 copy-done.25
  125.6 0.8 copy-done.29
  126.5 10.3 %edge_part.3 = (f32[1024,256]{1,0:T(8,128)S(1)}, f32[2,256]{1,0:T(2,128)S(1)}) custom-call(bf16[2048,256]{1,0:T(8,128)(2,1)S(1)} %bitcast.7, bf16[1024,256]{1,0:T(8,128)(2,1)S(1)} %copy-done.25, bf16[2048,256]{1,0:T(8,128)(2,1)S(1)} %copy-done.19, f32[1024,8]{1,0:T(8,128)S(1)} %get-tuple-element.27.refs_3_, f32[1024,256]{1,0:T(8,128)S(1)} %copy-done.17, ...), custom_call_target="tpu_custom_call" | custom-call | flops 5368709120 | bytes 4194304 | tf_op jit(solution)/shard_map/edge_part/pallas_call | solution.py:435
  136.8 11.5 %all_to_all.20 = f32[8,2,256]{2,1,0:T(2,128)S(1)} all-to-all(f32[8,2,256]{2,1,0:T(2,128)S(1)} %broadcast_in_dim.4), channel_id=1, replica_groups=mesh['grp'=4,'blk_0'=8,'blk_1'=4,'blk_2'=2] {'blk_1','blk_2'}, dimensions={0} | all-to-all | bytes 32768 | tf_op jit(solution)/shard_map/all_to_all | solution.py:565
  148.4 15.2 %all_to_all.21 = f32[32,2,256]{2,1,0:T(2,128)S(1)} all-to-all(f32[32,2,256]{2,1,0:T(2,128)S(1)} %broadcast_in_dim.5), channel_id=1, replica_groups=mesh['grp'=4,'blk_0'=8,'blk_1'=4,'blk_2'=2] {'grp','blk_0'}, dimensions={0} | all-to-all | bytes 131072 | tf_op jit(solution)/shard_map/all_to_all | solution.py:565
  163.6 1.2 norm_out.1
  (74 shorter events, 4.1 us)
Async XLA Ops:
  0.0 1.0 copy-start.2
  1.0 0.7 copy-start.11
  6.3 15.7 %copy-start.7 = (f32[8,2048]{1,0:T(8,128)S(1)}, f32[8,2048]{1,0:T(8,128)}, u32[]{:S(2)}) copy-start(f32[8,2048]{1,0:T(8,128)} %bias_ref.1) | copy-start | bytes 196612
  6.3 15.7 %copy-start.8 = (s32[16,128]{1,0:T(8,128)S(1)}, s32[16,128]{1,0:T(8,128)}, u32[]{:S(2)}) copy-start(s32[16,128]{1,0:T(8,128)} %param.13) | copy-start | bytes 24580
  6.3 15.7 %copy-start.9 = (s32[16,128]{1,0:T(8,128)S(1)}, s32[16,128]{1,0:T(8,128)}, u32[]{:S(2)}) copy-start(s32[16,128]{1,0:T(8,128)} %param.14) | copy-start | bytes 24580
  6.3 15.7 %copy-start.10 = (s32[16,128]{1,0:T(8,128)S(1)}, s32[16,128]{1,0:T(8,128)}, u32[]{:S(2)}) copy-start(s32[16,128]{1,0:T(8,128)} %param.15) | copy-start | bytes 24580
  6.3 46.8 %all-to-all-start = ((bf16[256,8,256]{2,1,0:T(8,128)(2,1)}), bf16[256,8,256]{2,1,0:T(8,128)(2,1)S(1)}, u32[]{:S(2)}, u32[]{:S(2)}) async-start(bf16[256,8,256]{2,1,0:T(8,128)(2,1)} %bitcast), calls=%async_computation | async-start | bytes 2097152 | tf_op jit(solution)/shard_map/all_to_all | solution.py:539
  22.0 9.5 %copy-start.3 = (bf16[1024,256]{1,0:T(8,128)(2,1)S(1)}, bf16[1024,256]{1,0:T(8,128)(2,1)}, u32[]{:S(2)}) copy-start(bf16[1024,256]{1,0:T(8,128)(2,1)} %refs_0_.1) | copy-start | bytes 1572868
  22.0 9.5 %copy-start.4 = (bf16[2,256,256]{2,1,0:T(8,128)(2,1)S(1)}, bf16[2,256,256]{2,1,0:T(8,128)(2,1)}, u32[]{:S(2)}) copy-start(bf16[2,256,256]{2,1,0:T(8,128)(2,1)} %refs_5_.4) | copy-start | bytes 786436
  22.0 9.5 %copy-start.5 = (bf16[2,256,256]{2,1,0:T(8,128)(2,1)S(1)}, bf16[2,256,256]{2,1,0:T(8,128)(2,1)}, u32[]{:S(2)}) copy-start(bf16[2,256,256]{2,1,0:T(8,128)(2,1)} %refs_6_.4) | copy-start | bytes 786436
  22.0 9.5 %copy-start.6 = (bf16[2,256,256]{2,1,0:T(8,128)(2,1)S(1)}, bf16[2,256,256]{2,1,0:T(8,128)(2,1)}, u32[]{:S(2)}) copy-start(bf16[2,256,256]{2,1,0:T(8,128)(2,1)} %refs_5_.5) | copy-start | bytes 786436
  30.9 0.7 copy-start.13
  37.0 1.0 copy-start.20
  38.0 1.0 copy-start.22
  39.0 0.8 copy-start.26
  40.4 12.6 %copy-start.12 = (s32[1,2048]{1,0:T(1,128)S(1)}, s32[1,2048]{1,0:T(1,128)}, u32[]{:S(2)}) copy-start(s32[1,2048]{1,0:T(1,128)} %refs_12_.1) | copy-start | bytes 24580
  53.0 0.7 copy-start.36
  53.7 1.2 copy-start.21
  54.9 1.2 copy-start.23
  56.2 1.0 copy-start.27
  57.2 0.8 copy-start.31
  58.0 0.7 copy-start.33
  73.2 1.0 copy-start.14
  74.1 37.7 %copy-start.1 = (bf16[2,256]{1,0:T(2,128)(2,1)S(1)}, bf16[2,256]{1,0:T(2,128)(2,1)}, u32[]{:S(2)}) copy-start(bf16[2,256]{1,0:T(2,128)(2,1)} %shift_ref.1) | copy-start | bytes 3076
  74.1 37.7 %copy-start.15 = (f32[1024,256]{1,0:T(8,128)S(1)}, f32[1024,256]{1,0:T(8,128)}, u32[]{:S(2)}) copy-start(f32[1024,256]{1,0:T(8,128)} %copy-done.14) | copy-start | bytes 3145732
  74.1 47.3 %all-to-all-start.1 = ((bf16[256,8,256]{2,1,0:T(8,128)(2,1)}), bf16[256,8,256]{2,1,0:T(8,128)(2,1)S(1)}, u32[]{:S(2)}, u32[]{:S(2)}) async-start(bf16[256,8,256]{2,1,0:T(8,128)(2,1)} %bitcast.5), calls=%async_computation.1 | async-start | bytes 2097152 | tf_op jit(solution)/shard_map/all_to_all | solution.py:539
  80.2 3.1 %collective-permute-start = (f32[2,256]{1,0:T(2,128)S(1)}, f32[2,256]{1,0:T(2,128)S(1)}, u32[]{:S(2)}, u32[]{:S(2)}) collective-permute-start(f32[2,256]{1,0:T(2,128)S(1)} %get-tuple-element.34), channel_id=1, source_target_pairs={{0,1},{1,0},{2,3},{3,2},{4,5},{5,4},{6,7},{7,6},{8,9},{9,8},{10,11... | collective-permute-start | bytes 6152 | tf_op jit(solution)/shard_map/ppermute | solution.py:546
  83.3 2.7 %collective-permute-start.3 = (f32[2,256]{1,0:T(2,128)S(1)}, f32[2,256]{1,0:T(2,128)S(1)}, u32[]{:S(2)}, u32[]{:S(2)}) collective-permute-start(f32[2,256]{1,0:T(2,128)S(1)} %add.33), channel_id=1, source_target_pairs={{0,6},{2,0},{4,2},{6,4},{1,7},{3,1},{5,3},{7,5},{8,14},{10,8},{12,... | collective-permute-start | bytes 6152 | tf_op jit(solution)/shard_map/ppermute | solution.py:546
  84.1 4.2 %collective-permute-start.2 = (f32[2,256]{1,0:T(2,128)S(1)}, f32[2,256]{1,0:T(2,128)S(1)}, u32[]{:S(2)}, u32[]{:S(2)}) collective-permute-start(f32[2,256]{1,0:T(2,128)S(1)} %add.33), channel_id=1, source_target_pairs={{0,4},{2,6},{4,0},{6,2},{1,5},{3,7},{5,1},{7,3},{8,12},{10,14},{12... | collective-permute-start | bytes 6152 | tf_op jit(solution)/shard_map/ppermute | solution.py:546
  84.7 4.1 %collective-permute-start.1 = (f32[2,256]{1,0:T(2,128)S(1)}, f32[2,256]{1,0:T(2,128)S(1)}, u32[]{:S(2)}, u32[]{:S(2)}) collective-permute-start(f32[2,256]{1,0:T(2,128)S(1)} %add.33), channel_id=1, source_target_pairs={{0,2},{2,4},{4,6},{6,0},{1,3},{3,5},{5,7},{7,1},{8,10},{10,12},{12... | collective-permute-start | bytes 6152 | tf_op jit(solution)/shard_map/ppermute | solution.py:546
  88.7 3.7 %collective-permute-start.6 = (f32[2,256]{1,0:T(2,128)S(1)}, f32[2,256]{1,0:T(2,128)S(1)}, u32[]{:S(2)}, u32[]{:S(2)}) collective-permute-start(f32[2,256]{1,0:T(2,128)S(1)} %add_add_fusion.2), channel_id=1, source_target_pairs={{0,192},{64,0},{128,64},{192,128},{1,193},{65,1},{129,65},{193,129... | collective-permute-start | bytes 6152 | tf_op jit(solution)/shard_map/ppermute | solution.py:546
  91.3 4.2 %collective-permute-start.5 = (f32[2,256]{1,0:T(2,128)S(1)}, f32[2,256]{1,0:T(2,128)S(1)}, u32[]{:S(2)}, u32[]{:S(2)}) collective-permute-start(f32[2,256]{1,0:T(2,128)S(1)} %add_add_fusion.2), channel_id=1, source_target_pairs={{0,128},{64,192},{128,0},{192,64},{1,129},{65,193},{129,1},{193,65... | collective-permute-start | bytes 6152 | tf_op jit(solution)/shard_map/ppermute | solution.py:546
  91.8 3.9 %collective-permute-start.4 = (f32[2,256]{1,0:T(2,128)S(1)}, f32[2,256]{1,0:T(2,128)S(1)}, u32[]{:S(2)}, u32[]{:S(2)}) collective-permute-start(f32[2,256]{1,0:T(2,128)S(1)} %add_add_fusion.2), channel_id=1, source_target_pairs={{0,64},{64,128},{128,192},{192,0},{1,65},{65,129},{129,193},{193,1... | collective-permute-start | bytes 6152 | tf_op jit(solution)/shard_map/ppermute | solution.py:546
  95.7 8.3 %collective-permute-start.9 = (f32[2,256]{1,0:T(2,128)S(1)}, f32[2,256]{1,0:T(2,128)S(1)}, u32[]{:S(2)}, u32[]{:S(2)}) collective-permute-start(f32[2,256]{1,0:T(2,128)S(1)} %add_add_fusion.1), channel_id=1, source_target_pairs={{0,48},{8,56},{16,0},{24,8},{32,16},{40,24},{48,32},{56,40},{1,49}... | collective-permute-start | bytes 6152 | tf_op jit(solution)/shard_map/ppermute | solution.py:546
  100.4 7.7 %collective-permute-start.8 = (f32[2,256]{1,0:T(2,128)S(1)}, f32[2,256]{1,0:T(2,128)S(1)}, u32[]{:S(2)}, u32[]{:S(2)}) collective-permute-start(f32[2,256]{1,0:T(2,128)S(1)} %add_add_fusion.1), channel_id=1, source_target_pairs={{0,32},{8,40},{16,48},{24,56},{32,0},{40,8},{48,16},{56,24},{1,33}... | collective-permute-start | bytes 6152 | tf_op jit(solution)/shard_map/ppermute | solution.py:546
  101.8 6.3 %collective-permute-start.7 = (f32[2,256]{1,0:T(2,128)S(1)}, f32[2,256]{1,0:T(2,128)S(1)}, u32[]{:S(2)}, u32[]{:S(2)}) collective-permute-start(f32[2,256]{1,0:T(2,128)S(1)} %add_add_fusion.1), channel_id=1, source_target_pairs={{0,16},{8,24},{16,32},{24,40},{32,48},{40,56},{48,0},{56,8},{1,17}... | collective-permute-start | bytes 6152 | tf_op jit(solution)/shard_map/ppermute | solution.py:546
  108.1 3.7 %collective-permute-start.10 = (f32[2,256]{1,0:T(2,128)S(1)}, f32[2,256]{1,0:T(2,128)S(1)}, u32[]{:S(2)}, u32[]{:S(2)}) collective-permute-start(f32[2,256]{1,0:T(2,128)S(1)} %add_add_fusion), channel_id=1, source_target_pairs={{0,8},{8,16},{16,24},{24,32},{32,40},{40,48},{48,56},{56,0},{1,9},... | collective-permute-start | bytes 6152 | tf_op jit(solution)/shard_map/ppermute | solution.py:546
  111.9 0.7 copy-start
  111.9 0.7 copy-start.37
  118.1 1.0 copy-start.16
  119.0 1.0 copy-start.18
  120.0 0.8 copy-start.24
  121.4 0.7 copy-start.34
  121.4 0.7 copy-start.38
  122.1 1.2 copy-start.17
  123.4 1.2 copy-start.19
  124.6 1.0 copy-start.25
  125.6 0.8 copy-start.29
  (4 other events, 2.4 us)

commit v3 on v2

--- a/solution.py
+++ b/solution.py
@@ -193,11 +193,23 @@
             shift_ref[layer - 1 : layer, :].astype(F32),
         )
     wl_ref, wr_ref, ws_ref, attn_ref, rows_ref, bound_ref = refs[:6]
-    left_ref, base_ref, dst_out, self_out, table_ref, acc_ref = refs[6:]
+    left_out, base_out, dst_hbm, self_out = refs[6:10]
+    table_ref, acc_ref, own_ref, left_ref, base_ref, dst_out, sems = refs[10:]
+    loads = []
+    for k in range(NODE_CHUNKS):
+        at = slice(k * CHUNK, (k + 1) * CHUNK)
+        loads.append(pltpu.make_async_copy(state_ref.at[at], own_ref.at[at], sems.at[k]))
+        loads[-1].start()
+    stores = [
+        pltpu.make_async_copy(left_ref, left_out, sems.at[NODE_CHUNKS]),
+        pltpu.make_async_copy(base_ref, base_out, sems.at[NODE_CHUNKS + 1]),
+        pltpu.make_async_copy(dst_out, dst_hbm, sems.at[NODE_CHUNKS + 2]),
+    ]
     heads = head_rows(attn_ref, layer)
     for k in range(NODE_CHUNKS):
         at = slice(k * CHUNK, (k + 1) * CHUNK)
-        states = state_ref[at, :]
+        loads[k].wait()
+        states = own_ref[at, :]
         if with_norm:
             states = normalize(states, terms)
         left = dot(states, wl_ref[layer]).astype(BF16)
@@ -211,6 +223,8 @@
         parts += [jnp.zeros((128 - 3 * HEADS, CHUNK), F32)]
         table_ref[at, FEAT:] = jnp.transpose(jnp.concatenate(parts, axis=0)).astype(BF16)
     table_ref[NODES_OWN:, :] = jnp.zeros((CHUNK, FEAT + 128), BF16)
+    stores[0].start()
+    stores[1].start()
 
     def step(c, carry):
         at = pl.ds(pl.multiple_of(c * CHUNK, CHUNK), CHUNK)
@@ -236,6 +250,9 @@
         return carry
 
     lax.fori_loop(0, EDGE_CHUNKS, step, 0, unroll=2)
+    stores[2].start()
+    for store in stores:
+        store.wait()
 
 
 def scan_both(ref, longest, lane, start, end, join, neutral, values):
@@ -270,16 +287,14 @@
         stats_in, gain_ref, shift_ref = refs[:3]
         refs = refs[3:]
     if with_send:
-        list_ref = refs.pop(0)
-    summed_ref, stats_ref = refs[:2]
-    refs = refs[2:]
-    if with_send:
-        send_ref = refs.pop(0)
+        summed_hbm, stats_ref, round_ref = refs[:3]
+        refs = refs[3:]
+        summed_ref, out_sems = refs.pop(), refs.pop()
+    else:
+        summed_ref, stats_ref = refs[:2]
+        refs = refs[2:]
     recv_ref, left_ref, dst_ref, noedge_ref, base_ref, sems = refs[:6]
     table_ref, even_ref, odd_ref, edge_ref, score_ref, scan_ref, mix_ref, acc_ref = refs[6:14]
-    refs = refs[14:]
-    if with_send:
-        round_ref, col_ref = refs
     copies = [
         pltpu.make_async_copy(source, target, sems.at[i])
         for i, (source, target) in enumerate(
@@ -397,6 +412,7 @@
     copies[3].wait()
     copies[4].wait()
     stats_ref[...] = jnp.zeros_like(stats_ref)
+    stores = []
     for k in range(NODE_CHUNKS):
         at = slice(k * CHUNK, (k + 1) * CHUNK)
         own_alpha = jnp.where(noedge_ref[at, 0:1] > 0, 1.0, acc_ref[at, FEAT:])
@@ -407,8 +423,11 @@
         stats_ref[1:2, :] += jnp.sum(summed * summed, axis=0, keepdims=True)
         if with_send:
             round_ref[at, :] = summed.astype(BF16)
-    if with_send:
-        pick_rows(list_ref, round_ref, send_ref, col_ref)
+            store = pltpu.make_async_copy(summed_ref.at[at], summed_hbm.at[at], out_sems.at[k])
+            store.start()
+            stores.append(store)
+    for store in stores:
+        store.wait()
 
 
 def norm_kernel(layer, total_nodes, summed_ref, stats_ref, gain_ref, shift_ref, out_ref):
@@ -428,6 +447,7 @@
 SMEM = pl.BlockSpec(memory_space=pltpu.SMEM)
 VMEM = pl.BlockSpec(memory_space=pltpu.VMEM)
 ANY = pl.BlockSpec(memory_space=pl.ANY)
+HBM = pl.BlockSpec(memory_space=pltpu.HBM)
 
 
 def call(body, name, outs, scratch, flops, args, in_specs=None, out_specs=None):
@@ -440,7 +460,7 @@
         out_specs=out_specs or [VMEM] * len(outs),
         scratch_shapes=scratch,
         cost_estimate=cost,
-        compiler_params=pltpu.CompilerParams(vmem_limit_bytes=24 << 20),
+        compiler_params=pltpu.CompilerParams(vmem_limit_bytes=67_000_000),
     )(*args)
 
 
@@ -482,6 +502,7 @@
 
 def own_part(layer, total_nodes, args):
     in_specs = [VMEM] * len(args)
+    in_specs[0] = HBM
     in_specs[-1] = SMEM
     return call(
         functools.partial(own_kernel, layer, total_nodes, layer > 0),
@@ -492,10 +513,19 @@
             shaped(EDGES_OWN, FEAT, BF16),
             shaped(8, EDGES_OWN, F32),
         ],
-        [pltpu.VMEM((NODES_OWN + CHUNK, FEAT + 128), BF16), pltpu.VMEM((CHUNK, FEAT + 128), F32)],
+        [
+            pltpu.VMEM((NODES_OWN + CHUNK, FEAT + 128), BF16),
+            pltpu.VMEM((CHUNK, FEAT + 128), F32),
+            pltpu.VMEM((NODES_OWN, FEAT), args[0].dtype),
+            pltpu.VMEM((NODES_OWN, FEAT), BF16),
+            pltpu.VMEM((NODES_OWN, FEAT), F32),
+            pltpu.VMEM((EDGES_OWN, FEAT), BF16),
+            pltpu.SemaphoreType.DMA((NODE_CHUNKS + 3,)),
+        ],
         3 * GIGA,
         args,
         in_specs=in_specs,
+        out_specs=[HBM, HBM, HBM, VMEM],
     )
 
 
@@ -519,9 +549,9 @@
         pltpu.VMEM((NODES_OWN + WINDOW, 2 * FEAT), F32),
     ]
     if with_send:
-        outs.append(shaped(ROWS_IN, FEAT, BF16))
-        scratch += [pltpu.VMEM((NODES_OWN, FEAT), BF16), pltpu.VMEM((ROWS_IN, 8), jnp.int32)]
-    in_specs = [ANY] * 5 + [VMEM] * (len(args) - 5)
+        outs.append(shaped(NODES_OWN, FEAT, BF16))
+        scratch += [pltpu.SemaphoreType.DMA((NODE_CHUNKS,)), pltpu.VMEM((NODES_OWN, FEAT), F32)]
+    in_specs = [ANY] + [HBM] * 4 + [VMEM] * (len(args) - 5)
     in_specs[9] = SMEM
     in_specs[11] = SMEM
     return call(
@@ -532,6 +562,7 @@
         5 * GIGA,
         args,
         in_specs=in_specs,
+        out_specs=[HBM, VMEM, VMEM] if with_send else None,
     )
 
 
@@ -544,6 +575,13 @@
 def shifted(value, axis, amount):
     size = lax.axis_size(axis)
     return lax.ppermute(value, axis, [(i, (i + amount) % size) for i in range(size)])
+
+
+def total_along(stats):
+    stats = stats + (
+        shifted(stats, "blk_0", 2) + shifted(stats, "blk_0", 4) + shifted(stats, "blk_0", 6)
+    )
+    return stats + shifted(stats, "blk_0", 1)
 
 
 def total_inside(stats):
@@ -552,10 +590,7 @@
         stats = stats + (
             shifted(stats, axis, 1) + shifted(stats, axis, 2) + shifted(stats, axis, 3)
         )
-    stats = stats + (
-        shifted(stats, "blk_0", 2) + shifted(stats, "blk_0", 4) + shifted(stats, "blk_0", 6)
-    )
-    return stats + shifted(stats, "blk_0", 1)
+    return stats
 
 
 def total_alone(stats):
@@ -591,12 +626,15 @@
     weights = [w_left, w_right, w_skip, attn_vec, rows, bound]
     left, base, dst, own = own_part(0, total_nodes, [features] + weights)
     edges = [rows, srcs, bias, bound]
-    summed, stats, sent = edge_part(
+    summed, stats, rounded = edge_part(
         0,
         total_nodes,
         True,
-        [received, left, dst, noedge, base, w_left, attn_vec, own] + edges + [send_list],
-    )
+        [received, left, dst, noedge, base, w_left, attn_vec, own] + edges,
+    )
+    stats = total_along(stats)
+    sent = send_rows(send_list, rounded)
+    sent, stats = lax.optimization_barrier((sent, stats))
     received = deliver(sent)
     stats = total_inside(stats)
     norms = [stats, norm_gain, norm_shift]

time: 166 us -> 162 us (0.976)
  local copies, waits for them, and re-layouts: 22.2 us -> 0.69 us
  Pallas kernels: 49.7 us -> 67.4 us
  blocking collectives: 26.7 us -> 23.9 us
  other arithmetic: 0.09 us -> 1.91 us
    unnamed x78 -> x0, local copies, waits for them, and re-layouts: 22.1 us -> none
    pallas_call x7 -> x8, Pallas kernels: 49.7 us -> 67.4 us  [call(): pl.pallas_call(body, name=name, out_shape=outs, in_specs=in_specs or [VME...]
    all_to_all x2, starting transfers between devices: 21.7 us -> 26.9 us  [deliver(): lax.all_to_all(rows.reshape(-1, 8, rows.shape[1]), GRP_BLK, split_axis=0,...]
    ppermute x11, starting transfers between devices: 16.8 us -> 12.6 us  [shifted(): lax.ppermute(value, axis, [(i, (i + amount) % size) for i in range(size)])]
    all_to_all x2, blocking collectives: 26.7 us -> 23.9 us  [total_alone(): stats = jnp.sum(lax.all_to_all(copies, axes, 0, 0, tiled=True), axis=0)]
    all_to_all x2, waiting for transfers between devices: 12.6 us -> 15 us  [deliver(): lax.all_to_all(rows.reshape(-1, 8, rows.shape[1]), GRP_BLK, split_axis=0,...]
    ppermute x11, waiting for transfers between devices: 14.8 us -> 12.7 us  [shifted(): lax.ppermute(value, axis, [(i, (i + amount) % size) for i in range(size)])]
  transfers between devices with their start and end apart: 13 -> 13, of which waited for: 9 -> 10; matrix products, arithmetic and copies ran while one was open for 0% -> 0% of each run, Pallas kernels for 12% -> 22%
where the time goes in v3:
time: 162 us; the launch traced here: 161 us
  Pallas kernels  67.4 us (42%)
  starting transfers between devices  39.5 us (24%)
  waiting for transfers between devices  27.7 us (17%)
  blocking collectives  23.9 us (15%)
  other arithmetic  1.91 us (1%)
    pallas_call x8, Pallas kernels, call(): pl.pallas_call(body, name=name, out_shape=outs, in_specs=in_specs or [VME...  67.4 us
    all_to_all x2, starting transfers between devices, deliver(): lax.all_to_all(rows.reshape(-1, 8, rows.shape[1]), GRP_BLK, split_axis=0,...  26.9 us
    all_to_all x2, blocking collectives, total_alone(): stats = jnp.sum(lax.all_to_all(copies, axes, 0, 0, tiled=True), axis=0)  23.9 us
    all_to_all x2, waiting for transfers between devices, deliver(): lax.all_to_all(rows.reshape(-1, 8, rows.shape[1]), GRP_BLK, split_axis=0,...  15 us
    ppermute x11, waiting for transfers between devices, shifted(): lax.ppermute(value, axis, [(i, (i + amount) % size) for i in range(size)])  12.7 us
    ppermute x11, starting transfers between devices, shifted(): lax.ppermute(value, axis, [(i, (i + amount) % size) for i in range(size)])  12.6 us
  transfers between devices with their start and end apart: 13, of which 10 were waited for; matrix products, arithmetic and copies ran while one was open for 0% of the time, Pallas kernels for 22%

profile of v3, /device:TPU:1, one launch (start us, length us, event | category | flops | bytes accessed | tf_op | source)
XLA Modules:
  0.0 161.1 jit_solution(6154424591722514291)
XLA Ops:
  0.0 5.6 %send_rows.2 = bf16[2048,256]{1,0:T(8,128)(2,1)} custom-call(s32[1,2048]{1,0:T(1,128)} %list_ref.3, bf16[1024,256]{1,0:T(8,128)(2,1)} %refs_0_.1), custom_call_target="tpu_custom_call" | custom-call | flops 1073741824 | bytes 4194304 | tf_op jit(solution)/shard_map/send_rows/pallas_call | solution.py:455
  5.6 16.6 %all-to-all-start = ((bf16[256,8,256]{2,1,0:T(8,128)(2,1)}), bf16[256,8,256]{2,1,0:T(8,128)(2,1)}, u32[]{:S(2)}, u32[]{:S(2)}) async-start(bf16[256,8,256]{2,1,0:T(8,128)(2,1)} %bitcast.8), calls=%async_computation | async-start | bytes 2097152 | tf_op jit(solution)/shard_map/all_to_all | solution.py:570
  22.2 9.4 %sort_edges.1 = (s32[8,2048]{1,0:T(8,128)}, s32[1,2048]{1,0:T(1,128)}, f32[8,2048]{1,0:T(8,128)}, f32[1024,8]{1,0:T(8,128)}, s32[1,32]{1,0:T(1,128)}) custom-call(s32[1,2048]{1,0:T(1,128)} %bitcast.9, s32[1,2048]{1,0:T(1,128)} %bitcast.10, s32[1,2048]{1,0:T(1,128)} %bitcast.11, f32[8,2048]{1,0:T(8,128)} %bias_ref.1), custom_call_target="tpu_custom_call" | custom-call | flops 2147483648 | bytes 4194304 | tf_op jit(solution)/shard_map/sort_edges/pallas_call | solution.py:455
  31.6 9.8 %own_part.2 = (bf16[1024,256]{1,0:T(8,128)(2,1)}, f32[1024,256]{1,0:T(8,128)}, bf16[2048,256]{1,0:T(8,128)(2,1)}, f32[8,2048]{1,0:T(8,128)}) custom-call(bf16[1024,256]{1,0:T(8,128)(2,1)} %refs_0_.1, bf16[2,256,256]{2,1,0:T(8,128)(2,1)} %refs_5_.5, bf16[2,256,256]{2,1,0:T(8,128)(2,1)} %refs_5_.4, bf16[2,256,256]{2,1,0:T(8,128)(2,1)} %refs_6_.4, ...), custom_call_target="tpu_custom_call" | custom-call | flops 3221225472 | bytes 4194304 | tf_op jit(solution)/shard_map/own_part/pallas_call | solution.py:455
  41.4 11.0 %all-to-all-done = bf16[256,8,256]{2,1,0:T(8,128)(2,1)} async-done(((bf16[256,8,256]{2,1,0:T(8,128)(2,1)}), bf16[256,8,256]{2,1,0:T(8,128)(2,1)}, u32[]{:S(2)}, u32[]{:S(2)}) %all-to-all-start) | async-done | bytes 1048608 | tf_op jit(solution)/shard_map/all_to_all | solution.py:570
  52.4 12.5 %edge_part.2 = (f32[1024,256]{1,0:T(8,128)}, f32[2,256]{1,0:T(2,128)}, bf16[1024,256]{1,0:T(8,128)(2,1)}) custom-call(bf16[2048,256]{1,0:T(8,128)(2,1)} %bitcast.1.refs_0_, bf16[1024,256]{1,0:T(8,128)(2,1)} %get-tuple-element.27.refs_1_, bf16[2048,256]{1,0:T(8,128)(2,1)} %get-tuple-element.28.refs_2_, f32[1024,8]{1,0:T(8,128)} %get-tuple-element.29.refs_3_, ...), custom_call_target="tpu_custom_call" | custom-call | flops 5368709120 | bytes 4194304 | tf_op jit(solution)/shard_map/edge_part/pallas_call | solution.py:455
  65.0 0.8 collective-permute-start.2
  65.8 3.1 %collective-permute-start.1 = (f32[2,256]{1,0:T(2,128)}, f32[2,256]{1,0:T(2,128)S(1)}, u32[]{:S(2)}, u32[]{:S(2)}) collective-permute-start(f32[2,256]{1,0:T(2,128)} %get-tuple-element.35), channel_id=1, source_target_pairs={{0,32},{8,40},{16,48},{24,56},{32,0},{40,8},{48,16},{56,24},{1,33}... | collective-permute-start | bytes 6152 | tf_op jit(solution)/shard_map/ppermute | solution.py:577
  68.8 0.0 collective-permute-start
  68.8 0.0 collective-permute-done.2
  68.8 3.5 %collective-permute-done.1 = f32[2,256]{1,0:T(2,128)S(1)} collective-permute-done((f32[2,256]{1,0:T(2,128)}, f32[2,256]{1,0:T(2,128)S(1)}, u32[]{:S(2)}, u32[]{:S(2)}) %collective-permute-start.1) | collective-permute-done | bytes 2080 | tf_op jit(solution)/shard_map/ppermute | solution.py:577
  72.3 1.3 collective-permute-done
  73.6 0.7 add_add_fusion.2
  74.2 0.9 collective-permute-start.3
  75.2 5.5 %send_rows.3 = bf16[2048,256]{1,0:T(8,128)(2,1)} custom-call(s32[1,2048]{1,0:T(1,128)} %list_ref.3, bf16[1024,256]{1,0:T(8,128)(2,1)} %get-tuple-element.34.table_ref), custom_call_target="tpu_custom_call" | custom-call | flops 1073741824 | bytes 4194304 | tf_op jit(solution)/shard_map/send_rows/pallas_call | solution.py:455
  80.7 0.0 collective-permute-done.3
  80.7 10.3 %all-to-all-start.1 = ((bf16[256,8,256]{2,1,0:T(8,128)(2,1)}), bf16[256,8,256]{2,1,0:T(8,128)(2,1)}, u32[]{:S(2)}, u32[]{:S(2)}) async-start(bf16[256,8,256]{2,1,0:T(8,128)(2,1)} %bitcast.7), calls=%async_computation.1 | async-start | bytes 2097152 | tf_op jit(solution)/shard_map/all_to_all | solution.py:570
  91.0 2.3 %collective-permute-start.4 = (f32[2,256]{1,0:T(2,128)S(1)}, f32[2,256]{1,0:T(2,128)S(1)}, u32[]{:S(2)}, u32[]{:S(2)}) collective-permute-start(f32[2,256]{1,0:T(2,128)S(1)} %add.36), channel_id=1, source_target_pairs={{0,1},{1,0},{2,3},{3,2},{4,5},{5,4},{6,7},{7,6},{8,9},{9,8},{10,11... | collective-permute-start | bytes 6152 | tf_op jit(solution)/shard_map/ppermute | solution.py:577
  93.3 0.8 collective-permute-done.4
  94.1 0.7 collective-permute-start.7
  94.9 0.6 collective-permute-start.6
  95.4 0.6 collective-permute-start.5
  96.0 1.0 collective-permute-done.7
  97.0 2.2 %collective-permute-done.6 = f32[2,256]{1,0:T(2,128)S(1)} collective-permute-done((f32[2,256]{1,0:T(2,128)S(1)}, f32[2,256]{1,0:T(2,128)S(1)}, u32[]{:S(2)}, u32[]{:S(2)}) %collective-permute-start.6) | collective-permute-done | bytes 2080 | tf_op jit(solution)/shard_map/ppermute | solution.py:577
  99.2 0.3 collective-permute-done.5
  99.5 2.5 %collective-permute-start.10 = (f32[2,256]{1,0:T(2,128)S(1)}, f32[2,256]{1,0:T(2,128)S(1)}, u32[]{:S(2)}, u32[]{:S(2)}) collective-permute-start(f32[2,256]{1,0:T(2,128)S(1)} %add_add_fusion.1), channel_id=1, source_target_pairs={{0,192},{64,0},{128,64},{192,128},{1,193},{65,1},{129,65},{193,129... | collective-permute-start | bytes 6152 | tf_op jit(solution)/shard_map/ppermute | solution.py:577
  102.0 0.5 collective-permute-start.9
  102.5 0.6 collective-permute-start.8
  103.1 0.0 collective-permute-done.10
  103.1 3.3 %collective-permute-done.9 = f32[2,256]{1,0:T(2,128)S(1)} collective-permute-done((f32[2,256]{1,0:T(2,128)S(1)}, f32[2,256]{1,0:T(2,128)S(1)}, u32[]{:S(2)}, u32[]{:S(2)}) %collective-permute-start.9) | collective-permute-done | bytes 2080 | tf_op jit(solution)/shard_map/ppermute | solution.py:577
  106.3 0.4 collective-permute-done.8
  106.7 0.6 add_add_fusion.refs_1_.refs_12_
  107.3 9.9 %own_part.3 = (bf16[1024,256]{1,0:T(8,128)(2,1)}, f32[1024,256]{1,0:T(8,128)}, bf16[2048,256]{1,0:T(8,128)(2,1)}, f32[8,2048]{1,0:T(8,128)}) custom-call(f32[1024,256]{1,0:T(8,128)} %get-tuple-element.37.refs_0_, f32[2,256]{1,0:T(2,128)} %add_add_fusion.refs_1_.refs_12_, bf16[2,256]{1,0:T(2,128)(2,1)} %gain_ref.1, bf16[2,256]{1,0:T(2,128)(2,1)} %shift_ref.1, ...), custom_call_target="tpu_custom_call" | custom-call | flops 3221225472 | bytes 4194304 | tf_op jit(solution)/shard_map/own_part/pallas_call | solution.py:455
  117.2 4.0 %all-to-all-done.1 = bf16[256,8,256]{2,1,0:T(8,128)(2,1)} async-done(((bf16[256,8,256]{2,1,0:T(8,128)(2,1)}), bf16[256,8,256]{2,1,0:T(8,128)(2,1)}, u32[]{:S(2)}, u32[]{:S(2)}) %all-to-all-start.1) | async-done | bytes 1048608 | tf_op jit(solution)/shard_map/all_to_all | solution.py:570
  121.2 12.3 %edge_part.3 = (f32[1024,256]{1,0:T(8,128)}, f32[2,256]{1,0:T(2,128)}) custom-call(bf16[2048,256]{1,0:T(8,128)(2,1)} %bitcast.6.refs_0_, bf16[1024,256]{1,0:T(8,128)(2,1)} %get-tuple-element.39.refs_1_, bf16[2048,256]{1,0:T(8,128)(2,1)} %get-tuple-element.40.refs_2_, f32[1024,8]{1,0:T(8,128)} %get-tuple-element.29.refs_3_, ...), custom_call_target="tpu_custom_call" | custom-call | flops 5368709120 | bytes 4194304 | tf_op jit(solution)/shard_map/edge_part/pallas_call | solution.py:455
  133.5 0.7 broadcast_in_dim.4
  134.2 9.0 %all_to_all.20 = f32[8,2,256]{2,1,0:T(2,128)S(1)} all-to-all(f32[8,2,256]{2,1,0:T(2,128)S(1)} %broadcast_in_dim.4), channel_id=1, replica_groups=mesh['grp'=4,'blk_0'=8,'blk_1'=4,'blk_2'=2] {'blk_1','blk_2'}, dimensions={0} | all-to-all | bytes 32768 | tf_op jit(solution)/shard_map/all_to_all | solution.py:600
  143.2 14.9 %all_to_all.21 = f32[32,2,256]{2,1,0:T(2,128)S(1)} all-to-all(f32[32,2,256]{2,1,0:T(2,128)S(1)} %broadcast_in_dim.5), channel_id=1, replica_groups=mesh['grp'=4,'blk_0'=8,'blk_1'=4,'blk_2'=2] {'grp','blk_0'}, dimensions={0} | all-to-all | bytes 131072 | tf_op jit(solution)/shard_map/all_to_all | solution.py:600
  158.1 0.6 reduce_sum.19.stats_ref
  158.7 2.4 %norm_out.1 = bf16[1024,256]{1,0:T(8,128)(2,1)} custom-call(f32[1024,256]{1,0:T(8,128)} %get-tuple-element.43.summed_ref, f32[2,256]{1,0:T(2,128)} %reduce_sum.19.stats_ref, bf16[2,256]{1,0:T(2,128)(2,1)} %gain_ref.1, bf16[2,256]{1,0:T(2,128)(2,1)} %shift_ref.1), custom_call_target="tpu_custom_call" | custom-call | flops 1048576 | bytes 4194304 | tf_op jit(solution)/shard_map/norm_out/pallas_call | solution.py:455
  (5 shorter events, 0.1 us)
Async XLA Ops:
  5.6 46.9 %all-to-all-start = ((bf16[256,8,256]{2,1,0:T(8,128)(2,1)}), bf16[256,8,256]{2,1,0:T(8,128)(2,1)}, u32[]{:S(2)}, u32[]{:S(2)}) async-start(bf16[256,8,256]{2,1,0:T(8,128)(2,1)} %bitcast.8), calls=%async_computation | async-start | bytes 2097152 | tf_op jit(solution)/shard_map/all_to_all | solution.py:570
  65.0 3.9 %collective-permute-start.2 = (f32[2,256]{1,0:T(2,128)}, f32[2,256]{1,0:T(2,128)S(1)}, u32[]{:S(2)}, u32[]{:S(2)}) collective-permute-start(f32[2,256]{1,0:T(2,128)} %get-tuple-element.35), channel_id=1, source_target_pairs={{0,48},{8,56},{16,0},{24,8},{32,16},{40,24},{48,32},{56,40},{1,49}... | collective-permute-start | bytes 6152 | tf_op jit(solution)/shard_map/ppermute | solution.py:577
  65.8 6.6 %collective-permute-start.1 = (f32[2,256]{1,0:T(2,128)}, f32[2,256]{1,0:T(2,128)S(1)}, u32[]{:S(2)}, u32[]{:S(2)}) collective-permute-start(f32[2,256]{1,0:T(2,128)} %get-tuple-element.35), channel_id=1, source_target_pairs={{0,32},{8,40},{16,48},{24,56},{32,0},{40,8},{48,16},{56,24},{1,33}... | collective-permute-start | bytes 6152 | tf_op jit(solution)/shard_map/ppermute | solution.py:577
  68.8 4.8 %collective-permute-start = (f32[2,256]{1,0:T(2,128)}, f32[2,256]{1,0:T(2,128)S(1)}, u32[]{:S(2)}, u32[]{:S(2)}) collective-permute-start(f32[2,256]{1,0:T(2,128)} %get-tuple-element.35), channel_id=1, source_target_pairs={{0,16},{8,24},{16,32},{24,40},{32,48},{40,56},{48,0},{56,8},{1,17}... | collective-permute-start | bytes 6152 | tf_op jit(solution)/shard_map/ppermute | solution.py:577
  74.2 6.5 %collective-permute-start.3 = (f32[2,256]{1,0:T(2,128)S(1)}, f32[2,256]{1,0:T(2,128)S(1)}, u32[]{:S(2)}, u32[]{:S(2)}) collective-permute-start(f32[2,256]{1,0:T(2,128)S(1)} %add_add_fusion.2), channel_id=1, source_target_pairs={{0,8},{8,16},{16,24},{24,32},{32,40},{40,48},{48,56},{56,0},{1,9},... | collective-permute-start | bytes 6152 | tf_op jit(solution)/shard_map/ppermute | solution.py:577
  80.7 40.5 %all-to-all-start.1 = ((bf16[256,8,256]{2,1,0:T(8,128)(2,1)}), bf16[256,8,256]{2,1,0:T(8,128)(2,1)}, u32[]{:S(2)}, u32[]{:S(2)}) async-start(bf16[256,8,256]{2,1,0:T(8,128)(2,1)} %bitcast.7), calls=%async_computation.1 | async-start | bytes 2097152 | tf_op jit(solution)/shard_map/all_to_all | solution.py:570
  91.0 3.1 %collective-permute-start.4 = (f32[2,256]{1,0:T(2,128)S(1)}, f32[2,256]{1,0:T(2,128)S(1)}, u32[]{:S(2)}, u32[]{:S(2)}) collective-permute-start(f32[2,256]{1,0:T(2,128)S(1)} %add.36), channel_id=1, source_target_pairs={{0,1},{1,0},{2,3},{3,2},{4,5},{5,4},{6,7},{7,6},{8,9},{9,8},{10,11... | collective-permute-start | bytes 6152 | tf_op jit(solution)/shard_map/ppermute | solution.py:577
  94.1 2.9 %collective-permute-start.7 = (f32[2,256]{1,0:T(2,128)S(1)}, f32[2,256]{1,0:T(2,128)S(1)}, u32[]{:S(2)}, u32[]{:S(2)}) collective-permute-start(f32[2,256]{1,0:T(2,128)S(1)} %add.37), channel_id=1, source_target_pairs={{0,6},{2,0},{4,2},{6,4},{1,7},{3,1},{5,3},{7,5},{8,14},{10,8},{12,... | collective-permute-start | bytes 6152 | tf_op jit(solution)/shard_map/ppermute | solution.py:577
  94.9 4.4 %collective-permute-start.6 = (f32[2,256]{1,0:T(2,128)S(1)}, f32[2,256]{1,0:T(2,128)S(1)}, u32[]{:S(2)}, u32[]{:S(2)}) collective-permute-start(f32[2,256]{1,0:T(2,128)S(1)} %add.37), channel_id=1, source_target_pairs={{0,4},{2,6},{4,0},{6,2},{1,5},{3,7},{5,1},{7,3},{8,12},{10,14},{12... | collective-permute-start | bytes 6152 | tf_op jit(solution)/shard_map/ppermute | solution.py:577
  95.4 4.0 %collective-permute-start.5 = (f32[2,256]{1,0:T(2,128)S(1)}, f32[2,256]{1,0:T(2,128)S(1)}, u32[]{:S(2)}, u32[]{:S(2)}) collective-permute-start(f32[2,256]{1,0:T(2,128)S(1)} %add.37), channel_id=1, source_target_pairs={{0,2},{2,4},{4,6},{6,0},{1,3},{3,5},{5,7},{7,1},{8,10},{10,12},{12... | collective-permute-start | bytes 6152 | tf_op jit(solution)/shard_map/ppermute | solution.py:577
  99.5 3.6 %collective-permute-start.10 = (f32[2,256]{1,0:T(2,128)S(1)}, f32[2,256]{1,0:T(2,128)S(1)}, u32[]{:S(2)}, u32[]{:S(2)}) collective-permute-start(f32[2,256]{1,0:T(2,128)S(1)} %add_add_fusion.1), channel_id=1, source_target_pairs={{0,192},{64,0},{128,64},{192,128},{1,193},{65,1},{129,65},{193,129... | collective-permute-start | bytes 6152 | tf_op jit(solution)/shard_map/ppermute | solution.py:577
  102.0 4.3 %collective-permute-start.9 = (f32[2,256]{1,0:T(2,128)S(1)}, f32[2,256]{1,0:T(2,128)S(1)}, u32[]{:S(2)}, u32[]{:S(2)}) collective-permute-start(f32[2,256]{1,0:T(2,128)S(1)} %add_add_fusion.1), channel_id=1, source_target_pairs={{0,128},{64,192},{128,0},{192,64},{1,129},{65,193},{129,1},{193,65... | collective-permute-start | bytes 6152 | tf_op jit(solution)/shard_map/ppermute | solution.py:577
  102.5 4.2 %collective-permute-start.8 = (f32[2,256]{1,0:T(2,128)S(1)}, f32[2,256]{1,0:T(2,128)S(1)}, u32[]{:S(2)}, u32[]{:S(2)}) collective-permute-start(f32[2,256]{1,0:T(2,128)S(1)} %add_add_fusion.1), channel_id=1, source_target_pairs={{0,64},{64,128},{128,192},{192,0},{1,65},{65,129},{129,193},{193,1... | collective-permute-start | bytes 6152 | tf_op jit(solution)/shard_map/ppermute | solution.py:577

commit v4 on v3

--- a/solution.py
+++ b/solution.py
@@ -90,20 +90,47 @@
     return jnp.transpose(jnp.broadcast_to(row, (8, row.shape[1])))
 
 
-def pick_rows(list_ref, table_ref, out_ref, col_ref):
-    col_ref[...] = columns_of(list_ref[...].astype(F32)).astype(jnp.int32)
-
-    def step(c, carry):
-        at = pl.ds(pl.multiple_of(c * CHUNK, CHUNK), CHUNK)
-        hot = one_hot(col_ref[at, 0:1] == iota((CHUNK, NODES_OWN), 1))
-        out_ref[at, :] = dot(hot, table_ref[...]).astype(BF16)
+def put_rows(pairs_ref, first, values):
+    half = FEAT // 2
+    pairs_ref[pl.ds(2 * first, CHUNK, stride=2), :] = values[:, :half]
+    pairs_ref[pl.ds(2 * first + 1, CHUNK, stride=2), :] = values[:, half:]
+
+
+def get_rows(pairs_ref):
+    return jnp.concatenate(
+        [pairs_ref[pl.ds(0, CHUNK, stride=2), :], pairs_ref[pl.ds(1, CHUNK, stride=2), :]], axis=1
+    )
+
+
+def fetch_rows(index_ref, first, pairs_ref, got_ref):
+    for e in range(CHUNK):
+        row = index_ref[0, first + e]
+        got_ref[2 * e : 2 * e + 2, :] = pairs_ref[pl.ds(pl.multiple_of(2 * row, 2), 2), :]
+
+
+def send_kernel(index_ref, list_ref, table_ref, out_hbm, pairs_ref, got_ref, out_ref, sems):
+    for k in range(NODE_CHUNKS):
+        put_rows(pairs_ref, k * CHUNK, table_ref[k * CHUNK : (k + 1) * CHUNK, :].astype(F32))
+
+    def store(c):
+        at = pl.ds(pl.multiple_of(c * 2 * CHUNK, 2 * CHUNK), 2 * CHUNK)
+        return pltpu.make_async_copy(out_ref.at[at], out_hbm.at[at], sems.at[c])
+
+    def pair(c, carry):
+        here = pl.ds(pl.multiple_of(c * 2 * CHUNK, CHUNK), CHUNK)
+        after = pl.ds(pl.multiple_of(c * 2 * CHUNK + CHUNK, CHUNK), CHUNK)
+        fetch_rows(index_ref, c * 2 * CHUNK + CHUNK, pairs_ref, got_ref)
+        col = columns_of(list_ref[0:1, here].astype(F32)).astype(jnp.int32)[:, 0:1]
+        hot = one_hot(col == iota((CHUNK, NODES_OWN), 1))
+        out_ref[here, :] = dot(hot, table_ref[...]).astype(BF16)
+        out_ref[after, :] = get_rows(got_ref).astype(BF16)
+        store(c).start()
         return carry
 
-    lax.fori_loop(0, ROWS_IN // CHUNK, step, 0)
-
-
-def send_kernel(list_ref, table_ref, out_ref, col_ref):
-    pick_rows(list_ref, table_ref, out_ref, col_ref)
+    count = ROWS_IN // (2 * CHUNK)
+    lax.fori_loop(0, count, pair, 0)
+    for c in range(count):
+        store(c).wait()
 
 
 def sort_kernel(
@@ -286,26 +313,23 @@
     if with_norm:
         stats_in, gain_ref, shift_ref = refs[:3]
         refs = refs[3:]
+    summed_hbm, stats_ref = refs[:2]
+    refs = refs[2:]
     if with_send:
-        summed_hbm, stats_ref, round_ref = refs[:3]
-        refs = refs[3:]
-        summed_ref, out_sems = refs.pop(), refs.pop()
-    else:
-        summed_ref, stats_ref = refs[:2]
-        refs = refs[2:]
+        round_ref = refs.pop(0)
+    summed_ref, out_sems = refs.pop(), refs.pop()
     recv_ref, left_ref, dst_ref, noedge_ref, base_ref, sems = refs[:6]
     table_ref, even_ref, odd_ref, edge_ref, score_ref, scan_ref, mix_ref, acc_ref = refs[6:14]
+    piece = ROWS_IN // 4
+    moves = [
+        (recv_any.at[k * piece : (k + 1) * piece], recv_ref.at[k * piece : (k + 1) * piece])
+        for k in range(4)
+    ]
+    moves += [(left_any, left_ref), (dst_any, dst_ref)]
+    moves += [(noedge_any, noedge_ref), (base_any, base_ref)]
     copies = [
         pltpu.make_async_copy(source, target, sems.at[i])
-        for i, (source, target) in enumerate(
-            (
-                (left_any, left_ref),
-                (recv_any, recv_ref),
-                (dst_any, dst_ref),
-                (noedge_any, noedge_ref),
-                (base_any, base_ref),
-            )
-        )
+        for i, (source, target) in enumerate(moves)
     ]
     for copy in copies:
         copy.start()
@@ -317,44 +341,29 @@
             shift_ref[layer - 1 : layer, :].astype(F32),
         )
     heads = head_rows(attn_ref, layer)
-    half = FEAT // 2
-
-    def put_rows(first, values):
-        table_ref[pl.ds(2 * first, CHUNK, stride=2), :] = values[:, :half]
-        table_ref[pl.ds(2 * first + 1, CHUNK, stride=2), :] = values[:, half:]
-
-    copies[0].wait()
-    for k in range(NODE_CHUNKS):
-        put_rows(k * CHUNK, left_ref[k * CHUNK : (k + 1) * CHUNK, :].astype(F32))
-    copies[1].wait()
-
-    def fill(c, carry):
-        at = pl.ds(pl.multiple_of(c * CHUNK, CHUNK), CHUNK)
-        states = recv_ref[at, :]
+    for c in range(ROWS_IN // CHUNK):
+        if c * CHUNK % piece == 0:
+            copies[c * CHUNK // piece].wait()
+        states = recv_ref[c * CHUNK : (c + 1) * CHUNK, :]
         if with_norm:
             states = normalize(states.astype(F32), terms)
         left = dot(states, wl_ref[layer]).astype(BF16).astype(F32)
-        put_rows(pl.multiple_of(NODES_OWN + c * CHUNK, CHUNK), left)
-        return carry
-
-    lax.fori_loop(0, ROWS_IN // CHUNK, fill, 0, unroll=2)
+        put_rows(table_ref, NODES_OWN + c * CHUNK, left)
+    copies[4].wait()
+    for k in range(NODE_CHUNKS):
+        put_rows(table_ref, k * CHUNK, left_ref[k * CHUNK : (k + 1) * CHUNK, :].astype(F32))
 
     def fetch(c, out_ref):
-        first = c * CHUNK
-        for e in range(CHUNK):
-            row = srcs_ref[0, first + e]
-            out_ref[2 * e : 2 * e + 2, :] = table_ref[pl.ds(pl.multiple_of(2 * row, 2), 2), :]
+        fetch_rows(srcs_ref, c * CHUNK, table_ref, out_ref)
 
     def score(c, in_ref):
         at = pl.ds(pl.multiple_of(c * CHUNK, CHUNK), CHUNK)
-        src = jnp.concatenate(
-            [in_ref[pl.ds(0, CHUNK, stride=2), :], in_ref[pl.ds(1, CHUNK, stride=2), :]], axis=1
-        )
+        src = get_rows(in_ref)
         edge_ref[at, :] = src.astype(BF16)
         score_ref[:, at] = scores_of(heads, leaky(src + dst_ref[at, :].astype(F32)))
 
     fetch(0, even_ref)
-    copies[2].wait()
+    copies[5].wait()
 
     def pair(c, carry):
         fetch(2 * c + 1, odd_ref)
@@ -409,8 +418,8 @@
         return lax.fori_loop(0, count, window, carry)
 
     lax.fori_loop(0, EDGE_CHUNKS, gather_in, 0)
-    copies[3].wait()
-    copies[4].wait()
+    copies[6].wait()
+    copies[7].wait()
     stats_ref[...] = jnp.zeros_like(stats_ref)
     stores = []
     for k in range(NODE_CHUNKS):
@@ -423,21 +432,11 @@
         stats_ref[1:2, :] += jnp.sum(summed * summed, axis=0, keepdims=True)
         if with_send:
             round_ref[at, :] = summed.astype(BF16)
-            store = pltpu.make_async_copy(summed_ref.at[at], summed_hbm.at[at], out_sems.at[k])
-            store.start()
-            stores.append(store)
+        store = pltpu.make_async_copy(summed_ref.at[at], summed_hbm.at[at], out_sems.at[k])
+        store.start()
+        stores.append(store)
     for store in stores:
         store.wait()
-
-
-def norm_kernel(layer, total_nodes, summed_ref, stats_ref, gain_ref, shift_ref, out_ref):
-    terms = norm_terms(
-        stats_ref[...],
-        total_nodes,
-        gain_ref[layer : layer + 1, :].astype(F32),
-        shift_ref[layer : layer + 1, :].astype(F32),
-    )
-    out_ref[...] = normalize(summed_ref[...], terms)
 
 
 def shaped(rows, cols, dtype):
@@ -472,9 +471,16 @@
         send_kernel,
         "send_rows",
         [shaped(ROWS_IN, FEAT, BF16)],
-        [pltpu.VMEM((ROWS_IN, 8), jnp.int32)],
+        [
+            pltpu.VMEM((2 * NODES_OWN, FEAT // 2), F32),
+            pltpu.VMEM((2 * CHUNK, FEAT // 2), F32),
+            pltpu.VMEM((ROWS_IN, FEAT), BF16),
+            pltpu.SemaphoreType.DMA((ROWS_IN // (2 * CHUNK),)),
+        ],
         GIGA,
-        [send_list, table],
+        [send_list, send_list, table],
+        in_specs=[SMEM, VMEM, VMEM],
+        out_specs=[HBM],
     )[0]
 
 
@@ -538,7 +544,7 @@
         pltpu.VMEM((EDGES_OWN, FEAT), BF16),
         pltpu.VMEM((NODES_OWN, 8), F32),
         pltpu.VMEM((NODES_OWN, FEAT), F32),
-        pltpu.SemaphoreType.DMA((5,)),
+        pltpu.SemaphoreType.DMA((8,)),
         pltpu.VMEM((2 * TABLE_ROWS, half), F32),
         pltpu.VMEM((2 * CHUNK, half), F32),
         pltpu.VMEM((2 * CHUNK, half), F32),
@@ -550,7 +556,7 @@
     ]
     if with_send:
         outs.append(shaped(NODES_OWN, FEAT, BF16))
-        scratch += [pltpu.SemaphoreType.DMA((NODE_CHUNKS,)), pltpu.VMEM((NODES_OWN, FEAT), F32)]
+    scratch += [pltpu.SemaphoreType.DMA((NODE_CHUNKS,)), pltpu.VMEM((NODES_OWN, FEAT), F32)]
     in_specs = [ANY] + [HBM] * 4 + [VMEM] * (len(args) - 5)
     in_specs[9] = SMEM
     in_specs[11] = SMEM
@@ -562,7 +568,7 @@
         5 * GIGA,
         args,
         in_specs=in_specs,
-        out_specs=[HBM, VMEM, VMEM] if with_send else None,
+        out_specs=[HBM] + [VMEM] * (len(outs) - 1),
     )
 
 
@@ -577,11 +583,14 @@
     return lax.ppermute(value, axis, [(i, (i + amount) % size) for i in range(size)])
 
 
+def copies_summed(stats, axes):
+    size = lax.axis_size(axes)
+    copies = jnp.broadcast_to(stats[None], (size,) + stats.shape)
+    return jnp.sum(lax.all_to_all(copies, axes, 0, 0, tiled=True), axis=0)
+
+
 def total_along(stats):
-    stats = stats + (
-        shifted(stats, "blk_0", 2) + shifted(stats, "blk_0", 4) + shifted(stats, "blk_0", 6)
-    )
-    return stats + shifted(stats, "blk_0", 1)
+    return copies_summed(stats, ("blk_0",))
 
 
 def total_inside(stats):
@@ -594,11 +603,13 @@
 
 
 def total_alone(stats):
-    for axes in (("blk_1", "blk_2"), ("grp", "blk_0")):
-        size = lax.axis_size(axes)
-        copies = jnp.broadcast_to(stats[None], (size,) + stats.shape)
-        stats = jnp.sum(lax.all_to_all(copies, axes, 0, 0, tiled=True), axis=0)
-    return stats
+    first = lax.axis_index("blk_2") == 0
+    mine = jnp.where(first, stats[0:1], stats[1:2])
+    other = jnp.where(first, stats[1:2], stats[0:1])
+    mine = (mine + shifted(other, "blk_2", 1)).reshape(2, FEAT // 2)
+    mine = copies_summed(mine, ("grp", "blk_0", "blk_1")).reshape(1, FEAT)
+    other = shifted(mine, "blk_2", 1)
+    return jnp.concatenate([jnp.where(first, mine, other), jnp.where(first, other, mine)])
 
 
 def local(
@@ -646,14 +657,8 @@
         [received, left, dst, noedge, base, w_left, attn_vec, own] + edges + norms,
     )
     stats = total_alone(stats)
-    return call(
-        functools.partial(norm_kernel, 1, total_nodes),
-        "norm_out",
-        [shaped(NODES_OWN, FEAT, BF16)],
-        [],
-        1 << 20,
-        [summed, stats, norm_gain, norm_shift],
-    )[0]
+    terms = norm_terms(stats, total_nodes, norm_gain[1:2].astype(F32), norm_shift[1:2].astype(F32))
+    return normalize(summed, terms)
 
 
 def solution(mesh):

time: 162 us -> 159 us (0.981)
  blocking collectives: 23.9 us -> 0 us
  starting transfers between devices: 39.5 us -> 55.3 us
  waiting for transfers between devices: 27.7 us -> 33.6 us
  Pallas kernels: 67.4 us -> 63.6 us
  other arithmetic: 1.91 us -> 3.93 us
    all_to_all x2 -> x0, blocking collectives: 23.9 us -> none  [total_alone(): stats = jnp.sum(lax.all_to_all(copies, axes, 0, 0, tiled=True), axis=0)]
    all_to_all x0 -> x2, starting transfers between devices: none -> 15.1 us  [copies_summed(): return jnp.sum(lax.all_to_all(copies, axes, 0, 0, tiled=True), axis=0)]
    all_to_all x0 -> x2, waiting for transfers between devices: none -> 12.9 us  [copies_summed(): return jnp.sum(lax.all_to_all(copies, axes, 0, 0, tiled=True), axis=0)]
    ppermute x11 -> x9, waiting for transfers between devices: 12.7 us -> 5.82 us  [shifted(): lax.ppermute(value, axis, [(i, (i + amount) % size) for i in range(size)])]
    pallas_call x8 -> x7, Pallas kernels: 67.4 us -> 63.6 us  [call(): pl.pallas_call(body, name=name, out_shape=outs, in_specs=in_specs or [VME...]
    convert_element_type x0 -> x1, other arithmetic: none -> 2.38 us  [normalize(): return jnp.where(scaled > 0, scaled, grown).astype(BF16)]
    ppermute x11 -> x9, starting transfers between devices: 12.6 us -> 13.2 us  [shifted(): lax.ppermute(value, axis, [(i, (i + amount) % size) for i in range(size)])]
  transfers between devices with their start and end apart: 13 -> 13, of which waited for: 10 -> 12; matrix products, arithmetic and copies ran while one was open for 0% -> 0% of each run, Pallas kernels for 22% -> 22%
where the time goes in v4:
time: 159 us
  Pallas kernels  63.6 us (40%)
  starting transfers between devices  55.3 us (35%)
  waiting for transfers between devices  33.6 us (21%)
  other arithmetic  3.93 us (2%)
  local copies, waits for them, and re-layouts  1.97 us (1%)
    pallas_call x7, Pallas kernels, call(): pl.pallas_call(body, name=name, out_shape=outs, in_specs=in_specs or [VME...  63.6 us
    all_to_all x2, starting transfers between devices, deliver(): lax.all_to_all(rows.reshape(-1, 8, rows.shape[1]), GRP_BLK, split_axis=0,...  26.9 us
    all_to_all x2, starting transfers between devices, copies_summed(): return jnp.sum(lax.all_to_all(copies, axes, 0, 0, tiled=True), axis=0)  15.1 us
    all_to_all x2, waiting for transfers between devices, deliver(): lax.all_to_all(rows.reshape(-1, 8, rows.shape[1]), GRP_BLK, split_axis=0,...  14.9 us
    ppermute x9, starting transfers between devices, shifted(): lax.ppermute(value, axis, [(i, (i + amount) % size) for i in range(size)])  13.2 us
    all_to_all x2, waiting for transfers between devices, copies_summed(): return jnp.sum(lax.all_to_all(copies, axes, 0, 0, tiled=True), axis=0)  12.9 us
    ppermute x9, waiting for transfers between devices, shifted(): lax.ppermute(value, axis, [(i, (i + amount) % size) for i in range(size)])  5.82 us
  transfers between devices with their start and end apart: 13, of which 12 were waited for; matrix products, arithmetic and copies ran while one was open for 0% of the time, Pallas kernels for 22%

profile of v4, /device:TPU:1, one launch (start us, length us, event | category | flops | bytes accessed | tf_op | source)
XLA Modules:
  0.0 158.5 jit_solution(3938479936404897688)
XLA Ops:
  0.0 4.6 %send_rows.2 = bf16[2048,256]{1,0:T(8,128)(2,1)} custom-call(s32[1,2048]{1,0:T(1,128)} %list_ref.3, s32[1,2048]{1,0:T(1,128)} %list_ref.3, bf16[1024,256]{1,0:T(8,128)(2,1)} %refs_0_.1), custom_call_target="tpu_custom_call" | custom-call | flops 1073741824 | bytes 4194304 | tf_op jit(solution)/shard_map/send_rows/pallas_call | solution.py:454
  4.6 16.7 %all-to-all-start = ((bf16[256,8,256]{2,1,0:T(8,128)(2,1)}), bf16[256,8,256]{2,1,0:T(8,128)(2,1)}, u32[]{:S(2)}, u32[]{:S(2)}) async-start(bf16[256,8,256]{2,1,0:T(8,128)(2,1)} %bitcast.14), calls=%async_computation | async-start | bytes 2097152 | tf_op jit(solution)/shard_map/all_to_all | solution.py:576
  21.2 9.4 %sort_edges.1 = (s32[8,2048]{1,0:T(8,128)}, s32[1,2048]{1,0:T(1,128)}, f32[8,2048]{1,0:T(8,128)}, f32[1024,8]{1,0:T(8,128)}, s32[1,32]{1,0:T(1,128)}) custom-call(s32[1,2048]{1,0:T(1,128)} %bitcast.22, s32[1,2048]{1,0:T(1,128)} %bitcast.23, s32[1,2048]{1,0:T(1,128)} %bitcast.24, f32[8,2048]{1,0:T(8,128)} %bias_ref.1), custom_call_target="tpu_custom_call" | custom-call | flops 2147483648 | bytes 4194304 | tf_op jit(solution)/shard_map/sort_edges/pallas_call | solution.py:454
  30.6 10.4 %own_part.2 = (bf16[1024,256]{1,0:T(8,128)(2,1)}, f32[1024,256]{1,0:T(8,128)}, bf16[2048,256]{1,0:T(8,128)(2,1)}, f32[8,2048]{1,0:T(8,128)}) custom-call(bf16[1024,256]{1,0:T(8,128)(2,1)} %refs_0_.1, bf16[2,256,256]{2,1,0:T(8,128)(2,1)} %refs_5_.5, bf16[2,256,256]{2,1,0:T(8,128)(2,1)} %refs_5_.4, bf16[2,256,256]{2,1,0:T(8,128)(2,1)} %refs_6_.4, ...), custom_call_target="tpu_custom_call" | custom-call | flops 3221225472 | bytes 4194304 | tf_op jit(solution)/shard_map/own_part/pallas_call | solution.py:454
  41.0 10.4 %all-to-all-done = bf16[256,8,256]{2,1,0:T(8,128)(2,1)} async-done(((bf16[256,8,256]{2,1,0:T(8,128)(2,1)}), bf16[256,8,256]{2,1,0:T(8,128)(2,1)}, u32[]{:S(2)}, u32[]{:S(2)}) %all-to-all-start) | async-done | bytes 1048608 | tf_op jit(solution)/shard_map/all_to_all | solution.py:576
  51.5 12.0 %edge_part.2 = (f32[1024,256]{1,0:T(8,128)}, f32[2,256]{1,0:T(2,128)}, bf16[1024,256]{1,0:T(8,128)(2,1)}) custom-call(bf16[2048,256]{1,0:T(8,128)(2,1)} %bitcast.1.refs_0_, bf16[1024,256]{1,0:T(8,128)(2,1)} %get-tuple-element.27.refs_1_, bf16[2048,256]{1,0:T(8,128)(2,1)} %get-tuple-element.28.refs_2_, f32[1024,8]{1,0:T(8,128)} %get-tuple-element.29.refs_3_, ...), custom_call_target="tpu_custom_call" | custom-call | flops 5368709120 | bytes 4194304 | tf_op jit(solution)/shard_map/edge_part/pallas_call | solution.py:454
  63.5 1.3 broadcast_in_dim.6
  64.7 3.3 %all-to-all-start.1 = ((f32[8,2,256]{2,1,0:T(2,128)}), f32[8,2,256]{2,1,0:T(2,128)S(1)}, u32[]{:S(2)}, u32[]{:S(2)}) async-start(f32[8,2,256]{2,1,0:T(2,128)} %broadcast_in_dim.6), calls=%async_computation.1 | async-start | bytes 32768 | tf_op jit(solution)/shard_map/all_to_all | solution.py:589
  68.1 4.6 %send_rows.3 = bf16[2048,256]{1,0:T(8,128)(2,1)} custom-call(s32[1,2048]{1,0:T(1,128)} %list_ref.3, s32[1,2048]{1,0:T(1,128)} %list_ref.3, bf16[1024,256]{1,0:T(8,128)(2,1)} %get-tuple-element.34.table_ref), custom_call_target="tpu_custom_call" | custom-call | flops 1073741824 | bytes 4194304 | tf_op jit(solution)/shard_map/send_rows/pallas_call | solution.py:454
  72.7 2.0 %all-to-all-done.1 = f32[8,2,256]{2,1,0:T(2,128)S(1)} async-done(((f32[8,2,256]{2,1,0:T(2,128)}), f32[8,2,256]{2,1,0:T(2,128)S(1)}, u32[]{:S(2)}, u32[]{:S(2)}) %all-to-all-start.1) | async-done | bytes 16416 | tf_op jit(solution)/shard_map/all_to_all | solution.py:589
  74.6 10.3 %all-to-all-start.2 = ((bf16[256,8,256]{2,1,0:T(8,128)(2,1)}), bf16[256,8,256]{2,1,0:T(8,128)(2,1)}, u32[]{:S(2)}, u32[]{:S(2)}) async-start(bf16[256,8,256]{2,1,0:T(8,128)(2,1)} %bitcast.13), calls=%async_computation.2 | async-start | bytes 2097152 | tf_op jit(solution)/shard_map/all_to_all | solution.py:576
  84.9 2.5 %collective-permute-start = (f32[2,256]{1,0:T(2,128)S(1)}, f32[2,256]{1,0:T(2,128)S(1)}, u32[]{:S(2)}, u32[]{:S(2)}) collective-permute-start(f32[2,256]{1,0:T(2,128)S(1)} %reduce_sum.18), channel_id=1, source_target_pairs={{0,1},{1,0},{2,3},{3,2},{4,5},{5,4},{6,7},{7,6},{8,9},{9,8},{10,11... | collective-permute-start | bytes 6152 | tf_op jit(solution)/shard_map/ppermute | solution.py:583
  87.4 0.8 collective-permute-done
  88.2 0.0 collective-permute-start.1
  88.2 1.9 %collective-permute-start.2 = (f32[2,256]{1,0:T(2,128)S(1)}, f32[2,256]{1,0:T(2,128)S(1)}, u32[]{:S(2)}, u32[]{:S(2)}) collective-permute-start(f32[2,256]{1,0:T(2,128)S(1)} %add.44), channel_id=1, source_target_pairs={{0,4},{2,6},{4,0},{6,2},{1,5},{3,7},{5,1},{7,3},{8,12},{10,14},{12... | collective-permute-start | bytes 6152 | tf_op jit(solution)/shard_map/ppermute | solution.py:583
  90.1 1.2 collective-permute-start.3
  91.3 1.2 collective-permute-done.1
  92.5 0.1 collective-permute-done.2
  92.6 0.4 collective-permute-done.3
  93.0 1.2 collective-permute-start.4
  94.2 2.5 %collective-permute-start.5 = (f32[2,256]{1,0:T(2,128)S(1)}, f32[2,256]{1,0:T(2,128)S(1)}, u32[]{:S(2)}, u32[]{:S(2)}) collective-permute-start(f32[2,256]{1,0:T(2,128)S(1)} %add_add_fusion.1), channel_id=1, source_target_pairs={{0,128},{64,192},{128,0},{192,64},{1,129},{65,193},{129,1},{193,65... | collective-permute-start | bytes 6152 | tf_op jit(solution)/shard_map/ppermute | solution.py:583
  96.7 1.1 collective-permute-start.6
  97.9 0.0 collective-permute-done.4
  97.9 0.7 collective-permute-done.5
  98.6 1.0 collective-permute-done.6
  99.6 0.6 add_add_fusion.refs_1_.refs_12_
  100.1 10.5 %own_part.3 = (bf16[1024,256]{1,0:T(8,128)(2,1)}, f32[1024,256]{1,0:T(8,128)}, bf16[2048,256]{1,0:T(8,128)(2,1)}, f32[8,2048]{1,0:T(8,128)}) custom-call(f32[1024,256]{1,0:T(8,128)} %get-tuple-element.37.refs_0_, f32[2,256]{1,0:T(2,128)} %add_add_fusion.refs_1_.refs_12_, bf16[2,256]{1,0:T(2,128)(2,1)} %refs_13_.1, bf16[2,256]{1,0:T(2,128)(2,1)} %refs_14_.1, ...), custom_call_target="tpu_custom_call" | custom-call | flops 3221225472 | bytes 4194304 | tf_op jit(solution)/shard_map/own_part/pallas_call | solution.py:454
  110.7 4.5 %all-to-all-done.2 = bf16[256,8,256]{2,1,0:T(8,128)(2,1)} async-done(((bf16[256,8,256]{2,1,0:T(8,128)(2,1)}), bf16[256,8,256]{2,1,0:T(8,128)(2,1)}, u32[]{:S(2)}, u32[]{:S(2)}) %all-to-all-start.2) | async-done | bytes 1048608 | tf_op jit(solution)/shard_map/all_to_all | solution.py:576
  115.1 12.2 %edge_part.3 = (f32[1024,256]{1,0:T(8,128)}, f32[2,256]{1,0:T(2,128)}) custom-call(bf16[2048,256]{1,0:T(8,128)(2,1)} %bitcast.6.refs_0_, bf16[1024,256]{1,0:T(8,128)(2,1)} %get-tuple-element.39.refs_1_, bf16[2048,256]{1,0:T(8,128)(2,1)} %get-tuple-element.40.refs_2_, f32[1024,8]{1,0:T(8,128)} %get-tuple-element.29.refs_3_, ...), custom_call_target="tpu_custom_call" | custom-call | flops 5368709120 | bytes 4194304 | tf_op jit(solution)/shard_map/edge_part/pallas_call | solution.py:454
  127.3 0.0 copy-start
  127.3 0.8 broadcast_select_fusion.2
  128.1 0.6 collective-permute-start.7
  128.7 0.8 collective-permute-done.7
  129.5 0.0 copy-done
  129.5 0.7 broadcast_in_dim.15
  130.2 0.0 copy-start.1
  130.2 11.8 %all-to-all-start.3 = ((f32[128,2,128]{2,1,0:T(2,128)}), f32[128,2,128]{2,1,0:T(2,128)S(1)}, u32[]{:S(2)}, u32[]{:S(2)}) async-start(f32[128,2,128]{2,1,0:T(2,128)} %broadcast_in_dim.15), calls=%async_computation.3 | async-start | bytes 262144 | tf_op jit(solution)/shard_map/all_to_all | solution.py:589
  142.0 0.0 copy-done.1
  142.0 10.9 %all-to-all-done.3 = f32[128,2,128]{2,1,0:T(2,128)S(1)} async-done(((f32[128,2,128]{2,1,0:T(2,128)}), f32[128,2,128]{2,1,0:T(2,128)S(1)}, u32[]{:S(2)}, u32[]{:S(2)}) %all-to-all-start.3) | async-done | bytes 131104 | tf_op jit(solution)/shard_map/all_to_all | solution.py:589
  153.0 0.1 reduce_sum.19
  153.1 0.0 copy-start.2
  153.1 2.2 %collective-permute-start.8 = (f32[1,256]{1,0:T(1,128)S(1)}, f32[1,256]{1,0:T(1,128)S(1)}, u32[]{:S(2)}, u32[]{:S(2)}) collective-permute-start(f32[1,256]{1,0:T(1,128)S(1)} %bitcast.17), channel_id=1, source_target_pairs={{0,1},{1,0},{2,3},{3,2},{4,5},{5,4},{6,7},{7,6},{8,9},{9,8},{10,11... | collective-permute-start | bytes 3080 | tf_op jit(solution)/shard_map/ppermute | solution.py:583
  155.3 0.0 copy-done.2
  155.3 0.8 collective-permute-done.8
  156.1 2.4 %fusion = bf16[1024,256]{1,0:T(8,128)(2,1)} fusion(f32[1024,256]{1,0:T(8,128)} %get-tuple-element.43, f32[256]{0:T(256)S(1)} %bitcast.16, f32[256]{0:T(256)S(1)} %bitcast.15, f32[256]{0:T(256)S(1)} %bitcast.20, f32[256]{0:T(256)S(1)} %bitcast.19), kind=kLoop, calls=%fused_computation.1 | loop fusion | flops 2359296 | bytes 1576960 | tf_op jit(solution)/shard_map/convert_element_type | solution.py:86
  (7 shorter events, 0.1 us)
Async XLA Ops:
  4.6 46.9 %all-to-all-start = ((bf16[256,8,256]{2,1,0:T(8,128)(2,1)}), bf16[256,8,256]{2,1,0:T(8,128)(2,1)}, u32[]{:S(2)}, u32[]{:S(2)}) async-start(bf16[256,8,256]{2,1,0:T(8,128)(2,1)} %bitcast.14), calls=%async_computation | async-start | bytes 2097152 | tf_op jit(solution)/shard_map/all_to_all | solution.py:576
  64.7 9.9 %all-to-all-start.1 = ((f32[8,2,256]{2,1,0:T(2,128)}), f32[8,2,256]{2,1,0:T(2,128)S(1)}, u32[]{:S(2)}, u32[]{:S(2)}) async-start(f32[8,2,256]{2,1,0:T(2,128)} %broadcast_in_dim.6), calls=%async_computation.1 | async-start | bytes 32768 | tf_op jit(solution)/shard_map/all_to_all | solution.py:589
  74.6 40.5 %all-to-all-start.2 = ((bf16[256,8,256]{2,1,0:T(8,128)(2,1)}), bf16[256,8,256]{2,1,0:T(8,128)(2,1)}, u32[]{:S(2)}, u32[]{:S(2)}) async-start(bf16[256,8,256]{2,1,0:T(8,128)(2,1)} %bitcast.13), calls=%async_computation.2 | async-start | bytes 2097152 | tf_op jit(solution)/shard_map/all_to_all | solution.py:576
  84.9 3.3 %collective-permute-start = (f32[2,256]{1,0:T(2,128)S(1)}, f32[2,256]{1,0:T(2,128)S(1)}, u32[]{:S(2)}, u32[]{:S(2)}) collective-permute-start(f32[2,256]{1,0:T(2,128)S(1)} %reduce_sum.18), channel_id=1, source_target_pairs={{0,1},{1,0},{2,3},{3,2},{4,5},{5,4},{6,7},{7,6},{8,9},{9,8},{10,11... | collective-permute-start | bytes 6152 | tf_op jit(solution)/shard_map/ppermute | solution.py:583
  88.2 4.3 %collective-permute-start.1 = (f32[2,256]{1,0:T(2,128)S(1)}, f32[2,256]{1,0:T(2,128)S(1)}, u32[]{:S(2)}, u32[]{:S(2)}) collective-permute-start(f32[2,256]{1,0:T(2,128)S(1)} %add.44), channel_id=1, source_target_pairs={{0,2},{2,4},{4,6},{6,0},{1,3},{3,5},{5,7},{7,1},{8,10},{10,12},{12... | collective-permute-start | bytes 6152 | tf_op jit(solution)/shard_map/ppermute | solution.py:583
  88.2 4.4 %collective-permute-start.2 = (f32[2,256]{1,0:T(2,128)S(1)}, f32[2,256]{1,0:T(2,128)S(1)}, u32[]{:S(2)}, u32[]{:S(2)}) collective-permute-start(f32[2,256]{1,0:T(2,128)S(1)} %add.44), channel_id=1, source_target_pairs={{0,4},{2,6},{4,0},{6,2},{1,5},{3,7},{5,1},{7,3},{8,12},{10,14},{12... | collective-permute-start | bytes 6152 | tf_op jit(solution)/shard_map/ppermute | solution.py:583
  90.1 2.9 %collective-permute-start.3 = (f32[2,256]{1,0:T(2,128)S(1)}, f32[2,256]{1,0:T(2,128)S(1)}, u32[]{:S(2)}, u32[]{:S(2)}) collective-permute-start(f32[2,256]{1,0:T(2,128)S(1)} %add.44), channel_id=1, source_target_pairs={{0,6},{2,0},{4,2},{6,4},{1,7},{3,1},{5,3},{7,5},{8,14},{10,8},{12,... | collective-permute-start | bytes 6152 | tf_op jit(solution)/shard_map/ppermute | solution.py:583
  93.0 4.9 %collective-permute-start.4 = (f32[2,256]{1,0:T(2,128)S(1)}, f32[2,256]{1,0:T(2,128)S(1)}, u32[]{:S(2)}, u32[]{:S(2)}) collective-permute-start(f32[2,256]{1,0:T(2,128)S(1)} %add_add_fusion.1), channel_id=1, source_target_pairs={{0,64},{64,128},{128,192},{192,0},{1,65},{65,129},{129,193},{193,1... | collective-permute-start | bytes 6152 | tf_op jit(solution)/shard_map/ppermute | solution.py:583
  94.2 4.4 %collective-permute-start.5 = (f32[2,256]{1,0:T(2,128)S(1)}, f32[2,256]{1,0:T(2,128)S(1)}, u32[]{:S(2)}, u32[]{:S(2)}) collective-permute-start(f32[2,256]{1,0:T(2,128)S(1)} %add_add_fusion.1), channel_id=1, source_target_pairs={{0,128},{64,192},{128,0},{192,64},{1,129},{65,193},{129,1},{193,65... | collective-permute-start | bytes 6152 | tf_op jit(solution)/shard_map/ppermute | solution.py:583
  96.7 2.8 %collective-permute-start.6 = (f32[2,256]{1,0:T(2,128)S(1)}, f32[2,256]{1,0:T(2,128)S(1)}, u32[]{:S(2)}, u32[]{:S(2)}) collective-permute-start(f32[2,256]{1,0:T(2,128)S(1)} %add_add_fusion.1), channel_id=1, source_target_pairs={{0,192},{64,0},{128,64},{192,128},{1,193},{65,1},{129,65},{193,129... | collective-permute-start | bytes 6152 | tf_op jit(solution)/shard_map/ppermute | solution.py:583
  127.3 2.2 %copy-start = (f32[2,256]{1,0:T(2,128)S(1)}, f32[2,256]{1,0:T(2,128)}, u32[]{:S(2)}) copy-start(f32[2,256]{1,0:T(2,128)} %get-tuple-element.44) | copy-start | bytes 6148
  128.1 1.4 collective-permute-start.7
  130.2 11.8 %copy-start.1 = (bf16[2,256]{1,0:T(2,128)(2,1)S(1)}, bf16[2,256]{1,0:T(2,128)(2,1)}, u32[]{:S(2)}) copy-start(bf16[2,256]{1,0:T(2,128)(2,1)} %refs_13_.1) | copy-start | bytes 3076
  130.2 22.8 %all-to-all-start.3 = ((f32[128,2,128]{2,1,0:T(2,128)}), f32[128,2,128]{2,1,0:T(2,128)S(1)}, u32[]{:S(2)}, u32[]{:S(2)}) async-start(f32[128,2,128]{2,1,0:T(2,128)} %broadcast_in_dim.15), calls=%async_computation.3 | async-start | bytes 262144 | tf_op jit(solution)/shard_map/all_to_all | solution.py:589
  153.1 2.2 %copy-start.2 = (bf16[2,256]{1,0:T(2,128)(2,1)S(1)}, bf16[2,256]{1,0:T(2,128)(2,1)}, u32[]{:S(2)}) copy-start(bf16[2,256]{1,0:T(2,128)(2,1)} %refs_14_.1) | copy-start | bytes 3076
  153.1 3.0 %collective-permute-start.8 = (f32[1,256]{1,0:T(1,128)S(1)}, f32[1,256]{1,0:T(1,128)S(1)}, u32[]{:S(2)}, u32[]{:S(2)}) collective-permute-start(f32[1,256]{1,0:T(1,128)S(1)} %bitcast.17), channel_id=1, source_target_pairs={{0,1},{1,0},{2,3},{3,2},{4,5},{5,4},{6,7},{7,6},{8,9},{9,8},{10,11... | collective-permute-start | bytes 3080 | tf_op jit(solution)/shard_map/ppermute | solution.py:583

commit v5 on v4

--- a/solution.py
+++ b/solution.py
@@ -19,6 +19,7 @@
 EDGE_CHUNKS = EDGES_OWN // CHUNK
 NODE_CHUNKS = NODES_OWN // CHUNK
 WINDOW = 160
+COPIES = 8
 TABLE_ROWS = NODES_OWN + ROWS_IN
 F32 = jnp.float32
 BF16 = jnp.bfloat16
@@ -308,24 +309,26 @@
 def edge_kernel(layer, total_nodes, with_norm, with_send, *refs):
     refs = list(refs)
     recv_any, left_any, dst_any, noedge_any, base_any = refs[:5]
-    wl_ref, attn_ref, self_ref, rows_ref, srcs_ref, bias_ref, bound_ref = refs[5:12]
-    refs = refs[12:]
-    if with_norm:
-        stats_in, gain_ref, shift_ref = refs[:3]
-        refs = refs[3:]
-    summed_hbm, stats_ref = refs[:2]
+    small = 10 if with_norm else 7
+    small_any = refs[5 : 5 + small]
+    refs = refs[5 + small :]
+    summed_hbm, stats_hbm = refs[:2]
     refs = refs[2:]
     if with_send:
-        round_ref = refs.pop(0)
-    summed_ref, out_sems = refs.pop(), refs.pop()
+        round_hbm = refs.pop(0)
     recv_ref, left_ref, dst_ref, noedge_ref, base_ref, sems = refs[:6]
     table_ref, even_ref, odd_ref, edge_ref, score_ref, scan_ref, mix_ref, acc_ref = refs[6:14]
+    out_sems, summed_ref, stats_ref, round_ref = refs[14:18]
+    small_refs = refs[18:]
+    wl_ref, attn_ref, self_ref, rows_ref, srcs_ref, bias_ref, bound_ref = small_refs[:7]
     piece = ROWS_IN // 4
-    moves = [
-        (recv_any.at[k * piece : (k + 1) * piece], recv_ref.at[k * piece : (k + 1) * piece])
-        for k in range(4)
-    ]
-    moves += [(left_any, left_ref), (dst_any, dst_ref)]
+    pieces = [slice(k * piece, (k + 1) * piece) for k in range(4)]
+    moves = [(small_any[0].at[layer], wl_ref), (recv_any.at[pieces[0]], recv_ref.at[pieces[0]])]
+    moves += list(zip(small_any[7:], small_refs[7:]))
+    moves += [(recv_any.at[at], recv_ref.at[at]) for at in pieces[1:]]
+    moves += [(small_any[4], srcs_ref), (left_any, left_ref), (small_any[1], attn_ref)]
+    moves += [(dst_any, dst_ref), (small_any[3], rows_ref), (small_any[6], bound_ref)]
+    moves += [(small_any[2], self_ref), (small_any[5], bias_ref)]
     moves += [(noedge_any, noedge_ref), (base_any, base_ref)]
     copies = [
         pltpu.make_async_copy(source, target, sems.at[i])
@@ -333,23 +336,33 @@
     ]
     for copy in copies:
         copy.start()
+    waiting = iter(copies)
+
+    def settle(count):
+        for _ in range(count):
+            next(waiting).wait()
+
     if with_norm:
+        stats_in, gain_ref, shift_ref = small_refs[7:]
+        settle(5)
         terms = norm_terms(
             stats_in[...],
             total_nodes,
             gain_ref[layer - 1 : layer, :].astype(F32),
             shift_ref[layer - 1 : layer, :].astype(F32),
         )
-    heads = head_rows(attn_ref, layer)
+    else:
+        settle(2)
     for c in range(ROWS_IN // CHUNK):
-        if c * CHUNK % piece == 0:
-            copies[c * CHUNK // piece].wait()
+        if c and c * CHUNK % piece == 0:
+            settle(1)
         states = recv_ref[c * CHUNK : (c + 1) * CHUNK, :]
         if with_norm:
             states = normalize(states.astype(F32), terms)
-        left = dot(states, wl_ref[layer]).astype(BF16).astype(F32)
+        left = dot(states, wl_ref[...]).astype(BF16).astype(F32)
         put_rows(table_ref, NODES_OWN + c * CHUNK, left)
-    copies[4].wait()
+    settle(3)
+    heads = head_rows(attn_ref, layer)
     for k in range(NODE_CHUNKS):
         put_rows(table_ref, k * CHUNK, left_ref[k * CHUNK : (k + 1) * CHUNK, :].astype(F32))
 
@@ -363,7 +376,7 @@
         score_ref[:, at] = scores_of(heads, leaky(src + dst_ref[at, :].astype(F32)))
 
     fetch(0, even_ref)
-    copies[5].wait()
+    settle(1)
 
     def pair(c, carry):
         fetch(2 * c + 1, odd_ref)
@@ -374,6 +387,7 @@
 
     lax.fori_loop(0, EDGE_CHUNKS // 2, pair, 0)
 
+    settle(4)
     tgt = rows_ref[0:1, :]
     start = rows_ref[1:2, :]
     end = rows_ref[2:3, :]
@@ -418,9 +432,8 @@
         return lax.fori_loop(0, count, window, carry)
 
     lax.fori_loop(0, EDGE_CHUNKS, gather_in, 0)
-    copies[6].wait()
-    copies[7].wait()
-    stats_ref[...] = jnp.zeros_like(stats_ref)
+    settle(2)
+    totals = jnp.zeros((2, FEAT), F32)
     stores = []
     for k in range(NODE_CHUNKS):
         at = slice(k * CHUNK, (k + 1) * CHUNK)
@@ -428,13 +441,21 @@
         message = acc_ref[at, :FEAT] + own_alpha * left_ref[at, :].astype(F32)
         summed = base_ref[at, :] + message
         summed_ref[at, :] = summed
-        stats_ref[0:1, :] += jnp.sum(summed, axis=0, keepdims=True)
-        stats_ref[1:2, :] += jnp.sum(summed * summed, axis=0, keepdims=True)
+        sums = [jnp.sum(summed, axis=0, keepdims=True)]
+        sums += [jnp.sum(summed * summed, axis=0, keepdims=True)]
+        totals += jnp.concatenate(sums, axis=0)
         if with_send:
             round_ref[at, :] = summed.astype(BF16)
         store = pltpu.make_async_copy(summed_ref.at[at], summed_hbm.at[at], out_sems.at[k])
         store.start()
         stores.append(store)
+    for k in range(COPIES):
+        stats_ref[k] = totals
+    stores.append(pltpu.make_async_copy(stats_ref, stats_hbm, out_sems.at[NODE_CHUNKS]))
+    stores[-1].start()
+    if with_send:
+        stores.append(pltpu.make_async_copy(round_ref, round_hbm, out_sems.at[NODE_CHUNKS + 1]))
+        stores[-1].start()
     for store in stores:
         store.wait()
 
@@ -536,7 +557,12 @@
 
 
 def edge_part(layer, total_nodes, with_send, args):
-    outs = [shaped(NODES_OWN, FEAT, F32), shaped(2, FEAT, F32)]
+    outs = [
+        shaped(NODES_OWN, FEAT, F32),
+        jax.ShapeDtypeStruct((COPIES, 2, FEAT), F32),
+    ]
+    if with_send:
+        outs.append(shaped(NODES_OWN, FEAT, BF16))
     half = FEAT // 2
     scratch = [
         pltpu.VMEM((ROWS_IN, FEAT), BF16),
@@ -544,7 +570,7 @@
         pltpu.VMEM((EDGES_OWN, FEAT), BF16),
         pltpu.VMEM((NODES_OWN, 8), F32),
         pltpu.VMEM((NODES_OWN, FEAT), F32),
-        pltpu.SemaphoreType.DMA((8,)),
+        pltpu.SemaphoreType.DMA((len(args) + 3,)),
         pltpu.VMEM((2 * TABLE_ROWS, half), F32),
         pltpu.VMEM((2 * CHUNK, half), F32),
         pltpu.VMEM((2 * CHUNK, half), F32),
@@ -553,13 +579,21 @@
         pltpu.VMEM((2, 8, EDGES_OWN), F32),
         pltpu.VMEM((EDGES_OWN, 2 * FEAT), BF16),
         pltpu.VMEM((NODES_OWN + WINDOW, 2 * FEAT), F32),
+        pltpu.SemaphoreType.DMA((NODE_CHUNKS + 2,)),
+        pltpu.VMEM((NODES_OWN, FEAT), F32),
+        pltpu.VMEM((COPIES, 2, FEAT), F32),
+        pltpu.VMEM((NODES_OWN, FEAT), BF16),
+        pltpu.VMEM((FEAT, FEAT), BF16),
+        pltpu.VMEM((LAYERS, FEAT), BF16),
+        pltpu.VMEM((8, EDGES_OWN), F32),
+        pltpu.VMEM((8, EDGES_OWN), jnp.int32),
+        pltpu.SMEM((1, EDGES_OWN), jnp.int32),
+        pltpu.VMEM((8, EDGES_OWN), F32),
+        pltpu.SMEM((1, 32), jnp.int32),
     ]
-    if with_send:
-        outs.append(shaped(NODES_OWN, FEAT, BF16))
-    scratch += [pltpu.SemaphoreType.DMA((NODE_CHUNKS,)), pltpu.VMEM((NODES_OWN, FEAT), F32)]
-    in_specs = [ANY] + [HBM] * 4 + [VMEM] * (len(args) - 5)
-    in_specs[9] = SMEM
-    in_specs[11] = SMEM
+    if layer > 0:
+        scratch += [pltpu.VMEM((2, FEAT), F32)]
+        scratch += [pltpu.VMEM((LAYERS, FEAT), BF16)] * 2
     return call(
         functools.partial(edge_kernel, layer, total_nodes, layer > 0, with_send),
         "edge_part",
@@ -567,8 +601,8 @@
         scratch,
         5 * GIGA,
         args,
-        in_specs=in_specs,
-        out_specs=[HBM] + [VMEM] * (len(outs) - 1),
+        in_specs=[HBM] * len(args),
+        out_specs=[HBM] * len(outs),
     )
 
 
@@ -583,14 +617,12 @@
     return lax.ppermute(value, axis, [(i, (i + amount) % size) for i in range(size)])
 
 
-def copies_summed(stats, axes):
-    size = lax.axis_size(axes)
-    copies = jnp.broadcast_to(stats[None], (size,) + stats.shape)
+def copies_summed(copies, axes):
     return jnp.sum(lax.all_to_all(copies, axes, 0, 0, tiled=True), axis=0)
 
 
-def total_along(stats):
-    return copies_summed(stats, ("blk_0",))
+def total_along(copies):
+    return copies_summed(copies, ("blk_0",))
 
 
 def total_inside(stats):
@@ -602,14 +634,11 @@
     return stats
 
 
-def total_alone(stats):
-    first = lax.axis_index("blk_2") == 0
-    mine = jnp.where(first, stats[0:1], stats[1:2])
-    other = jnp.where(first, stats[1:2], stats[0:1])
-    mine = (mine + shifted(other, "blk_2", 1)).reshape(2, FEAT // 2)
-    mine = copies_summed(mine, ("grp", "blk_0", "blk_1")).reshape(1, FEAT)
-    other = shifted(mine, "blk_2", 1)
-    return jnp.concatenate([jnp.where(first, mine, other), jnp.where(first, other, mine)])
+def total_alone(copies):
+    stats = copies_summed(copies, ("blk_1", "blk_2"))
+    axes = ("grp", "blk_0")
+    copies = jnp.broadcast_to(stats[None], (lax.axis_size(axes),) + stats.shape)
+    return copies_summed(copies, axes)
 
 
 def local(

time: 159 us -> 153 us (0.962)
  Pallas kernels: 63.6 us -> 60.4 us
  starting transfers between devices: 55.3 us -> 52.1 us
  waiting for transfers between devices: 33.6 us -> 36.1 us
    pallas_call x7, Pallas kernels: 63.6 us -> 60.4 us  [call(): pl.pallas_call(body, name=name, out_shape=outs, in_specs=in_specs or [VME...]
    ppermute x9 -> x7, starting transfers between devices: 13.2 us -> 10.4 us  [shifted(): lax.ppermute(value, axis, [(i, (i + amount) % size) for i in range(size)])]
    all_to_all x2 -> x3, waiting for transfers between devices: 12.9 us -> 15.4 us  [copies_summed(): return jnp.sum(lax.all_to_all(copies, axes, 0, 0, tiled=True), axis=0)]
    ppermute x9 -> x7, waiting for transfers between devices: 5.82 us -> 4.19 us  [shifted(): lax.ppermute(value, axis, [(i, (i + amount) % size) for i in range(size)])]
    all_to_all x2 -> x3, starting transfers between devices: 15.1 us -> 15.4 us  [copies_summed(): return jnp.sum(lax.all_to_all(copies, axes, 0, 0, tiled=True), axis=0)]
  transfers between devices with their start and end apart: 13 -> 12, of which waited for: 12 -> 11; matrix products, arithmetic and copies ran while one was open for 0% -> 0% of each run, Pallas kernels for 22% -> 22%
where the time goes in v5:
time: 153 us; the launch traced here: 152 us
  Pallas kernels  60.4 us (39%)
  starting transfers between devices  52.1 us (34%)
  waiting for transfers between devices  36.1 us (24%)
  other arithmetic  3.1 us (2%)
    pallas_call x7, Pallas kernels, call(): pl.pallas_call(body, name=name, out_shape=outs, in_specs=in_specs or [VME...  60.4 us
    all_to_all x2, starting transfers between devices, deliver(): lax.all_to_all(rows.reshape(-1, 8, rows.shape[1]), GRP_BLK, split_axis=0,...  26.2 us
    all_to_all x2, waiting for transfers between devices, deliver(): lax.all_to_all(rows.reshape(-1, 8, rows.shape[1]), GRP_BLK, split_axis=0,...  16.5 us
    all_to_all x3, starting transfers between devices, copies_summed(): return jnp.sum(lax.all_to_all(copies, axes, 0, 0, tiled=True), axis=0)  15.4 us
    all_to_all x3, waiting for transfers between devices, copies_summed(): return jnp.sum(lax.all_to_all(copies, axes, 0, 0, tiled=True), axis=0)  15.4 us
    ppermute x7, starting transfers between devices, shifted(): lax.ppermute(value, axis, [(i, (i + amount) % size) for i in range(size)])  10.4 us
    ppermute x7, waiting for transfers between devices, shifted(): lax.ppermute(value, axis, [(i, (i + amount) % size) for i in range(size)])  4.19 us
  transfers between devices with their start and end apart: 12, of which 11 were waited for; matrix products, arithmetic and copies ran while one was open for 0% of the time, Pallas kernels for 22%

profile of v5, /device:TPU:1, one launch (start us, length us, event | category | flops | bytes accessed | tf_op | source)
XLA Modules:
  0.0 152.5 jit_solution(17374664942820155835)
XLA Ops:
  0.0 4.6 %send_rows.2 = bf16[2048,256]{1,0:T(8,128)(2,1)} custom-call(s32[1,2048]{1,0:T(1,128)} %list_ref.3, s32[1,2048]{1,0:T(1,128)} %list_ref.3, bf16[1024,256]{1,0:T(8,128)(2,1)} %refs_0_.1), custom_call_target="tpu_custom_call" | custom-call | flops 1073741824 | bytes 4194304 | tf_op jit(solution)/shard_map/send_rows/pallas_call | solution.py:475
  4.6 16.7 %all-to-all-start = ((bf16[256,8,256]{2,1,0:T(8,128)(2,1)}), bf16[256,8,256]{2,1,0:T(8,128)(2,1)}, u32[]{:S(2)}, u32[]{:S(2)}) async-start(bf16[256,8,256]{2,1,0:T(8,128)(2,1)} %bitcast.12), calls=%async_computation | async-start | bytes 2097152 | tf_op jit(solution)/shard_map/all_to_all | solution.py:610
  21.3 9.4 %sort_edges.1 = (s32[8,2048]{1,0:T(8,128)}, s32[1,2048]{1,0:T(1,128)}, f32[8,2048]{1,0:T(8,128)}, f32[1024,8]{1,0:T(8,128)}, s32[1,32]{1,0:T(1,128)}) custom-call(s32[1,2048]{1,0:T(1,128)} %bitcast.17, s32[1,2048]{1,0:T(1,128)} %bitcast.18, s32[1,2048]{1,0:T(1,128)} %bitcast.19, f32[8,2048]{1,0:T(8,128)} %bias_ref.1), custom_call_target="tpu_custom_call" | custom-call | flops 2147483648 | bytes 4194304 | tf_op jit(solution)/shard_map/sort_edges/pallas_call | solution.py:475
  30.6 9.6 %own_part.2 = (bf16[1024,256]{1,0:T(8,128)(2,1)}, f32[1024,256]{1,0:T(8,128)}, bf16[2048,256]{1,0:T(8,128)(2,1)}, f32[8,2048]{1,0:T(8,128)}) custom-call(bf16[1024,256]{1,0:T(8,128)(2,1)} %refs_0_.1, bf16[2,256,256]{2,1,0:T(8,128)(2,1)} %refs_5_.5, bf16[2,256,256]{2,1,0:T(8,128)(2,1)} %refs_5_.4, bf16[2,256,256]{2,1,0:T(8,128)(2,1)} %refs_6_.4, ...), custom_call_target="tpu_custom_call" | custom-call | flops 3221225472 | bytes 4194304 | tf_op jit(solution)/shard_map/own_part/pallas_call | solution.py:475
  40.2 11.2 %all-to-all-done = bf16[256,8,256]{2,1,0:T(8,128)(2,1)} async-done(((bf16[256,8,256]{2,1,0:T(8,128)(2,1)}), bf16[256,8,256]{2,1,0:T(8,128)(2,1)}, u32[]{:S(2)}, u32[]{:S(2)}) %all-to-all-start) | async-done | bytes 1048608 | tf_op jit(solution)/shard_map/all_to_all | solution.py:610
  51.5 11.2 %edge_part.2 = (f32[1024,256]{1,0:T(8,128)}, f32[8,2,256]{2,1,0:T(2,128)}, bf16[1024,256]{1,0:T(8,128)(2,1)}) custom-call(bf16[2048,256]{1,0:T(8,128)(2,1)} %bitcast.1.refs_0_, bf16[1024,256]{1,0:T(8,128)(2,1)} %get-tuple-element.27.refs_1_, bf16[2048,256]{1,0:T(8,128)(2,1)} %get-tuple-element.28.refs_2_, f32[1024,8]{1,0:T(8,128)} %get-tuple-element.29.refs_3_, ...), custom_call_target="tpu_custom_call" | custom-call | flops 5368709120 | bytes 4194304 | tf_op jit(solution)/shard_map/edge_part/pallas_call | solution.py:475
  62.6 3.3 %all-to-all-start.1 = ((f32[8,2,256]{2,1,0:T(2,128)}), f32[8,2,256]{2,1,0:T(2,128)S(1)}, u32[]{:S(2)}, u32[]{:S(2)}) async-start(f32[8,2,256]{2,1,0:T(2,128)} %get-tuple-element.35), calls=%async_computation.1 | async-start | bytes 32768 | tf_op jit(solution)/shard_map/all_to_all | solution.py:621
  66.0 4.6 %send_rows.3 = bf16[2048,256]{1,0:T(8,128)(2,1)} custom-call(s32[1,2048]{1,0:T(1,128)} %list_ref.3, s32[1,2048]{1,0:T(1,128)} %list_ref.3, bf16[1024,256]{1,0:T(8,128)(2,1)} %get-tuple-element.34.table_ref), custom_call_target="tpu_custom_call" | custom-call | flops 1073741824 | bytes 4194304 | tf_op jit(solution)/shard_map/send_rows/pallas_call | solution.py:475
  70.6 1.9 %all-to-all-done.1 = f32[8,2,256]{2,1,0:T(2,128)S(1)} async-done(((f32[8,2,256]{2,1,0:T(2,128)}), f32[8,2,256]{2,1,0:T(2,128)S(1)}, u32[]{:S(2)}, u32[]{:S(2)}) %all-to-all-start.1) | async-done | bytes 16416 | tf_op jit(solution)/shard_map/all_to_all | solution.py:621
  72.6 9.6 %all-to-all-start.2 = ((bf16[256,8,256]{2,1,0:T(8,128)(2,1)}), bf16[256,8,256]{2,1,0:T(8,128)(2,1)}, u32[]{:S(2)}, u32[]{:S(2)}) async-start(bf16[256,8,256]{2,1,0:T(8,128)(2,1)} %bitcast.11), calls=%async_computation.2 | async-start | bytes 2097152 | tf_op jit(solution)/shard_map/all_to_all | solution.py:610
  82.1 2.5 %collective-permute-start = (f32[2,256]{1,0:T(2,128)S(1)}, f32[2,256]{1,0:T(2,128)S(1)}, u32[]{:S(2)}, u32[]{:S(2)}) collective-permute-start(f32[2,256]{1,0:T(2,128)S(1)} %reduce_sum.27), channel_id=1, source_target_pairs={{0,1},{1,0},{2,3},{3,2},{4,5},{5,4},{6,7},{7,6},{8,9},{9,8},{10,11... | collective-permute-start | bytes 6152 | tf_op jit(solution)/shard_map/ppermute | solution.py:617
  84.6 0.8 collective-permute-done
  85.5 0.0 collective-permute-start.1
  85.5 1.9 %collective-permute-start.2 = (f32[2,256]{1,0:T(2,128)S(1)}, f32[2,256]{1,0:T(2,128)S(1)}, u32[]{:S(2)}, u32[]{:S(2)}) collective-permute-start(f32[2,256]{1,0:T(2,128)S(1)} %add.41), channel_id=1, source_target_pairs={{0,4},{2,6},{4,0},{6,2},{1,5},{3,7},{5,1},{7,3},{8,12},{10,14},{12... | collective-permute-start | bytes 6152 | tf_op jit(solution)/shard_map/ppermute | solution.py:617
  87.4 1.2 collective-permute-start.3
  88.6 1.2 collective-permute-done.1
  89.8 0.1 collective-permute-done.2
  89.8 0.4 collective-permute-done.3
  90.2 1.2 collective-permute-start.4
  91.4 2.5 %collective-permute-start.5 = (f32[2,256]{1,0:T(2,128)S(1)}, f32[2,256]{1,0:T(2,128)S(1)}, u32[]{:S(2)}, u32[]{:S(2)}) collective-permute-start(f32[2,256]{1,0:T(2,128)S(1)} %add_add_fusion.1), channel_id=1, source_target_pairs={{0,128},{64,192},{128,0},{192,64},{1,129},{65,193},{129,1},{193,65... | collective-permute-start | bytes 6152 | tf_op jit(solution)/shard_map/ppermute | solution.py:617
  93.9 1.1 collective-permute-start.6
  95.1 0.0 collective-permute-done.4
  95.1 0.7 collective-permute-done.5
  95.8 1.0 collective-permute-done.6
  96.8 0.6 add_add_fusion.refs_1_.refs_12_
  97.4 9.7 %own_part.3 = (bf16[1024,256]{1,0:T(8,128)(2,1)}, f32[1024,256]{1,0:T(8,128)}, bf16[2048,256]{1,0:T(8,128)(2,1)}, f32[8,2048]{1,0:T(8,128)}) custom-call(f32[1024,256]{1,0:T(8,128)} %get-tuple-element.37.refs_0_, f32[2,256]{1,0:T(2,128)} %add_add_fusion.refs_1_.refs_12_, bf16[2,256]{1,0:T(2,128)(2,1)} %refs_13_.1, bf16[2,256]{1,0:T(2,128)(2,1)} %refs_14_.1, ...), custom_call_target="tpu_custom_call" | custom-call | flops 3221225472 | bytes 4194304 | tf_op jit(solution)/shard_map/own_part/pallas_call | solution.py:475
  107.1 5.3 %all-to-all-done.2 = bf16[256,8,256]{2,1,0:T(8,128)(2,1)} async-done(((bf16[256,8,256]{2,1,0:T(8,128)(2,1)}), bf16[256,8,256]{2,1,0:T(8,128)(2,1)}, u32[]{:S(2)}, u32[]{:S(2)}) %all-to-all-start.2) | async-done | bytes 1048608 | tf_op jit(solution)/shard_map/all_to_all | solution.py:610
  112.4 11.4 %edge_part.3 = (f32[1024,256]{1,0:T(8,128)}, f32[8,2,256]{2,1,0:T(2,128)}) custom-call(bf16[2048,256]{1,0:T(8,128)(2,1)} %bitcast.6.refs_0_, bf16[1024,256]{1,0:T(8,128)(2,1)} %get-tuple-element.39.refs_1_, bf16[2048,256]{1,0:T(8,128)(2,1)} %get-tuple-element.40.refs_2_, f32[1024,8]{1,0:T(8,128)} %get-tuple-element.29.refs_3_, ...), custom_call_target="tpu_custom_call" | custom-call | flops 5368709120 | bytes 4194304 | tf_op jit(solution)/shard_map/edge_part/pallas_call | solution.py:475
  123.7 0.0 copy-start
  123.7 4.2 %all-to-all-start.3 = ((f32[8,2,256]{2,1,0:T(2,128)}), f32[8,2,256]{2,1,0:T(2,128)S(1)}, u32[]{:S(2)}, u32[]{:S(2)}) async-start(f32[8,2,256]{2,1,0:T(2,128)} %get-tuple-element.44), calls=%async_computation.3 | async-start | bytes 32768 | tf_op jit(solution)/shard_map/all_to_all | solution.py:621
  127.9 0.0 copy-done
  127.9 4.6 %all-to-all-done.3 = f32[8,2,256]{2,1,0:T(2,128)S(1)} async-done(((f32[8,2,256]{2,1,0:T(2,128)}), f32[8,2,256]{2,1,0:T(2,128)S(1)}, u32[]{:S(2)}, u32[]{:S(2)}) %all-to-all-start.3) | async-done | bytes 16416 | tf_op jit(solution)/shard_map/all_to_all | solution.py:621
  132.6 0.7 broadcast_in_dim.2
  133.2 0.0 copy-start.1
  133.2 7.9 %all-to-all-start.4 = ((f32[32,2,256]{2,1,0:T(2,128)}), f32[32,2,256]{2,1,0:T(2,128)S(1)}, u32[]{:S(2)}, u32[]{:S(2)}) async-start(f32[32,2,256]{2,1,0:T(2,128)} %broadcast_in_dim.2), calls=%async_computation.4 | async-start | bytes 131072 | tf_op jit(solution)/shard_map/all_to_all | solution.py:621
  141.2 0.0 copy-done.1
  141.2 8.8 %all-to-all-done.4 = f32[32,2,256]{2,1,0:T(2,128)S(1)} async-done(((f32[32,2,256]{2,1,0:T(2,128)}), f32[32,2,256]{2,1,0:T(2,128)S(1)}, u32[]{:S(2)}, u32[]{:S(2)}) %all-to-all-start.4) | async-done | bytes 65568 | tf_op jit(solution)/shard_map/all_to_all | solution.py:621
  150.1 2.4 %fusion = bf16[1024,256]{1,0:T(8,128)(2,1)} fusion(f32[1024,256]{1,0:T(8,128)} %get-tuple-element.43, f32[256]{0:T(256)S(1)} %bitcast.13, f32[256]{0:T(256)S(1)} %bitcast.14, f32[256]{0:T(256)S(1)} %bitcast.16, f32[256]{0:T(256)S(1)} %bitcast.15), kind=kLoop, calls=%fused_computation.1 | loop fusion | flops 2359296 | bytes 1576960 | tf_op jit(solution)/shard_map/convert_element_type | solution.py:87
  (8 shorter events, 0.1 us)
Async XLA Ops:
  4.6 46.9 %all-to-all-start = ((bf16[256,8,256]{2,1,0:T(8,128)(2,1)}), bf16[256,8,256]{2,1,0:T(8,128)(2,1)}, u32[]{:S(2)}, u32[]{:S(2)}) async-start(bf16[256,8,256]{2,1,0:T(8,128)(2,1)} %bitcast.12), calls=%async_computation | async-start | bytes 2097152 | tf_op jit(solution)/shard_map/all_to_all | solution.py:610
  62.6 9.9 %all-to-all-start.1 = ((f32[8,2,256]{2,1,0:T(2,128)}), f32[8,2,256]{2,1,0:T(2,128)S(1)}, u32[]{:S(2)}, u32[]{:S(2)}) async-start(f32[8,2,256]{2,1,0:T(2,128)} %get-tuple-element.35), calls=%async_computation.1 | async-start | bytes 32768 | tf_op jit(solution)/shard_map/all_to_all | solution.py:621
  72.6 39.8 %all-to-all-start.2 = ((bf16[256,8,256]{2,1,0:T(8,128)(2,1)}), bf16[256,8,256]{2,1,0:T(8,128)(2,1)}, u32[]{:S(2)}, u32[]{:S(2)}) async-start(bf16[256,8,256]{2,1,0:T(8,128)(2,1)} %bitcast.11), calls=%async_computation.2 | async-start | bytes 2097152 | tf_op jit(solution)/shard_map/all_to_all | solution.py:610
  82.1 3.3 %collective-permute-start = (f32[2,256]{1,0:T(2,128)S(1)}, f32[2,256]{1,0:T(2,128)S(1)}, u32[]{:S(2)}, u32[]{:S(2)}) collective-permute-start(f32[2,256]{1,0:T(2,128)S(1)} %reduce_sum.27), channel_id=1, source_target_pairs={{0,1},{1,0},{2,3},{3,2},{4,5},{5,4},{6,7},{7,6},{8,9},{9,8},{10,11... | collective-permute-start | bytes 6152 | tf_op jit(solution)/shard_map/ppermute | solution.py:617
  85.5 4.3 %collective-permute-start.1 = (f32[2,256]{1,0:T(2,128)S(1)}, f32[2,256]{1,0:T(2,128)S(1)}, u32[]{:S(2)}, u32[]{:S(2)}) collective-permute-start(f32[2,256]{1,0:T(2,128)S(1)} %add.41), channel_id=1, source_target_pairs={{0,2},{2,4},{4,6},{6,0},{1,3},{3,5},{5,7},{7,1},{8,10},{10,12},{12... | collective-permute-start | bytes 6152 | tf_op jit(solution)/shard_map/ppermute | solution.py:617
  85.5 4.4 %collective-permute-start.2 = (f32[2,256]{1,0:T(2,128)S(1)}, f32[2,256]{1,0:T(2,128)S(1)}, u32[]{:S(2)}, u32[]{:S(2)}) collective-permute-start(f32[2,256]{1,0:T(2,128)S(1)} %add.41), channel_id=1, source_target_pairs={{0,4},{2,6},{4,0},{6,2},{1,5},{3,7},{5,1},{7,3},{8,12},{10,14},{12... | collective-permute-start | bytes 6152 | tf_op jit(solution)/shard_map/ppermute | solution.py:617
  87.4 2.9 %collective-permute-start.3 = (f32[2,256]{1,0:T(2,128)S(1)}, f32[2,256]{1,0:T(2,128)S(1)}, u32[]{:S(2)}, u32[]{:S(2)}) collective-permute-start(f32[2,256]{1,0:T(2,128)S(1)} %add.41), channel_id=1, source_target_pairs={{0,6},{2,0},{4,2},{6,4},{1,7},{3,1},{5,3},{7,5},{8,14},{10,8},{12,... | collective-permute-start | bytes 6152 | tf_op jit(solution)/shard_map/ppermute | solution.py:617
  90.2 4.9 %collective-permute-start.4 = (f32[2,256]{1,0:T(2,128)S(1)}, f32[2,256]{1,0:T(2,128)S(1)}, u32[]{:S(2)}, u32[]{:S(2)}) collective-permute-start(f32[2,256]{1,0:T(2,128)S(1)} %add_add_fusion.1), channel_id=1, source_target_pairs={{0,64},{64,128},{128,192},{192,0},{1,65},{65,129},{129,193},{193,1... | collective-permute-start | bytes 6152 | tf_op jit(solution)/shard_map/ppermute | solution.py:617
  91.4 4.4 %collective-permute-start.5 = (f32[2,256]{1,0:T(2,128)S(1)}, f32[2,256]{1,0:T(2,128)S(1)}, u32[]{:S(2)}, u32[]{:S(2)}) collective-permute-start(f32[2,256]{1,0:T(2,128)S(1)} %add_add_fusion.1), channel_id=1, source_target_pairs={{0,128},{64,192},{128,0},{192,64},{1,129},{65,193},{129,1},{193,65... | collective-permute-start | bytes 6152 | tf_op jit(solution)/shard_map/ppermute | solution.py:617
  93.9 2.8 %collective-permute-start.6 = (f32[2,256]{1,0:T(2,128)S(1)}, f32[2,256]{1,0:T(2,128)S(1)}, u32[]{:S(2)}, u32[]{:S(2)}) collective-permute-start(f32[2,256]{1,0:T(2,128)S(1)} %add_add_fusion.1), channel_id=1, source_target_pairs={{0,192},{64,0},{128,64},{192,128},{1,193},{65,1},{129,65},{193,129... | collective-permute-start | bytes 6152 | tf_op jit(solution)/shard_map/ppermute | solution.py:617
  123.7 4.2 %copy-start = (bf16[2,256]{1,0:T(2,128)(2,1)S(1)}, bf16[2,256]{1,0:T(2,128)(2,1)}, u32[]{:S(2)}) copy-start(bf16[2,256]{1,0:T(2,128)(2,1)} %refs_14_.1) | copy-start | bytes 3076
  123.7 8.8 %all-to-all-start.3 = ((f32[8,2,256]{2,1,0:T(2,128)}), f32[8,2,256]{2,1,0:T(2,128)S(1)}, u32[]{:S(2)}, u32[]{:S(2)}) async-start(f32[8,2,256]{2,1,0:T(2,128)} %get-tuple-element.44), calls=%async_computation.3 | async-start | bytes 32768 | tf_op jit(solution)/shard_map/all_to_all | solution.py:621
  133.2 7.9 %copy-start.1 = (bf16[2,256]{1,0:T(2,128)(2,1)S(1)}, bf16[2,256]{1,0:T(2,128)(2,1)}, u32[]{:S(2)}) copy-start(bf16[2,256]{1,0:T(2,128)(2,1)} %refs_13_.1) | copy-start | bytes 3076
  133.2 16.8 %all-to-all-start.4 = ((f32[32,2,256]{2,1,0:T(2,128)}), f32[32,2,256]{2,1,0:T(2,128)S(1)}, u32[]{:S(2)}, u32[]{:S(2)}) async-start(f32[32,2,256]{2,1,0:T(2,128)} %broadcast_in_dim.2), calls=%async_computation.4 | async-start | bytes 131072 | tf_op jit(solution)/shard_map/all_to_all | solution.py:621

commit v6 on v5

--- a/solution.py
+++ b/solution.py
@@ -635,8 +635,9 @@
 
 
 def total_alone(copies):
-    stats = copies_summed(copies, ("blk_1", "blk_2"))
-    axes = ("grp", "blk_0")
+    stats = copies_summed(copies, ("blk_0",))
+    stats = stats + shifted(stats, "blk_2", 1)
+    axes = ("grp", "blk_1")
     copies = jnp.broadcast_to(stats[None], (lax.axis_size(axes),) + stats.shape)
     return copies_summed(copies, axes)
 

time: 153 us -> 155 us (1.013)
  blocking collectives: 0 us -> 9.98 us
  waiting for transfers between devices: 36.1 us -> 29.5 us
    all_to_all x0 -> x1, blocking collectives: none -> 9.98 us  [copies_summed(): return jnp.sum(lax.all_to_all(copies, axes, 0, 0, tiled=True), axis=0)]
    all_to_all x3 -> x2, waiting for transfers between devices: 15.4 us -> 8.46 us  [copies_summed(): return jnp.sum(lax.all_to_all(copies, axes, 0, 0, tiled=True), axis=0)]
    all_to_all x3 -> x2, starting transfers between devices: 15.4 us -> 10.6 us  [copies_summed(): return jnp.sum(lax.all_to_all(copies, axes, 0, 0, tiled=True), axis=0)]
    ppermute x7 -> x8, starting transfers between devices: 10.4 us -> 13.4 us  [shifted(): lax.ppermute(value, axis, [(i, (i + amount) % size) for i in range(size)])]
    ppermute x7 -> x8, waiting for transfers between devices: 4.19 us -> 5.01 us  [shifted(): lax.ppermute(value, axis, [(i, (i + amount) % size) for i in range(size)])]
where the time goes in v6:
time: 155 us; the launch traced here: 154 us
  Pallas kernels  60.1 us (39%)
  starting transfers between devices  51 us (33%)
  waiting for transfers between devices  29.5 us (19%)
  blocking collectives  9.98 us (6%)
  other arithmetic  3.07 us (2%)
    pallas_call x7, Pallas kernels, call(): pl.pallas_call(body, name=name, out_shape=outs, in_specs=in_specs or [VME...  60.1 us
    all_to_all x2, starting transfers between devices, deliver(): lax.all_to_all(rows.reshape(-1, 8, rows.shape[1]), GRP_BLK, split_axis=0,...  27 us
    all_to_all x2, waiting for transfers between devices, deliver(): lax.all_to_all(rows.reshape(-1, 8, rows.shape[1]), GRP_BLK, split_axis=0,...  16 us
    ppermute x8, starting transfers between devices, shifted(): lax.ppermute(value, axis, [(i, (i + amount) % size) for i in range(size)])  13.4 us
    all_to_all x2, starting transfers between devices, copies_summed(): return jnp.sum(lax.all_to_all(copies, axes, 0, 0, tiled=True), axis=0)  10.6 us
    all_to_all x1, blocking collectives, copies_summed(): return jnp.sum(lax.all_to_all(copies, axes, 0, 0, tiled=True), axis=0)  9.98 us
    all_to_all x2, waiting for transfers between devices, copies_summed(): return jnp.sum(lax.all_to_all(copies, axes, 0, 0, tiled=True), axis=0)  8.46 us
    ppermute x8, waiting for transfers between devices, shifted(): lax.ppermute(value, axis, [(i, (i + amount) % size) for i in range(size)])  5.01 us
  transfers between devices with their start and end apart: 12, of which 11 were waited for; matrix products, arithmetic and copies ran while one was open for 0% of the time, Pallas kernels for 22%

profile of v6, /device:TPU:1, one launch (start us, length us, event | category | flops | bytes accessed | tf_op | source)
XLA Modules:
  0.0 154.3 jit_solution(1535529059525574255)
XLA Ops:
  0.0 4.6 %send_rows.2 = bf16[2048,256]{1,0:T(8,128)(2,1)} custom-call(s32[1,2048]{1,0:T(1,128)} %list_ref.3, s32[1,2048]{1,0:T(1,128)} %list_ref.3, bf16[1024,256]{1,0:T(8,128)(2,1)} %refs_0_.1), custom_call_target="tpu_custom_call" | custom-call | flops 1073741824 | bytes 4194304 | tf_op jit(solution)/shard_map/send_rows/pallas_call | solution.py:475
  4.6 16.7 %all-to-all-start = ((bf16[256,8,256]{2,1,0:T(8,128)(2,1)}), bf16[256,8,256]{2,1,0:T(8,128)(2,1)}, u32[]{:S(2)}, u32[]{:S(2)}) async-start(bf16[256,8,256]{2,1,0:T(8,128)(2,1)} %bitcast.12), calls=%async_computation | async-start | bytes 2097152 | tf_op jit(solution)/shard_map/all_to_all | solution.py:610
  21.3 9.4 %sort_edges.1 = (s32[8,2048]{1,0:T(8,128)}, s32[1,2048]{1,0:T(1,128)}, f32[8,2048]{1,0:T(8,128)}, f32[1024,8]{1,0:T(8,128)}, s32[1,32]{1,0:T(1,128)}) custom-call(s32[1,2048]{1,0:T(1,128)} %bitcast.17, s32[1,2048]{1,0:T(1,128)} %bitcast.18, s32[1,2048]{1,0:T(1,128)} %bitcast.19, f32[8,2048]{1,0:T(8,128)} %bias_ref.1), custom_call_target="tpu_custom_call" | custom-call | flops 2147483648 | bytes 4194304 | tf_op jit(solution)/shard_map/sort_edges/pallas_call | solution.py:475
  30.7 9.8 %own_part.2 = (bf16[1024,256]{1,0:T(8,128)(2,1)}, f32[1024,256]{1,0:T(8,128)}, bf16[2048,256]{1,0:T(8,128)(2,1)}, f32[8,2048]{1,0:T(8,128)}) custom-call(bf16[1024,256]{1,0:T(8,128)(2,1)} %refs_0_.1, bf16[2,256,256]{2,1,0:T(8,128)(2,1)} %refs_5_.5, bf16[2,256,256]{2,1,0:T(8,128)(2,1)} %refs_5_.4, bf16[2,256,256]{2,1,0:T(8,128)(2,1)} %refs_6_.4, ...), custom_call_target="tpu_custom_call" | custom-call | flops 3221225472 | bytes 4194304 | tf_op jit(solution)/shard_map/own_part/pallas_call | solution.py:475
  40.5 11.0 %all-to-all-done = bf16[256,8,256]{2,1,0:T(8,128)(2,1)} async-done(((bf16[256,8,256]{2,1,0:T(8,128)(2,1)}), bf16[256,8,256]{2,1,0:T(8,128)(2,1)}, u32[]{:S(2)}, u32[]{:S(2)}) %all-to-all-start) | async-done | bytes 1048608 | tf_op jit(solution)/shard_map/all_to_all | solution.py:610
  51.5 10.8 %edge_part.2 = (f32[1024,256]{1,0:T(8,128)}, f32[8,2,256]{2,1,0:T(2,128)}, bf16[1024,256]{1,0:T(8,128)(2,1)}) custom-call(bf16[2048,256]{1,0:T(8,128)(2,1)} %bitcast.1.refs_0_, bf16[1024,256]{1,0:T(8,128)(2,1)} %get-tuple-element.27.refs_1_, bf16[2048,256]{1,0:T(8,128)(2,1)} %get-tuple-element.28.refs_2_, f32[1024,8]{1,0:T(8,128)} %get-tuple-element.29.refs_3_, ...), custom_call_target="tpu_custom_call" | custom-call | flops 5368709120 | bytes 4194304 | tf_op jit(solution)/shard_map/edge_part/pallas_call | solution.py:475
  62.2 3.4 %all-to-all-start.1 = ((f32[8,2,256]{2,1,0:T(2,128)}), f32[8,2,256]{2,1,0:T(2,128)S(1)}, u32[]{:S(2)}, u32[]{:S(2)}) async-start(f32[8,2,256]{2,1,0:T(2,128)} %get-tuple-element.35), calls=%async_computation.1 | async-start | bytes 32768 | tf_op jit(solution)/shard_map/all_to_all | solution.py:621
  65.6 4.6 %send_rows.3 = bf16[2048,256]{1,0:T(8,128)(2,1)} custom-call(s32[1,2048]{1,0:T(1,128)} %list_ref.3, s32[1,2048]{1,0:T(1,128)} %list_ref.3, bf16[1024,256]{1,0:T(8,128)(2,1)} %get-tuple-element.34.table_ref), custom_call_target="tpu_custom_call" | custom-call | flops 1073741824 | bytes 4194304 | tf_op jit(solution)/shard_map/send_rows/pallas_call | solution.py:475
  70.2 2.0 %all-to-all-done.1 = f32[8,2,256]{2,1,0:T(2,128)S(1)} async-done(((f32[8,2,256]{2,1,0:T(2,128)}), f32[8,2,256]{2,1,0:T(2,128)S(1)}, u32[]{:S(2)}, u32[]{:S(2)}) %all-to-all-start.1) | async-done | bytes 16416 | tf_op jit(solution)/shard_map/all_to_all | solution.py:621
  72.3 10.3 %all-to-all-start.2 = ((bf16[256,8,256]{2,1,0:T(8,128)(2,1)}), bf16[256,8,256]{2,1,0:T(8,128)(2,1)}, u32[]{:S(2)}, u32[]{:S(2)}) async-start(bf16[256,8,256]{2,1,0:T(8,128)(2,1)} %bitcast.11), calls=%async_computation.2 | async-start | bytes 2097152 | tf_op jit(solution)/shard_map/all_to_all | solution.py:610
  82.6 2.5 %collective-permute-start = (f32[2,256]{1,0:T(2,128)S(1)}, f32[2,256]{1,0:T(2,128)S(1)}, u32[]{:S(2)}, u32[]{:S(2)}) collective-permute-start(f32[2,256]{1,0:T(2,128)S(1)} %reduce_sum.27), channel_id=1, source_target_pairs={{0,1},{1,0},{2,3},{3,2},{4,5},{5,4},{6,7},{7,6},{8,9},{9,8},{10,11... | collective-permute-start | bytes 6152 | tf_op jit(solution)/shard_map/ppermute | solution.py:617
  85.1 0.8 collective-permute-done
  85.9 0.0 collective-permute-start.1
  85.9 1.9 %collective-permute-start.2 = (f32[2,256]{1,0:T(2,128)S(1)}, f32[2,256]{1,0:T(2,128)S(1)}, u32[]{:S(2)}, u32[]{:S(2)}) collective-permute-start(f32[2,256]{1,0:T(2,128)S(1)} %add.44), channel_id=1, source_target_pairs={{0,4},{2,6},{4,0},{6,2},{1,5},{3,7},{5,1},{7,3},{8,12},{10,14},{12... | collective-permute-start | bytes 6152 | tf_op jit(solution)/shard_map/ppermute | solution.py:617
  87.8 1.2 collective-permute-start.3
  89.0 1.2 collective-permute-done.1
  90.2 0.1 collective-permute-done.2
  90.3 0.4 collective-permute-done.3
  90.7 1.2 collective-permute-start.4
  91.9 2.5 %collective-permute-start.5 = (f32[2,256]{1,0:T(2,128)S(1)}, f32[2,256]{1,0:T(2,128)S(1)}, u32[]{:S(2)}, u32[]{:S(2)}) collective-permute-start(f32[2,256]{1,0:T(2,128)S(1)} %add_add_fusion.1), channel_id=1, source_target_pairs={{0,128},{64,192},{128,0},{192,64},{1,129},{65,193},{129,1},{193,65... | collective-permute-start | bytes 6152 | tf_op jit(solution)/shard_map/ppermute | solution.py:617
  94.4 1.1 collective-permute-start.6
  95.5 0.0 collective-permute-done.4
  95.5 0.7 collective-permute-done.5
  96.2 1.0 collective-permute-done.6
  97.2 0.6 add_add_fusion.refs_1_.refs_12_
  97.8 10.0 %own_part.3 = (bf16[1024,256]{1,0:T(8,128)(2,1)}, f32[1024,256]{1,0:T(8,128)}, bf16[2048,256]{1,0:T(8,128)(2,1)}, f32[8,2048]{1,0:T(8,128)}) custom-call(f32[1024,256]{1,0:T(8,128)} %get-tuple-element.37.refs_0_, f32[2,256]{1,0:T(2,128)} %add_add_fusion.refs_1_.refs_12_, bf16[2,256]{1,0:T(2,128)(2,1)} %refs_13_.1, bf16[2,256]{1,0:T(2,128)(2,1)} %refs_14_.1, ...), custom_call_target="tpu_custom_call" | custom-call | flops 3221225472 | bytes 4194304 | tf_op jit(solution)/shard_map/own_part/pallas_call | solution.py:475
  107.8 5.0 %all-to-all-done.2 = bf16[256,8,256]{2,1,0:T(8,128)(2,1)} async-done(((bf16[256,8,256]{2,1,0:T(8,128)(2,1)}), bf16[256,8,256]{2,1,0:T(8,128)(2,1)}, u32[]{:S(2)}, u32[]{:S(2)}) %all-to-all-start.2) | async-done | bytes 1048608 | tf_op jit(solution)/shard_map/all_to_all | solution.py:610
  112.8 10.9 %edge_part.3 = (f32[1024,256]{1,0:T(8,128)}, f32[8,2,256]{2,1,0:T(2,128)}) custom-call(bf16[2048,256]{1,0:T(8,128)(2,1)} %bitcast.6.refs_0_, bf16[1024,256]{1,0:T(8,128)(2,1)} %get-tuple-element.39.refs_1_, bf16[2048,256]{1,0:T(8,128)(2,1)} %get-tuple-element.40.refs_2_, f32[1024,8]{1,0:T(8,128)} %get-tuple-element.29.refs_3_, ...), custom_call_target="tpu_custom_call" | custom-call | flops 5368709120 | bytes 4194304 | tf_op jit(solution)/shard_map/edge_part/pallas_call | solution.py:475
  123.7 10.0 %all_to_all.25 = f32[8,2,256]{2,1,0:T(2,128)S(1)} all-to-all(f32[8,2,256]{2,1,0:T(2,128)} %get-tuple-element.44), channel_id=1, replica_groups=mesh['grp'=4,'blk_0'=8,'blk_1'=4,'blk_2'=2] {'blk_0'}, dimensions={0} | all-to-all | bytes 32768 | tf_op jit(solution)/shard_map/all_to_all | solution.py:621
  133.7 0.0 copy-start
  133.8 3.0 %collective-permute-start.7 = (f32[2,256]{1,0:T(2,128)S(1)}, f32[2,256]{1,0:T(2,128)S(1)}, u32[]{:S(2)}, u32[]{:S(2)}) collective-permute-start(f32[2,256]{1,0:T(2,128)S(1)} %reduce_sum.28), channel_id=1, source_target_pairs={{0,1},{1,0},{2,3},{3,2},{4,5},{5,4},{6,7},{7,6},{8,9},{9,8},{10,11... | collective-permute-start | bytes 6152 | tf_op jit(solution)/shard_map/ppermute | solution.py:617
  136.7 0.0 copy-done
  136.7 0.8 collective-permute-done.7
  137.6 0.6 broadcast_in_dim.2
  138.2 0.0 copy-start.1
  138.2 7.2 %all-to-all-start.4 = ((f32[16,2,256]{2,1,0:T(2,128)}), f32[16,2,256]{2,1,0:T(2,128)S(1)}, u32[]{:S(2)}, u32[]{:S(2)}) async-start(f32[16,2,256]{2,1,0:T(2,128)} %broadcast_in_dim.2), calls=%async_computation.4 | async-start | bytes 65536 | tf_op jit(solution)/shard_map/all_to_all | solution.py:621
  145.4 0.0 copy-done.1
  145.5 6.4 %all-to-all-done.4 = f32[16,2,256]{2,1,0:T(2,128)S(1)} async-done(((f32[16,2,256]{2,1,0:T(2,128)}), f32[16,2,256]{2,1,0:T(2,128)S(1)}, u32[]{:S(2)}, u32[]{:S(2)}) %all-to-all-start.4) | async-done | bytes 32800 | tf_op jit(solution)/shard_map/all_to_all | solution.py:621
  151.9 2.4 %fusion = bf16[1024,256]{1,0:T(8,128)(2,1)} fusion(f32[1024,256]{1,0:T(8,128)} %get-tuple-element.43, f32[256]{0:T(256)S(1)} %bitcast.13, f32[256]{0:T(256)S(1)} %bitcast.14, f32[256]{0:T(256)S(1)} %bitcast.16, f32[256]{0:T(256)S(1)} %bitcast.15), kind=kLoop, calls=%fused_computation.1 | loop fusion | flops 2359296 | bytes 1576960 | tf_op jit(solution)/shard_map/convert_element_type | solution.py:87
  (9 shorter events, 0.1 us)
Async XLA Ops:
  4.6 46.9 %all-to-all-start = ((bf16[256,8,256]{2,1,0:T(8,128)(2,1)}), bf16[256,8,256]{2,1,0:T(8,128)(2,1)}, u32[]{:S(2)}, u32[]{:S(2)}) async-start(bf16[256,8,256]{2,1,0:T(8,128)(2,1)} %bitcast.12), calls=%async_computation | async-start | bytes 2097152 | tf_op jit(solution)/shard_map/all_to_all | solution.py:610
  62.2 10.0 %all-to-all-start.1 = ((f32[8,2,256]{2,1,0:T(2,128)}), f32[8,2,256]{2,1,0:T(2,128)S(1)}, u32[]{:S(2)}, u32[]{:S(2)}) async-start(f32[8,2,256]{2,1,0:T(2,128)} %get-tuple-element.35), calls=%async_computation.1 | async-start | bytes 32768 | tf_op jit(solution)/shard_map/all_to_all | solution.py:621
  72.3 40.5 %all-to-all-start.2 = ((bf16[256,8,256]{2,1,0:T(8,128)(2,1)}), bf16[256,8,256]{2,1,0:T(8,128)(2,1)}, u32[]{:S(2)}, u32[]{:S(2)}) async-start(bf16[256,8,256]{2,1,0:T(8,128)(2,1)} %bitcast.11), calls=%async_computation.2 | async-start | bytes 2097152 | tf_op jit(solution)/shard_map/all_to_all | solution.py:610
  82.6 3.3 %collective-permute-start = (f32[2,256]{1,0:T(2,128)S(1)}, f32[2,256]{1,0:T(2,128)S(1)}, u32[]{:S(2)}, u32[]{:S(2)}) collective-permute-start(f32[2,256]{1,0:T(2,128)S(1)} %reduce_sum.27), channel_id=1, source_target_pairs={{0,1},{1,0},{2,3},{3,2},{4,5},{5,4},{6,7},{7,6},{8,9},{9,8},{10,11... | collective-permute-start | bytes 6152 | tf_op jit(solution)/shard_map/ppermute | solution.py:617
  85.9 4.3 %collective-permute-start.1 = (f32[2,256]{1,0:T(2,128)S(1)}, f32[2,256]{1,0:T(2,128)S(1)}, u32[]{:S(2)}, u32[]{:S(2)}) collective-permute-start(f32[2,256]{1,0:T(2,128)S(1)} %add.44), channel_id=1, source_target_pairs={{0,2},{2,4},{4,6},{6,0},{1,3},{3,5},{5,7},{7,1},{8,10},{10,12},{12... | collective-permute-start | bytes 6152 | tf_op jit(solution)/shard_map/ppermute | solution.py:617
  85.9 4.4 %collective-permute-start.2 = (f32[2,256]{1,0:T(2,128)S(1)}, f32[2,256]{1,0:T(2,128)S(1)}, u32[]{:S(2)}, u32[]{:S(2)}) collective-permute-start(f32[2,256]{1,0:T(2,128)S(1)} %add.44), channel_id=1, source_target_pairs={{0,4},{2,6},{4,0},{6,2},{1,5},{3,7},{5,1},{7,3},{8,12},{10,14},{12... | collective-permute-start | bytes 6152 | tf_op jit(solution)/shard_map/ppermute | solution.py:617
  87.8 2.9 %collective-permute-start.3 = (f32[2,256]{1,0:T(2,128)S(1)}, f32[2,256]{1,0:T(2,128)S(1)}, u32[]{:S(2)}, u32[]{:S(2)}) collective-permute-start(f32[2,256]{1,0:T(2,128)S(1)} %add.44), channel_id=1, source_target_pairs={{0,6},{2,0},{4,2},{6,4},{1,7},{3,1},{5,3},{7,5},{8,14},{10,8},{12,... | collective-permute-start | bytes 6152 | tf_op jit(solution)/shard_map/ppermute | solution.py:617
  90.7 4.9 %collective-permute-start.4 = (f32[2,256]{1,0:T(2,128)S(1)}, f32[2,256]{1,0:T(2,128)S(1)}, u32[]{:S(2)}, u32[]{:S(2)}) collective-permute-start(f32[2,256]{1,0:T(2,128)S(1)} %add_add_fusion.1), channel_id=1, source_target_pairs={{0,64},{64,128},{128,192},{192,0},{1,65},{65,129},{129,193},{193,1... | collective-permute-start | bytes 6152 | tf_op jit(solution)/shard_map/ppermute | solution.py:617
  91.9 4.4 %collective-permute-start.5 = (f32[2,256]{1,0:T(2,128)S(1)}, f32[2,256]{1,0:T(2,128)S(1)}, u32[]{:S(2)}, u32[]{:S(2)}) collective-permute-start(f32[2,256]{1,0:T(2,128)S(1)} %add_add_fusion.1), channel_id=1, source_target_pairs={{0,128},{64,192},{128,0},{192,64},{1,129},{65,193},{129,1},{193,65... | collective-permute-start | bytes 6152 | tf_op jit(solution)/shard_map/ppermute | solution.py:617
  94.4 2.8 %collective-permute-start.6 = (f32[2,256]{1,0:T(2,128)S(1)}, f32[2,256]{1,0:T(2,128)S(1)}, u32[]{:S(2)}, u32[]{:S(2)}) collective-permute-start(f32[2,256]{1,0:T(2,128)S(1)} %add_add_fusion.1), channel_id=1, source_target_pairs={{0,192},{64,0},{128,64},{192,128},{1,193},{65,1},{129,65},{193,129... | collective-permute-start | bytes 6152 | tf_op jit(solution)/shard_map/ppermute | solution.py:617
  133.7 3.0 %copy-start = (bf16[2,256]{1,0:T(2,128)(2,1)S(1)}, bf16[2,256]{1,0:T(2,128)(2,1)}, u32[]{:S(2)}) copy-start(bf16[2,256]{1,0:T(2,128)(2,1)} %refs_14_.1) | copy-start | bytes 3076
  133.8 3.8 %collective-permute-start.7 = (f32[2,256]{1,0:T(2,128)S(1)}, f32[2,256]{1,0:T(2,128)S(1)}, u32[]{:S(2)}, u32[]{:S(2)}) collective-permute-start(f32[2,256]{1,0:T(2,128)S(1)} %reduce_sum.28), channel_id=1, source_target_pairs={{0,1},{1,0},{2,3},{3,2},{4,5},{5,4},{6,7},{7,6},{8,9},{9,8},{10,11... | collective-permute-start | bytes 6152 | tf_op jit(solution)/shard_map/ppermute | solution.py:617
  138.2 7.3 %copy-start.1 = (bf16[2,256]{1,0:T(2,128)(2,1)S(1)}, bf16[2,256]{1,0:T(2,128)(2,1)}, u32[]{:S(2)}) copy-start(bf16[2,256]{1,0:T(2,128)(2,1)} %refs_13_.1) | copy-start | bytes 3076
  138.2 13.7 %all-to-all-start.4 = ((f32[16,2,256]{2,1,0:T(2,128)}), f32[16,2,256]{2,1,0:T(2,128)S(1)}, u32[]{:S(2)}, u32[]{:S(2)}) async-start(f32[16,2,256]{2,1,0:T(2,128)} %broadcast_in_dim.2), calls=%async_computation.4 | async-start | bytes 65536 | tf_op jit(solution)/shard_map/all_to_all | solution.py:621

commit v7 on v5

--- a/solution.py
+++ b/solution.py
@@ -103,10 +103,10 @@
     )
 
 
-def fetch_rows(index_ref, first, pairs_ref, got_ref):
+def fetch_rows(index_ref, first, pairs_ref, got_ref, scale):
     for e in range(CHUNK):
-        row = index_ref[0, first + e]
-        got_ref[2 * e : 2 * e + 2, :] = pairs_ref[pl.ds(pl.multiple_of(2 * row, 2), 2), :]
+        row = pl.multiple_of(index_ref[0, first + e] * scale, 2)
+        got_ref[2 * e : 2 * e + 2, :] = pairs_ref[pl.ds(row, 2), :]
 
 
 def send_kernel(index_ref, list_ref, table_ref, out_hbm, pairs_ref, got_ref, out_ref, sems):
@@ -114,22 +114,19 @@
         put_rows(pairs_ref, k * CHUNK, table_ref[k * CHUNK : (k + 1) * CHUNK, :].astype(F32))
 
     def store(c):
-        at = pl.ds(pl.multiple_of(c * 2 * CHUNK, 2 * CHUNK), 2 * CHUNK)
+        at = slice(c * 2 * CHUNK, (c + 1) * 2 * CHUNK)
         return pltpu.make_async_copy(out_ref.at[at], out_hbm.at[at], sems.at[c])
 
-    def pair(c, carry):
-        here = pl.ds(pl.multiple_of(c * 2 * CHUNK, CHUNK), CHUNK)
-        after = pl.ds(pl.multiple_of(c * 2 * CHUNK + CHUNK, CHUNK), CHUNK)
-        fetch_rows(index_ref, c * 2 * CHUNK + CHUNK, pairs_ref, got_ref)
+    count = ROWS_IN // (2 * CHUNK)
+    for c in range(count):
+        here = slice(c * 2 * CHUNK, c * 2 * CHUNK + CHUNK)
+        after = slice(c * 2 * CHUNK + CHUNK, (c + 1) * 2 * CHUNK)
+        fetch_rows(index_ref, c * 2 * CHUNK + CHUNK, pairs_ref, got_ref, 2)
         col = columns_of(list_ref[0:1, here].astype(F32)).astype(jnp.int32)[:, 0:1]
         hot = one_hot(col == iota((CHUNK, NODES_OWN), 1))
         out_ref[here, :] = dot(hot, table_ref[...]).astype(BF16)
         out_ref[after, :] = get_rows(got_ref).astype(BF16)
         store(c).start()
-        return carry
-
-    count = ROWS_IN // (2 * CHUNK)
-    lax.fori_loop(0, count, pair, 0)
     for c in range(count):
         store(c).wait()
 
@@ -177,7 +174,7 @@
     src_s = (placed[0:1] * 256.0 + placed[1:2]).astype(jnp.int32)
     tgt_s = (placed[2:3] * 256.0 + placed[3:4]).astype(jnp.int32)
     lane8 = iota((8, EDGES_OWN), 1)
-    srcs_ref[...] = src_s
+    srcs_ref[...] = 2 * src_s
     tgt8 = jnp.broadcast_to(tgt_s, (8, EDGES_OWN))
     before = pltpu.roll(tgt8, 1, 1)
     after = pltpu.roll(tgt8, EDGES_OWN - 1, 1)
@@ -367,10 +364,10 @@
         put_rows(table_ref, k * CHUNK, left_ref[k * CHUNK : (k + 1) * CHUNK, :].astype(F32))
 
     def fetch(c, out_ref):
-        fetch_rows(srcs_ref, c * CHUNK, table_ref, out_ref)
+        fetch_rows(srcs_ref, c * CHUNK, table_ref, out_ref, 1)
 
     def score(c, in_ref):
-        at = pl.ds(pl.multiple_of(c * CHUNK, CHUNK), CHUNK)
+        at = slice(c * CHUNK, (c + 1) * CHUNK)
         src = get_rows(in_ref)
         edge_ref[at, :] = src.astype(BF16)
         score_ref[:, at] = scores_of(heads, leaky(src + dst_ref[at, :].astype(F32)))
@@ -378,14 +375,12 @@
     fetch(0, even_ref)
     settle(1)
 
-    def pair(c, carry):
+    for c in range(EDGE_CHUNKS // 2):
         fetch(2 * c + 1, odd_ref)
         score(2 * c, even_ref)
-        fetch(lax.rem(2 * c + 2, EDGE_CHUNKS), even_ref)
+        if 2 * c + 2 < EDGE_CHUNKS:
+            fetch(2 * c + 2, even_ref)
         score(2 * c + 1, odd_ref)
-        return carry
-
-    lax.fori_loop(0, EDGE_CHUNKS // 2, pair, 0)
 
     settle(4)
     tgt = rows_ref[0:1, :]

time: 153 us -> 148 us (0.967)
  Pallas kernels: 60.4 us -> 53.8 us
    pallas_call x7, Pallas kernels: 60.4 us -> 53.8 us  [call(): pl.pallas_call(body, name=name, out_shape=outs, in_specs=in_specs or [VME...]
where the time goes in v7:
time: 148 us
  Pallas kernels  53.8 us (36%)
  starting transfers between devices  52.4 us (35%)
  waiting for transfers between devices  37.4 us (25%)
  other arithmetic  3.1 us (2%)
    pallas_call x7, Pallas kernels, call(): pl.pallas_call(body, name=name, out_shape=outs, in_specs=in_specs or [VME...  53.8 us
    all_to_all x2, starting transfers between devices, deliver(): lax.all_to_all(rows.reshape(-1, 8, rows.shape[1]), GRP_BLK, split_axis=0,...  26 us
    all_to_all x2, waiting for transfers between devices, deliver(): lax.all_to_all(rows.reshape(-1, 8, rows.shape[1]), GRP_BLK, split_axis=0,...  16.7 us
    all_to_all x3, waiting for transfers between devices, copies_summed(): return jnp.sum(lax.all_to_all(copies, axes, 0, 0, tiled=True), axis=0)  16.5 us
    all_to_all x3, starting transfers between devices, copies_summed(): return jnp.sum(lax.all_to_all(copies, axes, 0, 0, tiled=True), axis=0)  16.2 us
    ppermute x7, starting transfers between devices, shifted(): lax.ppermute(value, axis, [(i, (i + amount) % size) for i in range(size)])  10.2 us
    ppermute x7, waiting for transfers between devices, shifted(): lax.ppermute(value, axis, [(i, (i + amount) % size) for i in range(size)])  4.2 us
  transfers between devices with their start and end apart: 12, of which 11 were waited for; matrix products, arithmetic and copies ran while one was open for 0% of the time, Pallas kernels for 22%

profile of v7, /device:TPU:1, one launch (start us, length us, event | category | flops | bytes accessed | tf_op | source)
XLA Modules:
  0.0 147.5 jit_solution(3263675849615473631)
XLA Ops:
  0.0 3.5 %send_rows.2 = bf16[2048,256]{1,0:T(8,128)(2,1)} custom-call(s32[1,2048]{1,0:T(1,128)} %list_ref.3, s32[1,2048]{1,0:T(1,128)} %list_ref.3, bf16[1024,256]{1,0:T(8,128)(2,1)} %refs_0_.1), custom_call_target="tpu_custom_call" | custom-call | flops 1073741824 | bytes 4194304 | tf_op jit(solution)/shard_map/send_rows/pallas_call | solution.py:470
  3.5 16.6 %all-to-all-start = ((bf16[256,8,256]{2,1,0:T(8,128)(2,1)}), bf16[256,8,256]{2,1,0:T(8,128)(2,1)}, u32[]{:S(2)}, u32[]{:S(2)}) async-start(bf16[256,8,256]{2,1,0:T(8,128)(2,1)} %bitcast.12), calls=%async_computation | async-start | bytes 2097152 | tf_op jit(solution)/shard_map/all_to_all | solution.py:605
  20.1 9.4 %sort_edges.1 = (s32[8,2048]{1,0:T(8,128)}, s32[1,2048]{1,0:T(1,128)}, f32[8,2048]{1,0:T(8,128)}, f32[1024,8]{1,0:T(8,128)}, s32[1,32]{1,0:T(1,128)}) custom-call(s32[1,2048]{1,0:T(1,128)} %bitcast.17, s32[1,2048]{1,0:T(1,128)} %bitcast.18, s32[1,2048]{1,0:T(1,128)} %bitcast.19, f32[8,2048]{1,0:T(8,128)} %bias_ref.1), custom_call_target="tpu_custom_call" | custom-call | flops 2147483648 | bytes 4194304 | tf_op jit(solution)/shard_map/sort_edges/pallas_call | solution.py:470
  29.5 9.6 %own_part.2 = (bf16[1024,256]{1,0:T(8,128)(2,1)}, f32[1024,256]{1,0:T(8,128)}, bf16[2048,256]{1,0:T(8,128)(2,1)}, f32[8,2048]{1,0:T(8,128)}) custom-call(bf16[1024,256]{1,0:T(8,128)(2,1)} %refs_0_.1, bf16[2,256,256]{2,1,0:T(8,128)(2,1)} %refs_5_.5, bf16[2,256,256]{2,1,0:T(8,128)(2,1)} %refs_5_.4, bf16[2,256,256]{2,1,0:T(8,128)(2,1)} %refs_6_.4, ...), custom_call_target="tpu_custom_call" | custom-call | flops 3221225472 | bytes 4194304 | tf_op jit(solution)/shard_map/own_part/pallas_call | solution.py:470
  39.1 11.2 %all-to-all-done = bf16[256,8,256]{2,1,0:T(8,128)(2,1)} async-done(((bf16[256,8,256]{2,1,0:T(8,128)(2,1)}), bf16[256,8,256]{2,1,0:T(8,128)(2,1)}, u32[]{:S(2)}, u32[]{:S(2)}) %all-to-all-start) | async-done | bytes 1048608 | tf_op jit(solution)/shard_map/all_to_all | solution.py:605
  50.3 9.0 %edge_part.2 = (f32[1024,256]{1,0:T(8,128)}, f32[8,2,256]{2,1,0:T(2,128)}, bf16[1024,256]{1,0:T(8,128)(2,1)}) custom-call(bf16[2048,256]{1,0:T(8,128)(2,1)} %bitcast.1.refs_0_, bf16[1024,256]{1,0:T(8,128)(2,1)} %get-tuple-element.27.refs_1_, bf16[2048,256]{1,0:T(8,128)(2,1)} %get-tuple-element.28.refs_2_, f32[1024,8]{1,0:T(8,128)} %get-tuple-element.29.refs_3_, ...), custom_call_target="tpu_custom_call" | custom-call | flops 5368709120 | bytes 4194304 | tf_op jit(solution)/shard_map/edge_part/pallas_call | solution.py:470
  59.3 3.5 %all-to-all-start.1 = ((f32[8,2,256]{2,1,0:T(2,128)}), f32[8,2,256]{2,1,0:T(2,128)S(1)}, u32[]{:S(2)}, u32[]{:S(2)}) async-start(f32[8,2,256]{2,1,0:T(2,128)} %get-tuple-element.35), calls=%async_computation.1 | async-start | bytes 32768 | tf_op jit(solution)/shard_map/all_to_all | solution.py:616
  62.9 3.5 %send_rows.3 = bf16[2048,256]{1,0:T(8,128)(2,1)} custom-call(s32[1,2048]{1,0:T(1,128)} %list_ref.3, s32[1,2048]{1,0:T(1,128)} %list_ref.3, bf16[1024,256]{1,0:T(8,128)(2,1)} %get-tuple-element.34.table_ref), custom_call_target="tpu_custom_call" | custom-call | flops 1073741824 | bytes 4194304 | tf_op jit(solution)/shard_map/send_rows/pallas_call | solution.py:470
  66.3 3.0 %all-to-all-done.1 = f32[8,2,256]{2,1,0:T(2,128)S(1)} async-done(((f32[8,2,256]{2,1,0:T(2,128)}), f32[8,2,256]{2,1,0:T(2,128)S(1)}, u32[]{:S(2)}, u32[]{:S(2)}) %all-to-all-start.1) | async-done | bytes 16416 | tf_op jit(solution)/shard_map/all_to_all | solution.py:616
  69.4 9.3 %all-to-all-start.2 = ((bf16[256,8,256]{2,1,0:T(8,128)(2,1)}), bf16[256,8,256]{2,1,0:T(8,128)(2,1)}, u32[]{:S(2)}, u32[]{:S(2)}) async-start(bf16[256,8,256]{2,1,0:T(8,128)(2,1)} %bitcast.11), calls=%async_computation.2 | async-start | bytes 2097152 | tf_op jit(solution)/shard_map/all_to_all | solution.py:605
  78.7 2.3 %collective-permute-start = (f32[2,256]{1,0:T(2,128)S(1)}, f32[2,256]{1,0:T(2,128)S(1)}, u32[]{:S(2)}, u32[]{:S(2)}) collective-permute-start(f32[2,256]{1,0:T(2,128)S(1)} %reduce_sum.27), channel_id=1, source_target_pairs={{0,1},{1,0},{2,3},{3,2},{4,5},{5,4},{6,7},{7,6},{8,9},{9,8},{10,11... | collective-permute-start | bytes 6152 | tf_op jit(solution)/shard_map/ppermute | solution.py:612
  81.0 0.8 collective-permute-done
  81.8 0.0 collective-permute-start.1
  81.8 1.9 %collective-permute-start.2 = (f32[2,256]{1,0:T(2,128)S(1)}, f32[2,256]{1,0:T(2,128)S(1)}, u32[]{:S(2)}, u32[]{:S(2)}) collective-permute-start(f32[2,256]{1,0:T(2,128)S(1)} %add.41), channel_id=1, source_target_pairs={{0,4},{2,6},{4,0},{6,2},{1,5},{3,7},{5,1},{7,3},{8,12},{10,14},{12... | collective-permute-start | bytes 6152 | tf_op jit(solution)/shard_map/ppermute | solution.py:612
  83.8 1.2 collective-permute-start.3
  84.9 1.0 collective-permute-done.1
  85.9 0.3 collective-permute-done.2
  86.2 0.4 collective-permute-done.3
  86.6 1.2 collective-permute-start.4
  87.8 2.5 %collective-permute-start.5 = (f32[2,256]{1,0:T(2,128)S(1)}, f32[2,256]{1,0:T(2,128)S(1)}, u32[]{:S(2)}, u32[]{:S(2)}) collective-permute-start(f32[2,256]{1,0:T(2,128)S(1)} %add_add_fusion.1), channel_id=1, source_target_pairs={{0,128},{64,192},{128,0},{192,64},{1,129},{65,193},{129,1},{193,65... | collective-permute-start | bytes 6152 | tf_op jit(solution)/shard_map/ppermute | solution.py:612
  90.3 1.1 collective-permute-start.6
  91.4 0.0 collective-permute-done.4
  91.4 0.7 collective-permute-done.5
  92.1 1.0 collective-permute-done.6
  93.1 0.6 add_add_fusion.refs_1_.refs_12_
  93.7 9.7 %own_part.3 = (bf16[1024,256]{1,0:T(8,128)(2,1)}, f32[1024,256]{1,0:T(8,128)}, bf16[2048,256]{1,0:T(8,128)(2,1)}, f32[8,2048]{1,0:T(8,128)}) custom-call(f32[1024,256]{1,0:T(8,128)} %get-tuple-element.37.refs_0_, f32[2,256]{1,0:T(2,128)} %add_add_fusion.refs_1_.refs_12_, bf16[2,256]{1,0:T(2,128)(2,1)} %refs_13_.1, bf16[2,256]{1,0:T(2,128)(2,1)} %refs_14_.1, ...), custom_call_target="tpu_custom_call" | custom-call | flops 3221225472 | bytes 4194304 | tf_op jit(solution)/shard_map/own_part/pallas_call | solution.py:470
  103.4 5.5 %all-to-all-done.2 = bf16[256,8,256]{2,1,0:T(8,128)(2,1)} async-done(((bf16[256,8,256]{2,1,0:T(8,128)(2,1)}), bf16[256,8,256]{2,1,0:T(8,128)(2,1)}, u32[]{:S(2)}, u32[]{:S(2)}) %all-to-all-start.2) | async-done | bytes 1048608 | tf_op jit(solution)/shard_map/all_to_all | solution.py:605
  108.9 9.2 %edge_part.3 = (f32[1024,256]{1,0:T(8,128)}, f32[8,2,256]{2,1,0:T(2,128)}) custom-call(bf16[2048,256]{1,0:T(8,128)(2,1)} %bitcast.6.refs_0_, bf16[1024,256]{1,0:T(8,128)(2,1)} %get-tuple-element.39.refs_1_, bf16[2048,256]{1,0:T(8,128)(2,1)} %get-tuple-element.40.refs_2_, f32[1024,8]{1,0:T(8,128)} %get-tuple-element.29.refs_3_, ...), custom_call_target="tpu_custom_call" | custom-call | flops 5368709120 | bytes 4194304 | tf_op jit(solution)/shard_map/edge_part/pallas_call | solution.py:470
  118.1 0.0 copy-start
  118.1 4.9 %all-to-all-start.3 = ((f32[8,2,256]{2,1,0:T(2,128)}), f32[8,2,256]{2,1,0:T(2,128)S(1)}, u32[]{:S(2)}, u32[]{:S(2)}) async-start(f32[8,2,256]{2,1,0:T(2,128)} %get-tuple-element.44), calls=%async_computation.3 | async-start | bytes 32768 | tf_op jit(solution)/shard_map/all_to_all | solution.py:616
  123.0 0.0 copy-done
  123.0 4.6 %all-to-all-done.3 = f32[8,2,256]{2,1,0:T(2,128)S(1)} async-done(((f32[8,2,256]{2,1,0:T(2,128)}), f32[8,2,256]{2,1,0:T(2,128)S(1)}, u32[]{:S(2)}, u32[]{:S(2)}) %all-to-all-start.3) | async-done | bytes 16416 | tf_op jit(solution)/shard_map/all_to_all | solution.py:616
  127.7 0.7 broadcast_in_dim.2
  128.3 0.0 copy-start.1
  128.3 7.9 %all-to-all-start.4 = ((f32[32,2,256]{2,1,0:T(2,128)}), f32[32,2,256]{2,1,0:T(2,128)S(1)}, u32[]{:S(2)}, u32[]{:S(2)}) async-start(f32[32,2,256]{2,1,0:T(2,128)} %broadcast_in_dim.2), calls=%async_computation.4 | async-start | bytes 131072 | tf_op jit(solution)/shard_map/all_to_all | solution.py:616
  136.2 0.0 copy-done.1
  136.2 8.8 %all-to-all-done.4 = f32[32,2,256]{2,1,0:T(2,128)S(1)} async-done(((f32[32,2,256]{2,1,0:T(2,128)}), f32[32,2,256]{2,1,0:T(2,128)S(1)}, u32[]{:S(2)}, u32[]{:S(2)}) %all-to-all-start.4) | async-done | bytes 65568 | tf_op jit(solution)/shard_map/all_to_all | solution.py:616
  145.1 2.4 %fusion = bf16[1024,256]{1,0:T(8,128)(2,1)} fusion(f32[1024,256]{1,0:T(8,128)} %get-tuple-element.43, f32[256]{0:T(256)S(1)} %bitcast.13, f32[256]{0:T(256)S(1)} %bitcast.14, f32[256]{0:T(256)S(1)} %bitcast.16, f32[256]{0:T(256)S(1)} %bitcast.15), kind=kLoop, calls=%fused_computation.1 | loop fusion | flops 2359296 | bytes 1576960 | tf_op jit(solution)/shard_map/convert_element_type | solution.py:87
  (8 shorter events, 0.1 us)
Async XLA Ops:
  3.5 46.9 %all-to-all-start = ((bf16[256,8,256]{2,1,0:T(8,128)(2,1)}), bf16[256,8,256]{2,1,0:T(8,128)(2,1)}, u32[]{:S(2)}, u32[]{:S(2)}) async-start(bf16[256,8,256]{2,1,0:T(8,128)(2,1)} %bitcast.12), calls=%async_computation | async-start | bytes 2097152 | tf_op jit(solution)/shard_map/all_to_all | solution.py:605
  59.3 10.0 %all-to-all-start.1 = ((f32[8,2,256]{2,1,0:T(2,128)}), f32[8,2,256]{2,1,0:T(2,128)S(1)}, u32[]{:S(2)}, u32[]{:S(2)}) async-start(f32[8,2,256]{2,1,0:T(2,128)} %get-tuple-element.35), calls=%async_computation.1 | async-start | bytes 32768 | tf_op jit(solution)/shard_map/all_to_all | solution.py:616
  69.4 39.5 %all-to-all-start.2 = ((bf16[256,8,256]{2,1,0:T(8,128)(2,1)}), bf16[256,8,256]{2,1,0:T(8,128)(2,1)}, u32[]{:S(2)}, u32[]{:S(2)}) async-start(bf16[256,8,256]{2,1,0:T(8,128)(2,1)} %bitcast.11), calls=%async_computation.2 | async-start | bytes 2097152 | tf_op jit(solution)/shard_map/all_to_all | solution.py:605
  78.7 3.1 %collective-permute-start = (f32[2,256]{1,0:T(2,128)S(1)}, f32[2,256]{1,0:T(2,128)S(1)}, u32[]{:S(2)}, u32[]{:S(2)}) collective-permute-start(f32[2,256]{1,0:T(2,128)S(1)} %reduce_sum.27), channel_id=1, source_target_pairs={{0,1},{1,0},{2,3},{3,2},{4,5},{5,4},{6,7},{7,6},{8,9},{9,8},{10,11... | collective-permute-start | bytes 6152 | tf_op jit(solution)/shard_map/ppermute | solution.py:612
  81.8 4.1 %collective-permute-start.1 = (f32[2,256]{1,0:T(2,128)S(1)}, f32[2,256]{1,0:T(2,128)S(1)}, u32[]{:S(2)}, u32[]{:S(2)}) collective-permute-start(f32[2,256]{1,0:T(2,128)S(1)} %add.41), channel_id=1, source_target_pairs={{0,2},{2,4},{4,6},{6,0},{1,3},{3,5},{5,7},{7,1},{8,10},{10,12},{12... | collective-permute-start | bytes 6152 | tf_op jit(solution)/shard_map/ppermute | solution.py:612
  81.8 4.4 %collective-permute-start.2 = (f32[2,256]{1,0:T(2,128)S(1)}, f32[2,256]{1,0:T(2,128)S(1)}, u32[]{:S(2)}, u32[]{:S(2)}) collective-permute-start(f32[2,256]{1,0:T(2,128)S(1)} %add.41), channel_id=1, source_target_pairs={{0,4},{2,6},{4,0},{6,2},{1,5},{3,7},{5,1},{7,3},{8,12},{10,14},{12... | collective-permute-start | bytes 6152 | tf_op jit(solution)/shard_map/ppermute | solution.py:612
  83.8 2.8 %collective-permute-start.3 = (f32[2,256]{1,0:T(2,128)S(1)}, f32[2,256]{1,0:T(2,128)S(1)}, u32[]{:S(2)}, u32[]{:S(2)}) collective-permute-start(f32[2,256]{1,0:T(2,128)S(1)} %add.41), channel_id=1, source_target_pairs={{0,6},{2,0},{4,2},{6,4},{1,7},{3,1},{5,3},{7,5},{8,14},{10,8},{12,... | collective-permute-start | bytes 6152 | tf_op jit(solution)/shard_map/ppermute | solution.py:612
  86.6 4.8 %collective-permute-start.4 = (f32[2,256]{1,0:T(2,128)S(1)}, f32[2,256]{1,0:T(2,128)S(1)}, u32[]{:S(2)}, u32[]{:S(2)}) collective-permute-start(f32[2,256]{1,0:T(2,128)S(1)} %add_add_fusion.1), channel_id=1, source_target_pairs={{0,64},{64,128},{128,192},{192,0},{1,65},{65,129},{129,193},{193,1... | collective-permute-start | bytes 6152 | tf_op jit(solution)/shard_map/ppermute | solution.py:612
  87.8 4.3 %collective-permute-start.5 = (f32[2,256]{1,0:T(2,128)S(1)}, f32[2,256]{1,0:T(2,128)S(1)}, u32[]{:S(2)}, u32[]{:S(2)}) collective-permute-start(f32[2,256]{1,0:T(2,128)S(1)} %add_add_fusion.1), channel_id=1, source_target_pairs={{0,128},{64,192},{128,0},{192,64},{1,129},{65,193},{129,1},{193,65... | collective-permute-start | bytes 6152 | tf_op jit(solution)/shard_map/ppermute | solution.py:612
  90.3 2.8 %collective-permute-start.6 = (f32[2,256]{1,0:T(2,128)S(1)}, f32[2,256]{1,0:T(2,128)S(1)}, u32[]{:S(2)}, u32[]{:S(2)}) collective-permute-start(f32[2,256]{1,0:T(2,128)S(1)} %add_add_fusion.1), channel_id=1, source_target_pairs={{0,192},{64,0},{128,64},{192,128},{1,193},{65,1},{129,65},{193,129... | collective-permute-start | bytes 6152 | tf_op jit(solution)/shard_map/ppermute | solution.py:612
  118.1 4.9 %copy-start = (bf16[2,256]{1,0:T(2,128)(2,1)S(1)}, bf16[2,256]{1,0:T(2,128)(2,1)}, u32[]{:S(2)}) copy-start(bf16[2,256]{1,0:T(2,128)(2,1)} %refs_14_.1) | copy-start | bytes 3076
  118.1 9.5 %all-to-all-start.3 = ((f32[8,2,256]{2,1,0:T(2,128)}), f32[8,2,256]{2,1,0:T(2,128)S(1)}, u32[]{:S(2)}, u32[]{:S(2)}) async-start(f32[8,2,256]{2,1,0:T(2,128)} %get-tuple-element.44), calls=%async_computation.3 | async-start | bytes 32768 | tf_op jit(solution)/shard_map/all_to_all | solution.py:616
  128.3 7.9 %copy-start.1 = (bf16[2,256]{1,0:T(2,128)(2,1)S(1)}, bf16[2,256]{1,0:T(2,128)(2,1)}, u32[]{:S(2)}) copy-start(bf16[2,256]{1,0:T(2,128)(2,1)} %refs_13_.1) | copy-start | bytes 3076
  128.3 16.7 %all-to-all-start.4 = ((f32[32,2,256]{2,1,0:T(2,128)}), f32[32,2,256]{2,1,0:T(2,128)S(1)}, u32[]{:S(2)}, u32[]{:S(2)}) async-start(f32[32,2,256]{2,1,0:T(2,128)} %broadcast_in_dim.2), calls=%async_computation.4 | async-start | bytes 131072 | tf_op jit(solution)/shard_map/all_to_all | solution.py:616

commit v8 on v7

--- a/solution.py
+++ b/solution.py
@@ -410,23 +410,23 @@
         mix_ref[at, FEAT:] = wide[:, FEAT:].astype(BF16)
         return carry
 
-    lax.fori_loop(0, EDGE_CHUNKS, mix, 0, unroll=4)
+    lax.fori_loop(0, EDGE_CHUNKS, mix, 0, unroll=EDGE_CHUNKS)
     acc_ref[...] = jnp.zeros_like(acc_ref)
 
-    def gather_in(c, carry):
-        here = pl.ds(pl.multiple_of(c * CHUNK, CHUNK), CHUNK)
+    for c in range(EDGE_CHUNKS):
+        here = slice(c * CHUNK, (c + 1) * CHUNK)
         low = lax.div(bound_ref[0, 2 * c], 8) * 8
         count = lax.div(jnp.maximum(bound_ref[0, 2 * c + 1] - low + WINDOW, 0), WINDOW)
 
-        def window(w, carry):
+        def window(w, carry, low=low, here=here):
             first = pl.multiple_of(low + w * WINDOW, 8)
             hot = one_hot(iota((WINDOW, CHUNK), 0) + first == rows_ref[0:1, here])
             acc_ref[pl.ds(first, WINDOW), :] += dot(hot, mix_ref[here, :])
             return carry
 
-        return lax.fori_loop(0, count, window, carry)
-
-    lax.fori_loop(0, EDGE_CHUNKS, gather_in, 0)
+        window(0, 0)
+        lax.fori_loop(1, count, window, 0)
+
     settle(2)
     totals = jnp.zeros((2, FEAT), F32)
     stores = []

time: 148 us -> 148 us (level)
  no operation moved by 1% of the time
where the time goes in v8:
time: 148 us; the launch traced here: 147 us
  Pallas kernels  52.9 us (36%)
  starting transfers between devices  52.6 us (36%)
  waiting for transfers between devices  37.6 us (25%)
  other arithmetic  3.1 us (2%)
    pallas_call x7, Pallas kernels, call(): pl.pallas_call(body, name=name, out_shape=outs, in_specs=in_specs or [VME...  52.9 us
    all_to_all x2, starting transfers between devices, deliver(): lax.all_to_all(rows.reshape(-1, 8, rows.shape[1]), GRP_BLK, split_axis=0,...  25.6 us
    all_to_all x3, starting transfers between devices, copies_summed(): return jnp.sum(lax.all_to_all(copies, axes, 0, 0, tiled=True), axis=0)  16.8 us
    all_to_all x2, waiting for transfers between devices, deliver(): lax.all_to_all(rows.reshape(-1, 8, rows.shape[1]), GRP_BLK, split_axis=0,...  16.7 us
    all_to_all x3, waiting for transfers between devices, copies_summed(): return jnp.sum(lax.all_to_all(copies, axes, 0, 0, tiled=True), axis=0)  16.6 us
    ppermute x7, starting transfers between devices, shifted(): lax.ppermute(value, axis, [(i, (i + amount) % size) for i in range(size)])  10.2 us
    ppermute x7, waiting for transfers between devices, shifted(): lax.ppermute(value, axis, [(i, (i + amount) % size) for i in range(size)])  4.2 us
  transfers between devices with their start and end apart: 12, of which 11 were waited for; matrix products, arithmetic and copies ran while one was open for 0% of the time, Pallas kernels for 22%

profile of v8, /device:TPU:1, one launch (start us, length us, event | category | flops | bytes accessed | tf_op | source)
XLA Modules:
  0.0 146.9 jit_solution(16273707553739077294)
XLA Ops:
  0.0 3.4 %send_rows.2 = bf16[2048,256]{1,0:T(8,128)(2,1)} custom-call(s32[1,2048]{1,0:T(1,128)} %list_ref.3, s32[1,2048]{1,0:T(1,128)} %list_ref.3, bf16[1024,256]{1,0:T(8,128)(2,1)} %refs_0_.1), custom_call_target="tpu_custom_call" | custom-call | flops 1073741824 | bytes 4194304 | tf_op jit(solution)/shard_map/send_rows/pallas_call | solution.py:470
  3.5 16.7 %all-to-all-start = ((bf16[256,8,256]{2,1,0:T(8,128)(2,1)}), bf16[256,8,256]{2,1,0:T(8,128)(2,1)}, u32[]{:S(2)}, u32[]{:S(2)}) async-start(bf16[256,8,256]{2,1,0:T(8,128)(2,1)} %bitcast.12), calls=%async_computation | async-start | bytes 2097152 | tf_op jit(solution)/shard_map/all_to_all | solution.py:605
  20.1 9.4 %sort_edges.1 = (s32[8,2048]{1,0:T(8,128)}, s32[1,2048]{1,0:T(1,128)}, f32[8,2048]{1,0:T(8,128)}, f32[1024,8]{1,0:T(8,128)}, s32[1,32]{1,0:T(1,128)}) custom-call(s32[1,2048]{1,0:T(1,128)} %bitcast.17, s32[1,2048]{1,0:T(1,128)} %bitcast.18, s32[1,2048]{1,0:T(1,128)} %bitcast.19, f32[8,2048]{1,0:T(8,128)} %bias_ref.1), custom_call_target="tpu_custom_call" | custom-call | flops 2147483648 | bytes 4194304 | tf_op jit(solution)/shard_map/sort_edges/pallas_call | solution.py:470
  29.5 9.6 %own_part.2 = (bf16[1024,256]{1,0:T(8,128)(2,1)}, f32[1024,256]{1,0:T(8,128)}, bf16[2048,256]{1,0:T(8,128)(2,1)}, f32[8,2048]{1,0:T(8,128)}) custom-call(bf16[1024,256]{1,0:T(8,128)(2,1)} %refs_0_.1, bf16[2,256,256]{2,1,0:T(8,128)(2,1)} %refs_5_.5, bf16[2,256,256]{2,1,0:T(8,128)(2,1)} %refs_5_.4, bf16[2,256,256]{2,1,0:T(8,128)(2,1)} %refs_6_.4, ...), custom_call_target="tpu_custom_call" | custom-call | flops 3221225472 | bytes 4194304 | tf_op jit(solution)/shard_map/own_part/pallas_call | solution.py:470
  39.1 11.2 %all-to-all-done = bf16[256,8,256]{2,1,0:T(8,128)(2,1)} async-done(((bf16[256,8,256]{2,1,0:T(8,128)(2,1)}), bf16[256,8,256]{2,1,0:T(8,128)(2,1)}, u32[]{:S(2)}, u32[]{:S(2)}) %all-to-all-start) | async-done | bytes 1048608 | tf_op jit(solution)/shard_map/all_to_all | solution.py:605
  50.3 8.6 %edge_part.2 = (f32[1024,256]{1,0:T(8,128)}, f32[8,2,256]{2,1,0:T(2,128)}, bf16[1024,256]{1,0:T(8,128)(2,1)}) custom-call(bf16[2048,256]{1,0:T(8,128)(2,1)} %bitcast.1.refs_0_, bf16[1024,256]{1,0:T(8,128)(2,1)} %get-tuple-element.27.refs_1_, bf16[2048,256]{1,0:T(8,128)(2,1)} %get-tuple-element.28.refs_2_, f32[1024,8]{1,0:T(8,128)} %get-tuple-element.29.refs_3_, ...), custom_call_target="tpu_custom_call" | custom-call | flops 5368709120 | bytes 4194304 | tf_op jit(solution)/shard_map/edge_part/pallas_call | solution.py:470
  59.0 3.9 %all-to-all-start.1 = ((f32[8,2,256]{2,1,0:T(2,128)}), f32[8,2,256]{2,1,0:T(2,128)S(1)}, u32[]{:S(2)}, u32[]{:S(2)}) async-start(f32[8,2,256]{2,1,0:T(2,128)} %get-tuple-element.35), calls=%async_computation.1 | async-start | bytes 32768 | tf_op jit(solution)/shard_map/all_to_all | solution.py:616
  62.9 3.5 %send_rows.3 = bf16[2048,256]{1,0:T(8,128)(2,1)} custom-call(s32[1,2048]{1,0:T(1,128)} %list_ref.3, s32[1,2048]{1,0:T(1,128)} %list_ref.3, bf16[1024,256]{1,0:T(8,128)(2,1)} %get-tuple-element.34.table_ref), custom_call_target="tpu_custom_call" | custom-call | flops 1073741824 | bytes 4194304 | tf_op jit(solution)/shard_map/send_rows/pallas_call | solution.py:470
  66.4 3.1 %all-to-all-done.1 = f32[8,2,256]{2,1,0:T(2,128)S(1)} async-done(((f32[8,2,256]{2,1,0:T(2,128)}), f32[8,2,256]{2,1,0:T(2,128)S(1)}, u32[]{:S(2)}, u32[]{:S(2)}) %all-to-all-start.1) | async-done | bytes 16416 | tf_op jit(solution)/shard_map/all_to_all | solution.py:616
  69.6 9.0 %all-to-all-start.2 = ((bf16[256,8,256]{2,1,0:T(8,128)(2,1)}), bf16[256,8,256]{2,1,0:T(8,128)(2,1)}, u32[]{:S(2)}, u32[]{:S(2)}) async-start(bf16[256,8,256]{2,1,0:T(8,128)(2,1)} %bitcast.11), calls=%async_computation.2 | async-start | bytes 2097152 | tf_op jit(solution)/shard_map/all_to_all | solution.py:605
  78.5 2.3 %collective-permute-start = (f32[2,256]{1,0:T(2,128)S(1)}, f32[2,256]{1,0:T(2,128)S(1)}, u32[]{:S(2)}, u32[]{:S(2)}) collective-permute-start(f32[2,256]{1,0:T(2,128)S(1)} %reduce_sum.27), channel_id=1, source_target_pairs={{0,1},{1,0},{2,3},{3,2},{4,5},{5,4},{6,7},{7,6},{8,9},{9,8},{10,11... | collective-permute-start | bytes 6152 | tf_op jit(solution)/shard_map/ppermute | solution.py:612
  80.9 0.8 collective-permute-done
  81.7 0.0 collective-permute-start.1
  81.7 1.9 %collective-permute-start.2 = (f32[2,256]{1,0:T(2,128)S(1)}, f32[2,256]{1,0:T(2,128)S(1)}, u32[]{:S(2)}, u32[]{:S(2)}) collective-permute-start(f32[2,256]{1,0:T(2,128)S(1)} %add.41), channel_id=1, source_target_pairs={{0,4},{2,6},{4,0},{6,2},{1,5},{3,7},{5,1},{7,3},{8,12},{10,14},{12... | collective-permute-start | bytes 6152 | tf_op jit(solution)/shard_map/ppermute | solution.py:612
  83.6 1.2 collective-permute-start.3
  84.8 1.0 collective-permute-done.1
  85.8 0.3 collective-permute-done.2
  86.1 0.4 collective-permute-done.3
  86.4 1.2 collective-permute-start.4
  87.6 2.5 %collective-permute-start.5 = (f32[2,256]{1,0:T(2,128)S(1)}, f32[2,256]{1,0:T(2,128)S(1)}, u32[]{:S(2)}, u32[]{:S(2)}) collective-permute-start(f32[2,256]{1,0:T(2,128)S(1)} %add_add_fusion.1), channel_id=1, source_target_pairs={{0,128},{64,192},{128,0},{192,64},{1,129},{65,193},{129,1},{193,65... | collective-permute-start | bytes 6152 | tf_op jit(solution)/shard_map/ppermute | solution.py:612
  90.1 1.1 collective-permute-start.6
  91.2 0.0 collective-permute-done.4
  91.2 0.7 collective-permute-done.5
  92.0 1.0 collective-permute-done.6
  93.0 0.6 add_add_fusion.refs_1_.refs_12_
  93.6 9.7 %own_part.3 = (bf16[1024,256]{1,0:T(8,128)(2,1)}, f32[1024,256]{1,0:T(8,128)}, bf16[2048,256]{1,0:T(8,128)(2,1)}, f32[8,2048]{1,0:T(8,128)}) custom-call(f32[1024,256]{1,0:T(8,128)} %get-tuple-element.37.refs_0_, f32[2,256]{1,0:T(2,128)} %add_add_fusion.refs_1_.refs_12_, bf16[2,256]{1,0:T(2,128)(2,1)} %refs_13_.1, bf16[2,256]{1,0:T(2,128)(2,1)} %refs_14_.1, ...), custom_call_target="tpu_custom_call" | custom-call | flops 3221225472 | bytes 4194304 | tf_op jit(solution)/shard_map/own_part/pallas_call | solution.py:470
  103.3 5.5 %all-to-all-done.2 = bf16[256,8,256]{2,1,0:T(8,128)(2,1)} async-done(((bf16[256,8,256]{2,1,0:T(8,128)(2,1)}), bf16[256,8,256]{2,1,0:T(8,128)(2,1)}, u32[]{:S(2)}, u32[]{:S(2)}) %all-to-all-start.2) | async-done | bytes 1048608 | tf_op jit(solution)/shard_map/all_to_all | solution.py:605
  108.8 8.7 %edge_part.3 = (f32[1024,256]{1,0:T(8,128)}, f32[8,2,256]{2,1,0:T(2,128)}) custom-call(bf16[2048,256]{1,0:T(8,128)(2,1)} %bitcast.6.refs_0_, bf16[1024,256]{1,0:T(8,128)(2,1)} %get-tuple-element.39.refs_1_, bf16[2048,256]{1,0:T(8,128)(2,1)} %get-tuple-element.40.refs_2_, f32[1024,8]{1,0:T(8,128)} %get-tuple-element.29.refs_3_, ...), custom_call_target="tpu_custom_call" | custom-call | flops 5368709120 | bytes 4194304 | tf_op jit(solution)/shard_map/edge_part/pallas_call | solution.py:470
  117.4 0.0 copy-start
  117.4 5.6 %all-to-all-start.3 = ((f32[8,2,256]{2,1,0:T(2,128)}), f32[8,2,256]{2,1,0:T(2,128)S(1)}, u32[]{:S(2)}, u32[]{:S(2)}) async-start(f32[8,2,256]{2,1,0:T(2,128)} %get-tuple-element.44), calls=%async_computation.3 | async-start | bytes 32768 | tf_op jit(solution)/shard_map/all_to_all | solution.py:616
  123.1 0.0 copy-done
  123.1 4.6 %all-to-all-done.3 = f32[8,2,256]{2,1,0:T(2,128)S(1)} async-done(((f32[8,2,256]{2,1,0:T(2,128)}), f32[8,2,256]{2,1,0:T(2,128)S(1)}, u32[]{:S(2)}, u32[]{:S(2)}) %all-to-all-start.3) | async-done | bytes 16416 | tf_op jit(solution)/shard_map/all_to_all | solution.py:616
  127.7 0.7 broadcast_in_dim.2
  128.4 0.0 copy-start.1
  128.4 7.2 %all-to-all-start.4 = ((f32[32,2,256]{2,1,0:T(2,128)}), f32[32,2,256]{2,1,0:T(2,128)S(1)}, u32[]{:S(2)}, u32[]{:S(2)}) async-start(f32[32,2,256]{2,1,0:T(2,128)} %broadcast_in_dim.2), calls=%async_computation.4 | async-start | bytes 131072 | tf_op jit(solution)/shard_map/all_to_all | solution.py:616
  135.6 0.0 copy-done.1
  135.7 8.8 %all-to-all-done.4 = f32[32,2,256]{2,1,0:T(2,128)S(1)} async-done(((f32[32,2,256]{2,1,0:T(2,128)}), f32[32,2,256]{2,1,0:T(2,128)S(1)}, u32[]{:S(2)}, u32[]{:S(2)}) %all-to-all-start.4) | async-done | bytes 65568 | tf_op jit(solution)/shard_map/all_to_all | solution.py:616
  144.5 2.4 %fusion = bf16[1024,256]{1,0:T(8,128)(2,1)} fusion(f32[1024,256]{1,0:T(8,128)} %get-tuple-element.43, f32[256]{0:T(256)S(1)} %bitcast.13, f32[256]{0:T(256)S(1)} %bitcast.14, f32[256]{0:T(256)S(1)} %bitcast.16, f32[256]{0:T(256)S(1)} %bitcast.15), kind=kLoop, calls=%fused_computation.1 | loop fusion | flops 2359296 | bytes 1576960 | tf_op jit(solution)/shard_map/convert_element_type | solution.py:87
  (8 shorter events, 0.1 us)
Async XLA Ops:
  3.5 46.9 %all-to-all-start = ((bf16[256,8,256]{2,1,0:T(8,128)(2,1)}), bf16[256,8,256]{2,1,0:T(8,128)(2,1)}, u32[]{:S(2)}, u32[]{:S(2)}) async-start(bf16[256,8,256]{2,1,0:T(8,128)(2,1)} %bitcast.12), calls=%async_computation | async-start | bytes 2097152 | tf_op jit(solution)/shard_map/all_to_all | solution.py:605
  59.0 10.6 %all-to-all-start.1 = ((f32[8,2,256]{2,1,0:T(2,128)}), f32[8,2,256]{2,1,0:T(2,128)S(1)}, u32[]{:S(2)}, u32[]{:S(2)}) async-start(f32[8,2,256]{2,1,0:T(2,128)} %get-tuple-element.35), calls=%async_computation.1 | async-start | bytes 32768 | tf_op jit(solution)/shard_map/all_to_all | solution.py:616
  69.6 39.2 %all-to-all-start.2 = ((bf16[256,8,256]{2,1,0:T(8,128)(2,1)}), bf16[256,8,256]{2,1,0:T(8,128)(2,1)}, u32[]{:S(2)}, u32[]{:S(2)}) async-start(bf16[256,8,256]{2,1,0:T(8,128)(2,1)} %bitcast.11), calls=%async_computation.2 | async-start | bytes 2097152 | tf_op jit(solution)/shard_map/all_to_all | solution.py:605
  78.5 3.1 %collective-permute-start = (f32[2,256]{1,0:T(2,128)S(1)}, f32[2,256]{1,0:T(2,128)S(1)}, u32[]{:S(2)}, u32[]{:S(2)}) collective-permute-start(f32[2,256]{1,0:T(2,128)S(1)} %reduce_sum.27), channel_id=1, source_target_pairs={{0,1},{1,0},{2,3},{3,2},{4,5},{5,4},{6,7},{7,6},{8,9},{9,8},{10,11... | collective-permute-start | bytes 6152 | tf_op jit(solution)/shard_map/ppermute | solution.py:612
  81.7 4.1 %collective-permute-start.1 = (f32[2,256]{1,0:T(2,128)S(1)}, f32[2,256]{1,0:T(2,128)S(1)}, u32[]{:S(2)}, u32[]{:S(2)}) collective-permute-start(f32[2,256]{1,0:T(2,128)S(1)} %add.41), channel_id=1, source_target_pairs={{0,2},{2,4},{4,6},{6,0},{1,3},{3,5},{5,7},{7,1},{8,10},{10,12},{12... | collective-permute-start | bytes 6152 | tf_op jit(solution)/shard_map/ppermute | solution.py:612
  81.7 4.4 %collective-permute-start.2 = (f32[2,256]{1,0:T(2,128)S(1)}, f32[2,256]{1,0:T(2,128)S(1)}, u32[]{:S(2)}, u32[]{:S(2)}) collective-permute-start(f32[2,256]{1,0:T(2,128)S(1)} %add.41), channel_id=1, source_target_pairs={{0,4},{2,6},{4,0},{6,2},{1,5},{3,7},{5,1},{7,3},{8,12},{10,14},{12... | collective-permute-start | bytes 6152 | tf_op jit(solution)/shard_map/ppermute | solution.py:612
  83.6 2.8 %collective-permute-start.3 = (f32[2,256]{1,0:T(2,128)S(1)}, f32[2,256]{1,0:T(2,128)S(1)}, u32[]{:S(2)}, u32[]{:S(2)}) collective-permute-start(f32[2,256]{1,0:T(2,128)S(1)} %add.41), channel_id=1, source_target_pairs={{0,6},{2,0},{4,2},{6,4},{1,7},{3,1},{5,3},{7,5},{8,14},{10,8},{12,... | collective-permute-start | bytes 6152 | tf_op jit(solution)/shard_map/ppermute | solution.py:612
  86.4 4.8 %collective-permute-start.4 = (f32[2,256]{1,0:T(2,128)S(1)}, f32[2,256]{1,0:T(2,128)S(1)}, u32[]{:S(2)}, u32[]{:S(2)}) collective-permute-start(f32[2,256]{1,0:T(2,128)S(1)} %add_add_fusion.1), channel_id=1, source_target_pairs={{0,64},{64,128},{128,192},{192,0},{1,65},{65,129},{129,193},{193,1... | collective-permute-start | bytes 6152 | tf_op jit(solution)/shard_map/ppermute | solution.py:612
  87.6 4.3 %collective-permute-start.5 = (f32[2,256]{1,0:T(2,128)S(1)}, f32[2,256]{1,0:T(2,128)S(1)}, u32[]{:S(2)}, u32[]{:S(2)}) collective-permute-start(f32[2,256]{1,0:T(2,128)S(1)} %add_add_fusion.1), channel_id=1, source_target_pairs={{0,128},{64,192},{128,0},{192,64},{1,129},{65,193},{129,1},{193,65... | collective-permute-start | bytes 6152 | tf_op jit(solution)/shard_map/ppermute | solution.py:612
  90.1 2.8 %collective-permute-start.6 = (f32[2,256]{1,0:T(2,128)S(1)}, f32[2,256]{1,0:T(2,128)S(1)}, u32[]{:S(2)}, u32[]{:S(2)}) collective-permute-start(f32[2,256]{1,0:T(2,128)S(1)} %add_add_fusion.1), channel_id=1, source_target_pairs={{0,192},{64,0},{128,64},{192,128},{1,193},{65,1},{129,65},{193,129... | collective-permute-start | bytes 6152 | tf_op jit(solution)/shard_map/ppermute | solution.py:612
  117.4 5.6 %copy-start = (bf16[2,256]{1,0:T(2,128)(2,1)S(1)}, bf16[2,256]{1,0:T(2,128)(2,1)}, u32[]{:S(2)}) copy-start(bf16[2,256]{1,0:T(2,128)(2,1)} %refs_14_.1) | copy-start | bytes 3076
  117.4 10.3 %all-to-all-start.3 = ((f32[8,2,256]{2,1,0:T(2,128)}), f32[8,2,256]{2,1,0:T(2,128)S(1)}, u32[]{:S(2)}, u32[]{:S(2)}) async-start(f32[8,2,256]{2,1,0:T(2,128)} %get-tuple-element.44), calls=%async_computation.3 | async-start | bytes 32768 | tf_op jit(solution)/shard_map/all_to_all | solution.py:616
  128.4 7.2 %copy-start.1 = (bf16[2,256]{1,0:T(2,128)(2,1)S(1)}, bf16[2,256]{1,0:T(2,128)(2,1)}, u32[]{:S(2)}) copy-start(bf16[2,256]{1,0:T(2,128)(2,1)} %refs_13_.1) | copy-start | bytes 3076
  128.4 16.1 %all-to-all-start.4 = ((f32[32,2,256]{2,1,0:T(2,128)}), f32[32,2,256]{2,1,0:T(2,128)S(1)}, u32[]{:S(2)}, u32[]{:S(2)}) async-start(f32[32,2,256]{2,1,0:T(2,128)} %broadcast_in_dim.2), calls=%async_computation.4 | async-start | bytes 131072 | tf_op jit(solution)/shard_map/all_to_all | solution.py:616

commit v9 on v8

--- a/solution.py
+++ b/solution.py
@@ -630,10 +630,7 @@
 
 
 def total_alone(copies):
-    stats = copies_summed(copies, ("blk_1", "blk_2"))
-    axes = ("grp", "blk_0")
-    copies = jnp.broadcast_to(stats[None], (lax.axis_size(axes),) + stats.shape)
-    return copies_summed(copies, axes)
+    return total_inside(total_along(copies))
 
 
 def local(

time: 148 us -> 150 us (1.014)
  blocking collectives: 0 us -> 9.87 us
  waiting for transfers between devices: 37.6 us -> 30.4 us
  starting transfers between devices: 52.6 us -> 50.9 us
    all_to_all x3 -> x1, waiting for transfers between devices: 16.6 us -> 3.07 us  [copies_summed(): return jnp.sum(lax.all_to_all(copies, axes, 0, 0, tiled=True), axis=0)]
    all_to_all x3 -> x1, starting transfers between devices: 16.8 us -> 3.33 us  [copies_summed(): return jnp.sum(lax.all_to_all(copies, axes, 0, 0, tiled=True), axis=0)]
    ppermute x7 -> x14, starting transfers between devices: 10.2 us -> 21.8 us  [shifted(): lax.ppermute(value, axis, [(i, (i + amount) % size) for i in range(size)])]
    all_to_all x0 -> x1, blocking collectives: none -> 9.87 us  [copies_summed(): return jnp.sum(lax.all_to_all(copies, axes, 0, 0, tiled=True), axis=0)]
    ppermute x7 -> x14, waiting for transfers between devices: 4.2 us -> 10.5 us  [shifted(): lax.ppermute(value, axis, [(i, (i + amount) % size) for i in range(size)])]
  transfers between devices with their start and end apart: 12 -> 17, of which waited for: 11 -> 14; matrix products, arithmetic and copies ran while one was open for 0% -> 0% of each run, Pallas kernels for 22% -> 22%
where the time goes in v9:
time: 150 us; the launch traced here: 149 us
  Pallas kernels  54.3 us (36%)
  starting transfers between devices  50.9 us (34%)
  waiting for transfers between devices  30.4 us (20%)
  blocking collectives  9.87 us (7%)
  other arithmetic  3.07 us (2%)
    pallas_call x7, Pallas kernels, call(): pl.pallas_call(body, name=name, out_shape=outs, in_specs=in_specs or [VME...  54.3 us
    all_to_all x2, starting transfers between devices, deliver(): lax.all_to_all(rows.reshape(-1, 8, rows.shape[1]), GRP_BLK, split_axis=0,...  25.7 us
    ppermute x14, starting transfers between devices, shifted(): lax.ppermute(value, axis, [(i, (i + amount) % size) for i in range(size)])  21.8 us
    all_to_all x2, waiting for transfers between devices, deliver(): lax.all_to_all(rows.reshape(-1, 8, rows.shape[1]), GRP_BLK, split_axis=0,...  16.8 us
    ppermute x14, waiting for transfers between devices, shifted(): lax.ppermute(value, axis, [(i, (i + amount) % size) for i in range(size)])  10.5 us
    all_to_all x1, blocking collectives, copies_summed(): return jnp.sum(lax.all_to_all(copies, axes, 0, 0, tiled=True), axis=0)  9.87 us
    all_to_all x1, starting transfers between devices, copies_summed(): return jnp.sum(lax.all_to_all(copies, axes, 0, 0, tiled=True), axis=0)  3.33 us
    all_to_all x1, waiting for transfers between devices, copies_summed(): return jnp.sum(lax.all_to_all(copies, axes, 0, 0, tiled=True), axis=0)  3.07 us
  transfers between devices with their start and end apart: 17, of which 14 were waited for; matrix products, arithmetic and copies ran while one was open for 0% of the time, Pallas kernels for 22%

profile of v9, /device:TPU:1, one launch (start us, length us, event | category | flops | bytes accessed | tf_op | source)
XLA Modules:
  0.0 148.6 jit_solution(4156903234124606023)
XLA Ops:
  0.0 3.4 %send_rows.2 = bf16[2048,256]{1,0:T(8,128)(2,1)} custom-call(s32[1,2048]{1,0:T(1,128)} %list_ref.3, s32[1,2048]{1,0:T(1,128)} %list_ref.3, bf16[1024,256]{1,0:T(8,128)(2,1)} %refs_0_.1), custom_call_target="tpu_custom_call" | custom-call | flops 1073741824 | bytes 4194304 | tf_op jit(solution)/shard_map/send_rows/pallas_call | solution.py:470
  3.5 16.7 %all-to-all-start = ((bf16[256,8,256]{2,1,0:T(8,128)(2,1)}), bf16[256,8,256]{2,1,0:T(8,128)(2,1)}, u32[]{:S(2)}, u32[]{:S(2)}) async-start(bf16[256,8,256]{2,1,0:T(8,128)(2,1)} %bitcast.12), calls=%async_computation | async-start | bytes 2097152 | tf_op jit(solution)/shard_map/all_to_all | solution.py:605
  20.1 9.4 %sort_edges.1 = (s32[8,2048]{1,0:T(8,128)}, s32[1,2048]{1,0:T(1,128)}, f32[8,2048]{1,0:T(8,128)}, f32[1024,8]{1,0:T(8,128)}, s32[1,32]{1,0:T(1,128)}) custom-call(s32[1,2048]{1,0:T(1,128)} %bitcast.17, s32[1,2048]{1,0:T(1,128)} %bitcast.18, s32[1,2048]{1,0:T(1,128)} %bitcast.19, f32[8,2048]{1,0:T(8,128)} %bias_ref.1), custom_call_target="tpu_custom_call" | custom-call | flops 2147483648 | bytes 4194304 | tf_op jit(solution)/shard_map/sort_edges/pallas_call | solution.py:470
  29.5 9.5 %own_part.2 = (bf16[1024,256]{1,0:T(8,128)(2,1)}, f32[1024,256]{1,0:T(8,128)}, bf16[2048,256]{1,0:T(8,128)(2,1)}, f32[8,2048]{1,0:T(8,128)}) custom-call(bf16[1024,256]{1,0:T(8,128)(2,1)} %refs_0_.1, bf16[2,256,256]{2,1,0:T(8,128)(2,1)} %refs_5_.5, bf16[2,256,256]{2,1,0:T(8,128)(2,1)} %refs_5_.4, bf16[2,256,256]{2,1,0:T(8,128)(2,1)} %refs_6_.4, ...), custom_call_target="tpu_custom_call" | custom-call | flops 3221225472 | bytes 4194304 | tf_op jit(solution)/shard_map/own_part/pallas_call | solution.py:470
  39.1 11.3 %all-to-all-done = bf16[256,8,256]{2,1,0:T(8,128)(2,1)} async-done(((bf16[256,8,256]{2,1,0:T(8,128)(2,1)}), bf16[256,8,256]{2,1,0:T(8,128)(2,1)}, u32[]{:S(2)}, u32[]{:S(2)}) %all-to-all-start) | async-done | bytes 1048608 | tf_op jit(solution)/shard_map/all_to_all | solution.py:605
  50.3 9.4 %edge_part.2 = (f32[1024,256]{1,0:T(8,128)}, f32[8,2,256]{2,1,0:T(2,128)}, bf16[1024,256]{1,0:T(8,128)(2,1)}) custom-call(bf16[2048,256]{1,0:T(8,128)(2,1)} %bitcast.1.refs_0_, bf16[1024,256]{1,0:T(8,128)(2,1)} %get-tuple-element.27.refs_1_, bf16[2048,256]{1,0:T(8,128)(2,1)} %get-tuple-element.28.refs_2_, f32[1024,8]{1,0:T(8,128)} %get-tuple-element.29.refs_3_, ...), custom_call_target="tpu_custom_call" | custom-call | flops 5368709120 | bytes 4194304 | tf_op jit(solution)/shard_map/edge_part/pallas_call | solution.py:470
  59.7 3.3 %all-to-all-start.1 = ((f32[8,2,256]{2,1,0:T(2,128)}), f32[8,2,256]{2,1,0:T(2,128)S(1)}, u32[]{:S(2)}, u32[]{:S(2)}) async-start(f32[8,2,256]{2,1,0:T(2,128)} %get-tuple-element.35), calls=%async_computation.1 | async-start | bytes 32768 | tf_op jit(solution)/shard_map/all_to_all | solution.py:616
  63.0 3.5 %send_rows.3 = bf16[2048,256]{1,0:T(8,128)(2,1)} custom-call(s32[1,2048]{1,0:T(1,128)} %list_ref.3, s32[1,2048]{1,0:T(1,128)} %list_ref.3, bf16[1024,256]{1,0:T(8,128)(2,1)} %get-tuple-element.34.table_ref), custom_call_target="tpu_custom_call" | custom-call | flops 1073741824 | bytes 4194304 | tf_op jit(solution)/shard_map/send_rows/pallas_call | solution.py:470
  66.5 3.1 %all-to-all-done.1 = f32[8,2,256]{2,1,0:T(2,128)S(1)} async-done(((f32[8,2,256]{2,1,0:T(2,128)}), f32[8,2,256]{2,1,0:T(2,128)S(1)}, u32[]{:S(2)}, u32[]{:S(2)}) %all-to-all-start.1) | async-done | bytes 16416 | tf_op jit(solution)/shard_map/all_to_all | solution.py:616
  69.6 9.1 %all-to-all-start.2 = ((bf16[256,8,256]{2,1,0:T(8,128)(2,1)}), bf16[256,8,256]{2,1,0:T(8,128)(2,1)}, u32[]{:S(2)}, u32[]{:S(2)}) async-start(bf16[256,8,256]{2,1,0:T(8,128)(2,1)} %bitcast.11), calls=%async_computation.2 | async-start | bytes 2097152 | tf_op jit(solution)/shard_map/all_to_all | solution.py:605
  78.7 2.4 %collective-permute-start = (f32[2,256]{1,0:T(2,128)S(1)}, f32[2,256]{1,0:T(2,128)S(1)}, u32[]{:S(2)}, u32[]{:S(2)}) collective-permute-start(f32[2,256]{1,0:T(2,128)S(1)} %reduce_sum.18), channel_id=1, source_target_pairs={{0,1},{1,0},{2,3},{3,2},{4,5},{5,4},{6,7},{7,6},{8,9},{9,8},{10,11... | collective-permute-start | bytes 6152 | tf_op jit(solution)/shard_map/ppermute | solution.py:612
  81.1 0.8 collective-permute-done
  81.9 0.0 collective-permute-start.1
  81.9 1.8 %collective-permute-start.2 = (f32[2,256]{1,0:T(2,128)S(1)}, f32[2,256]{1,0:T(2,128)S(1)}, u32[]{:S(2)}, u32[]{:S(2)}) collective-permute-start(f32[2,256]{1,0:T(2,128)S(1)} %add.62), channel_id=1, source_target_pairs={{0,4},{2,6},{4,0},{6,2},{1,5},{3,7},{5,1},{7,3},{8,12},{10,14},{12... | collective-permute-start | bytes 6152 | tf_op jit(solution)/shard_map/ppermute | solution.py:612
  83.8 1.2 collective-permute-start.3
  84.9 1.1 collective-permute-done.1
  86.0 0.3 collective-permute-done.2
  86.3 0.3 collective-permute-done.3
  86.6 1.2 collective-permute-start.4
  87.9 2.5 %collective-permute-start.5 = (f32[2,256]{1,0:T(2,128)S(1)}, f32[2,256]{1,0:T(2,128)S(1)}, u32[]{:S(2)}, u32[]{:S(2)}) collective-permute-start(f32[2,256]{1,0:T(2,128)S(1)} %add_add_fusion.3), channel_id=1, source_target_pairs={{0,128},{64,192},{128,0},{192,64},{1,129},{65,193},{129,1},{193,65... | collective-permute-start | bytes 6152 | tf_op jit(solution)/shard_map/ppermute | solution.py:612
  90.4 1.1 collective-permute-start.6
  91.5 0.0 collective-permute-done.4
  91.5 0.7 collective-permute-done.5
  92.2 1.0 collective-permute-done.6
  93.2 0.6 add_add_fusion.2.refs_1_.refs_12_
  93.8 9.6 %own_part.3 = (bf16[1024,256]{1,0:T(8,128)(2,1)}, f32[1024,256]{1,0:T(8,128)}, bf16[2048,256]{1,0:T(8,128)(2,1)}, f32[8,2048]{1,0:T(8,128)}) custom-call(f32[1024,256]{1,0:T(8,128)} %get-tuple-element.37.refs_0_, f32[2,256]{1,0:T(2,128)} %add_add_fusion.2.refs_1_.refs_12_, bf16[2,256]{1,0:T(2,128)(2,1)} %refs_13_.1, bf16[2,256]{1,0:T(2,128)(2,1)} %refs_14_.1, ...), custom_call_target="tpu_custom_call" | custom-call | flops 3221225472 | bytes 4194304 | tf_op jit(solution)/shard_map/own_part/pallas_call | solution.py:470
  103.5 5.5 %all-to-all-done.2 = bf16[256,8,256]{2,1,0:T(8,128)(2,1)} async-done(((bf16[256,8,256]{2,1,0:T(8,128)(2,1)}), bf16[256,8,256]{2,1,0:T(8,128)(2,1)}, u32[]{:S(2)}, u32[]{:S(2)}) %all-to-all-start.2) | async-done | bytes 1048608 | tf_op jit(solution)/shard_map/all_to_all | solution.py:605
  109.0 9.5 %edge_part.3 = (f32[1024,256]{1,0:T(8,128)}, f32[8,2,256]{2,1,0:T(2,128)}) custom-call(bf16[2048,256]{1,0:T(8,128)(2,1)} %bitcast.6.refs_0_, bf16[1024,256]{1,0:T(8,128)(2,1)} %get-tuple-element.39.refs_1_, bf16[2048,256]{1,0:T(8,128)(2,1)} %get-tuple-element.40.refs_2_, f32[1024,8]{1,0:T(8,128)} %get-tuple-element.29.refs_3_, ...), custom_call_target="tpu_custom_call" | custom-call | flops 5368709120 | bytes 4194304 | tf_op jit(solution)/shard_map/edge_part/pallas_call | solution.py:470
  118.5 9.9 %all_to_all.20 = f32[8,2,256]{2,1,0:T(2,128)S(1)} all-to-all(f32[8,2,256]{2,1,0:T(2,128)} %get-tuple-element.44), channel_id=1, replica_groups=mesh['grp'=4,'blk_0'=8,'blk_1'=4,'blk_2'=2] {'blk_0'}, dimensions={0} | all-to-all | bytes 32768 | tf_op jit(solution)/shard_map/all_to_all | solution.py:616
  128.4 0.0 copy-start
  128.4 3.5 %collective-permute-start.7 = (f32[2,256]{1,0:T(2,128)S(1)}, f32[2,256]{1,0:T(2,128)S(1)}, u32[]{:S(2)}, u32[]{:S(2)}) collective-permute-start(f32[2,256]{1,0:T(2,128)S(1)} %reduce_sum.19), channel_id=1, source_target_pairs={{0,1},{1,0},{2,3},{3,2},{4,5},{5,4},{6,7},{7,6},{8,9},{9,8},{10,11... | collective-permute-start | bytes 6152 | tf_op jit(solution)/shard_map/ppermute | solution.py:612
  131.8 0.8 collective-permute-done.7
  132.7 2.6 %collective-permute-start.10 = (f32[2,256]{1,0:T(2,128)S(1)}, f32[2,256]{1,0:T(2,128)S(1)}, u32[]{:S(2)}, u32[]{:S(2)}) collective-permute-start(f32[2,256]{1,0:T(2,128)S(1)} %add.69), channel_id=1, source_target_pairs={{0,6},{2,0},{4,2},{6,4},{1,7},{3,1},{5,3},{7,5},{8,14},{10,8},{12,... | collective-permute-start | bytes 6152 | tf_op jit(solution)/shard_map/ppermute | solution.py:612
  135.2 0.0 collective-permute-start.8
  135.2 1.2 collective-permute-start.9
  136.4 0.0 copy-done
  136.4 0.0 copy-start.1
  136.4 0.0 collective-permute-done.10
  136.4 2.4 %collective-permute-done.8 = f32[2,256]{1,0:T(2,128)S(1)} collective-permute-done((f32[2,256]{1,0:T(2,128)S(1)}, f32[2,256]{1,0:T(2,128)S(1)}, u32[]{:S(2)}, u32[]{:S(2)}) %collective-permute-start.8) | collective-permute-done | bytes 2080 | tf_op jit(solution)/shard_map/ppermute | solution.py:612
  138.9 0.3 collective-permute-done.9
  139.2 0.0 collective-permute-start.11
  139.2 4.3 %collective-permute-start.12 = (f32[2,256]{1,0:T(2,128)S(1)}, f32[2,256]{1,0:T(2,128)S(1)}, u32[]{:S(2)}, u32[]{:S(2)}) collective-permute-start(f32[2,256]{1,0:T(2,128)S(1)} %add_add_fusion.1), channel_id=1, source_target_pairs={{0,128},{64,192},{128,0},{192,64},{1,129},{65,193},{129,1},{193,65... | collective-permute-start | bytes 6152 | tf_op jit(solution)/shard_map/ppermute | solution.py:612
  143.5 0.0 collective-permute-start.13
  143.5 0.0 copy-done.1
  143.5 0.0 collective-permute-done.11
  143.5 1.0 collective-permute-done.12
  144.4 1.7 %collective-permute-done.13 = f32[2,256]{1,0:T(2,128)S(1)} collective-permute-done((f32[2,256]{1,0:T(2,128)S(1)}, f32[2,256]{1,0:T(2,128)S(1)}, u32[]{:S(2)}, u32[]{:S(2)}) %collective-permute-start.13) | collective-permute-done | bytes 2080 | tf_op jit(solution)/shard_map/ppermute | solution.py:612
  146.2 2.4 %fusion = bf16[1024,256]{1,0:T(8,128)(2,1)} fusion(f32[1024,256]{1,0:T(8,128)} %get-tuple-element.43, f32[256]{0:T(256)S(1)} %bitcast.13, f32[256]{0:T(256)S(1)} %bitcast.14, f32[256]{0:T(256)S(1)} %bitcast.16, f32[256]{0:T(256)S(1)} %bitcast.15), kind=kLoop, calls=%fused_computation.1 | loop fusion | flops 2359296 | bytes 1576960 | tf_op jit(solution)/shard_map/convert_element_type | solution.py:87
  (10 shorter events, 0.1 us)
Async XLA Ops:
  3.5 46.9 %all-to-all-start = ((bf16[256,8,256]{2,1,0:T(8,128)(2,1)}), bf16[256,8,256]{2,1,0:T(8,128)(2,1)}, u32[]{:S(2)}, u32[]{:S(2)}) async-start(bf16[256,8,256]{2,1,0:T(8,128)(2,1)} %bitcast.12), calls=%async_computation | async-start | bytes 2097152 | tf_op jit(solution)/shard_map/all_to_all | solution.py:605
  59.7 9.9 %all-to-all-start.1 = ((f32[8,2,256]{2,1,0:T(2,128)}), f32[8,2,256]{2,1,0:T(2,128)S(1)}, u32[]{:S(2)}, u32[]{:S(2)}) async-start(f32[8,2,256]{2,1,0:T(2,128)} %get-tuple-element.35), calls=%async_computation.1 | async-start | bytes 32768 | tf_op jit(solution)/shard_map/all_to_all | solution.py:616
  69.6 39.4 %all-to-all-start.2 = ((bf16[256,8,256]{2,1,0:T(8,128)(2,1)}), bf16[256,8,256]{2,1,0:T(8,128)(2,1)}, u32[]{:S(2)}, u32[]{:S(2)}) async-start(bf16[256,8,256]{2,1,0:T(8,128)(2,1)} %bitcast.11), calls=%async_computation.2 | async-start | bytes 2097152 | tf_op jit(solution)/shard_map/all_to_all | solution.py:605
  78.7 3.3 %collective-permute-start = (f32[2,256]{1,0:T(2,128)S(1)}, f32[2,256]{1,0:T(2,128)S(1)}, u32[]{:S(2)}, u32[]{:S(2)}) collective-permute-start(f32[2,256]{1,0:T(2,128)S(1)} %reduce_sum.18), channel_id=1, source_target_pairs={{0,1},{1,0},{2,3},{3,2},{4,5},{5,4},{6,7},{7,6},{8,9},{9,8},{10,11... | collective-permute-start | bytes 6152 | tf_op jit(solution)/shard_map/ppermute | solution.py:612
  81.9 4.1 %collective-permute-start.1 = (f32[2,256]{1,0:T(2,128)S(1)}, f32[2,256]{1,0:T(2,128)S(1)}, u32[]{:S(2)}, u32[]{:S(2)}) collective-permute-start(f32[2,256]{1,0:T(2,128)S(1)} %add.62), channel_id=1, source_target_pairs={{0,2},{2,4},{4,6},{6,0},{1,3},{3,5},{5,7},{7,1},{8,10},{10,12},{12... | collective-permute-start | bytes 6152 | tf_op jit(solution)/shard_map/ppermute | solution.py:612
  81.9 4.4 %collective-permute-start.2 = (f32[2,256]{1,0:T(2,128)S(1)}, f32[2,256]{1,0:T(2,128)S(1)}, u32[]{:S(2)}, u32[]{:S(2)}) collective-permute-start(f32[2,256]{1,0:T(2,128)S(1)} %add.62), channel_id=1, source_target_pairs={{0,4},{2,6},{4,0},{6,2},{1,5},{3,7},{5,1},{7,3},{8,12},{10,14},{12... | collective-permute-start | bytes 6152 | tf_op jit(solution)/shard_map/ppermute | solution.py:612
  83.8 2.8 %collective-permute-start.3 = (f32[2,256]{1,0:T(2,128)S(1)}, f32[2,256]{1,0:T(2,128)S(1)}, u32[]{:S(2)}, u32[]{:S(2)}) collective-permute-start(f32[2,256]{1,0:T(2,128)S(1)} %add.62), channel_id=1, source_target_pairs={{0,6},{2,0},{4,2},{6,4},{1,7},{3,1},{5,3},{7,5},{8,14},{10,8},{12,... | collective-permute-start | bytes 6152 | tf_op jit(solution)/shard_map/ppermute | solution.py:612
  86.6 4.9 %collective-permute-start.4 = (f32[2,256]{1,0:T(2,128)S(1)}, f32[2,256]{1,0:T(2,128)S(1)}, u32[]{:S(2)}, u32[]{:S(2)}) collective-permute-start(f32[2,256]{1,0:T(2,128)S(1)} %add_add_fusion.3), channel_id=1, source_target_pairs={{0,64},{64,128},{128,192},{192,0},{1,65},{65,129},{129,193},{193,1... | collective-permute-start | bytes 6152 | tf_op jit(solution)/shard_map/ppermute | solution.py:612
  87.9 4.3 %collective-permute-start.5 = (f32[2,256]{1,0:T(2,128)S(1)}, f32[2,256]{1,0:T(2,128)S(1)}, u32[]{:S(2)}, u32[]{:S(2)}) collective-permute-start(f32[2,256]{1,0:T(2,128)S(1)} %add_add_fusion.3), channel_id=1, source_target_pairs={{0,128},{64,192},{128,0},{192,64},{1,129},{65,193},{129,1},{193,65... | collective-permute-start | bytes 6152 | tf_op jit(solution)/shard_map/ppermute | solution.py:612
  90.4 2.8 %collective-permute-start.6 = (f32[2,256]{1,0:T(2,128)S(1)}, f32[2,256]{1,0:T(2,128)S(1)}, u32[]{:S(2)}, u32[]{:S(2)}) collective-permute-start(f32[2,256]{1,0:T(2,128)S(1)} %add_add_fusion.3), channel_id=1, source_target_pairs={{0,192},{64,0},{128,64},{192,128},{1,193},{65,1},{129,65},{193,129... | collective-permute-start | bytes 6152 | tf_op jit(solution)/shard_map/ppermute | solution.py:612
  128.4 8.0 %copy-start = (bf16[2,256]{1,0:T(2,128)(2,1)S(1)}, bf16[2,256]{1,0:T(2,128)(2,1)}, u32[]{:S(2)}) copy-start(bf16[2,256]{1,0:T(2,128)(2,1)} %refs_14_.1) | copy-start | bytes 3076
  128.4 4.3 %collective-permute-start.7 = (f32[2,256]{1,0:T(2,128)S(1)}, f32[2,256]{1,0:T(2,128)S(1)}, u32[]{:S(2)}, u32[]{:S(2)}) collective-permute-start(f32[2,256]{1,0:T(2,128)S(1)} %reduce_sum.19), channel_id=1, source_target_pairs={{0,1},{1,0},{2,3},{3,2},{4,5},{5,4},{6,7},{7,6},{8,9},{9,8},{10,11... | collective-permute-start | bytes 6152 | tf_op jit(solution)/shard_map/ppermute | solution.py:612
  132.7 3.8 %collective-permute-start.10 = (f32[2,256]{1,0:T(2,128)S(1)}, f32[2,256]{1,0:T(2,128)S(1)}, u32[]{:S(2)}, u32[]{:S(2)}) collective-permute-start(f32[2,256]{1,0:T(2,128)S(1)} %add.69), channel_id=1, source_target_pairs={{0,6},{2,0},{4,2},{6,4},{1,7},{3,1},{5,3},{7,5},{8,14},{10,8},{12,... | collective-permute-start | bytes 6152 | tf_op jit(solution)/shard_map/ppermute | solution.py:612
  135.2 3.6 %collective-permute-start.8 = (f32[2,256]{1,0:T(2,128)S(1)}, f32[2,256]{1,0:T(2,128)S(1)}, u32[]{:S(2)}, u32[]{:S(2)}) collective-permute-start(f32[2,256]{1,0:T(2,128)S(1)} %add.69), channel_id=1, source_target_pairs={{0,2},{2,4},{4,6},{6,0},{1,3},{3,5},{5,7},{7,1},{8,10},{10,12},{12... | collective-permute-start | bytes 6152 | tf_op jit(solution)/shard_map/ppermute | solution.py:612
  135.2 3.9 %collective-permute-start.9 = (f32[2,256]{1,0:T(2,128)S(1)}, f32[2,256]{1,0:T(2,128)S(1)}, u32[]{:S(2)}, u32[]{:S(2)}) collective-permute-start(f32[2,256]{1,0:T(2,128)S(1)} %add.69), channel_id=1, source_target_pairs={{0,4},{2,6},{4,0},{6,2},{1,5},{3,7},{5,1},{7,3},{8,12},{10,14},{12... | collective-permute-start | bytes 6152 | tf_op jit(solution)/shard_map/ppermute | solution.py:612
  136.4 7.0 %copy-start.1 = (bf16[2,256]{1,0:T(2,128)(2,1)S(1)}, bf16[2,256]{1,0:T(2,128)(2,1)}, u32[]{:S(2)}) copy-start(bf16[2,256]{1,0:T(2,128)(2,1)} %refs_13_.1) | copy-start | bytes 3076
  139.2 4.3 %collective-permute-start.11 = (f32[2,256]{1,0:T(2,128)S(1)}, f32[2,256]{1,0:T(2,128)S(1)}, u32[]{:S(2)}, u32[]{:S(2)}) collective-permute-start(f32[2,256]{1,0:T(2,128)S(1)} %add_add_fusion.1), channel_id=1, source_target_pairs={{0,64},{64,128},{128,192},{192,0},{1,65},{65,129},{129,193},{193,1... | collective-permute-start | bytes 6152 | tf_op jit(solution)/shard_map/ppermute | solution.py:612
  139.2 5.3 %collective-permute-start.12 = (f32[2,256]{1,0:T(2,128)S(1)}, f32[2,256]{1,0:T(2,128)S(1)}, u32[]{:S(2)}, u32[]{:S(2)}) collective-permute-start(f32[2,256]{1,0:T(2,128)S(1)} %add_add_fusion.1), channel_id=1, source_target_pairs={{0,128},{64,192},{128,0},{192,64},{1,129},{65,193},{129,1},{193,65... | collective-permute-start | bytes 6152 | tf_op jit(solution)/shard_map/ppermute | solution.py:612
  143.5 2.7 %collective-permute-start.13 = (f32[2,256]{1,0:T(2,128)S(1)}, f32[2,256]{1,0:T(2,128)S(1)}, u32[]{:S(2)}, u32[]{:S(2)}) collective-permute-start(f32[2,256]{1,0:T(2,128)S(1)} %add_add_fusion.1), channel_id=1, source_target_pairs={{0,192},{64,0},{128,64},{192,128},{1,193},{65,1},{129,65},{193,129... | collective-permute-start | bytes 6152 | tf_op jit(solution)/shard_map/ppermute | solution.py:612
